TPU v7x, 32 devices: a whole 2x2x4 slice. The times are simulated.
32 devices in a mesh: groups: 2 (over y), path: 4 (over z), half: 2 (over x), tile: 2 (over core).
Axes of the slice: x: 2, y: 2, z: 4, core: 2. Of those that a mesh axis runs over, the one named last changes fastest.
Arguments:
- left_prefix: bfloat16 [64, 4096], P(('groups', 'path'), ('half', 'tile')), parts along dimension 0, may hold values from -6 to 6
- right_prefix: bfloat16 [64, 4096], P(('groups', 'half', 'tile'), 'path'), parts along dimension 0, may hold values from -6 to 6
- left_layer: bfloat16 [2048, 1024], P(('groups', 'half', 'tile')), parts along dimension 0, may hold values from -0.1875 to 0.1875
- right_layer: bfloat16 [2048, 1024], P(('groups', 'path')), parts along dimension 0, may hold values from -0.1875 to 0.1875
- left_map: int32 [512], P('groups'), parts along dimension 0, may hold values from 0 to 31
- right_map: int32 [512], P('groups'), parts along dimension 0, may hold values from 0 to 31
- branch_bits: int32 [512, 10], P('groups'), parts along dimension 0, may hold values 0 or 1
- cut_side: int32 [20], P('groups'), parts along dimension 0, may hold values 0 or 1
Outputs:
- amplitude: bfloat16 [8192, 4096], P(('groups', 'half', 'tile'), 'path'), parts along dimension 0
There are 2 independent parts, one for each index of `groups`. A program takes and returns all parts, laid end to end along the dimension named above; each array names one. Nothing has to cross between parts.
All inputs are finite; a program needn't handle non-finite values.
Results may differ from a plain program's by a relative error of at most 0.0058.
Values may be sent and summed in bfloat16 or wider, within the bound.
No kernel may reach another device: no remote copies, remote signals or barrier semaphores. Data moves between devices by JAX's collectives and lax.ppermute only.
A program may use at most 64 MiB of HBM per device.

v0:
```python
import jax
import jax.numpy as jnp
from jax import lax
from jax.sharding import PartitionSpec as P


def cut_factors(branch, cut_side, gate_count, on_left):
    cut_count = cut_side.shape[0]
    bit_place = lax.broadcasted_iota(jnp.int32, (cut_count, gate_count), 0)
    gate_code = lax.broadcasted_iota(jnp.int32, (cut_count, gate_count), 1)
    bit_table = jnp.right_shift(gate_code, bit_place) & 1
    projector = cut_side if on_left else 1 - cut_side
    phased = 1 - projector
    chosen = branch * projector[None, :]
    misses = (
        jnp.sum(chosen, axis=1, keepdims=True)
        + jnp.dot(projector, bit_table)[None, :]
        - 2 * jnp.dot(chosen, bit_table)
    )
    parity = jnp.dot(branch * phased[None, :], bit_table)
    sign_value = 1 - 2 * (parity % 2)
    return jnp.where(misses == 0, sign_value, 0).astype(jnp.bfloat16)


def project(prefix_rows, path_map, branch, cut_side, on_left):
    factor = cut_factors(branch, cut_side, prefix_rows.shape[1], on_left)
    return prefix_rows[path_map] * factor


def apply_left(projected, left_layer):

    def columns(layer_piece, first_row):
        return lax.dot_general(
            projected, layer_piece, (((1,), (1,)), ((), ())), preferred_element_type=jnp.float32
        )

    states = columns(lax.all_gather(left_layer, ("half", "tile"), axis=0, tiled=True), jnp.int32(0))
    return states.astype(jnp.bfloat16)


def apply_right(projected, right_layer):

    def columns(layer_piece, first_row):
        return lax.dot_general(
            projected, layer_piece, (((1,), (1,)), ((), ())), preferred_element_type=jnp.float32
        )

    states = columns(lax.all_gather(right_layer, "path", axis=0, tiled=True), jnp.int32(0))
    return states.astype(jnp.bfloat16)


def on_device(
    left_prefix, right_prefix, left_layer, right_layer, left_map, right_map, branch_bits, cut_side
):
    left_rows = lax.all_gather(left_prefix, "path", axis=0, tiled=True)
    right_rows = lax.all_gather(right_prefix, ("half", "tile"), axis=0, tiled=True)
    left_states = apply_left(project(left_rows, left_map, branch_bits, cut_side, True), left_layer)
    right_states = apply_right(
        project(right_rows, right_map, branch_bits, cut_side, False), right_layer
    )
    amplitude = lax.dot_general(
        left_states, right_states, (((0,), (0,)), ((), ())), preferred_element_type=jnp.float32
    )
    return amplitude.astype(jnp.bfloat16)


def solution(mesh):
    in_specs = (
        P(("groups", "path"), ("half", "tile")),
        P(("groups", "half", "tile"), "path"),
        P(("groups", "half", "tile"), None),
        P(("groups", "path"), None),
        P("groups"),
        P("groups"),
        P("groups", None),
        P("groups"),
    )
    out_specs = P(("groups", "half", "tile"), "path")
    return jax.shard_map(
        on_device, mesh=mesh, in_specs=in_specs, out_specs=out_specs, check_vma=False
    )
```

profile of v0, /device:TPU:0, one launch (start us, length us, event | category | flops | bytes accessed | tf_op | source)
XLA Modules:
  0.0 92.8 jit_solution(1956754094180607474)
XLA Ops:
  6.5 0.0 all-gather.5.cloned.1.call-start
  6.5 0.7 all-gather.5.cloned.1.call-update
  7.3 0.0 all-gather.3.cloned.1.call-start
  7.3 0.7 all-gather.3.cloned.1.call-update
  8.0 6.5 %all_gather.14 = bf16[32,1024]{1,0:T(8,128)(2,1)S(1)} all-gather(bf16[8,1024]{1,0:T(8,128)(2,1)} %param.9), channel_id=1, replica_groups=mesh['groups'=2,'path'=4,'half'=2,'tile'=2] {'half','tile'}, dimensions={0}, use_global_device_ids=true | all-gather | bytes 81920 | tf_op jit(solution)/shard_map/all_gather | solution.py:56
  14.5 0.7 compare_select_fusion
  15.2 0.0 copy-start.3
  15.2 1.2 %gather_fusion.1 = bf16[256,1024]{1,0:T(8,128)(2,1)S(1)} fusion(bf16[32,1024]{1,0:T(8,128)(2,1)S(1)} %all_gather.14, s32[1024]{0:T(1024)S(1)} %pad_clamp_fusion), kind=kCustom, calls=%fused_computation.1 | custom fusion | bytes 1049600 | tf_op jit(solution)/shard_map/gather | solution.py:27
  16.3 0.0 copy-done.1
  16.3 14.5 %all_gather.12 = bf16[32,1024]{1,0:T(8,128)(2,1)S(1)} all-gather(bf16[8,1024]{1,0:T(8,128)(2,1)S(1)} %copy-done.1), channel_id=1, replica_groups=mesh['groups'=2,'path'=4,'half'=2,'tile'=2] {'path'}, dimensions={0}, use_global_device_ids=true | all-gather | bytes 81920 | tf_op jit(solution)/shard_map/all_gather | solution.py:55
  30.8 0.0 copy-done.3
  30.8 0.0 copy-start.2
  30.9 0.0 copy-start
  30.9 1.2 %gather_fusion = bf16[256,1024]{1,0:T(8,128)(2,1)S(1)} fusion(bf16[32,1024]{1,0:T(8,128)(2,1)S(1)} %all_gather.12, s32[1024]{0:T(1024)S(1)} %pad_clamp_fusion.1), kind=kCustom, calls=%fused_computation | custom fusion | bytes 1049600 | tf_op jit(solution)/shard_map/gather | solution.py:27
  32.1 0.0 copy-done
  32.1 0.1 multiply_reduce_fusion.1
  32.2 0.2 fusion.28
  32.3 0.2 fusion.31
  32.5 1.7 %fusion.29 = s32[256,1024]{1,0:T(8,128)S(1)} fusion(s32[256,10]{0,1:T(8,128)S(1)} %copy-done, s32[10]{0:T(128)S(1)} %broadcast_subtract_fusion), kind=kOutput, calls=%fused_computation.35 | convolution fusion | flops 5265920 | bytes 1058856 | tf_op jit(solution)/shard_map/dot_general | solution.py:20
  34.2 1.7 %fusion.30 = s32[256,1024]{1,0:T(8,128)S(1)} fusion(s32[256,10]{0,1:T(8,128)S(1)} %copy-done, s32[10]{0:T(128)S(1)} %copy-done.2), kind=kOutput, calls=%fused_computation.36 | convolution fusion | flops 5265920 | bytes 1058856 | tf_op jit(solution)/shard_map/dot_general | solution.py:18
  35.9 22.1 %all-gather.5.cloned.1.call-done = bf16[1024,1024]{1,0:T(8,128)(2,1)} async-done(((bf16[256,1024]{1,0:T(8,128)(2,1)}), bf16[1024,1024]{1,0:T(8,128)(2,1)}) %all-gather.5.cloned.1.call-update) | async-done | bytes 2097168 | tf_op jit(solution)/shard_map/all_gather | solution.py:48
  58.0 3.6 %convolution_convert_fusion.1 = bf16[256,1024]{1,0:T(8,128)(2,1)} fusion(bf16[1024,1024]{1,0:T(8,128)(2,1)} %all-gather.5.cloned.1.call-done, bf16[256,1024]{1,0:T(8,128)(2,1)S(1)} %gather_fusion.1, s32[256,1024]{1,0:T(8,128)S(1)} %fusion.29, s32[256,1024]{1,0:T(8,128)S(1)} %fusion.30, s32[1024]{0:T(1024)S(1)} %bitcast.12, s32[256]{0:T(256)S(1)} %get-tuple-element.6), kind=kOutput, calls=%fused_computation.9 | convolution fusion | flops 543162368 | bytes 5248000 | tf_op jit(solution)/shard_map/dot_general | solution.py:44
  61.7 19.5 %all-gather.3.cloned.1.call-done = bf16[1024,1024]{1,0:T(8,128)(2,1)} async-done(((bf16[256,1024]{1,0:T(8,128)(2,1)}), bf16[1024,1024]{1,0:T(8,128)(2,1)}) %all-gather.3.cloned.1.call-update) | async-done | bytes 2097168 | tf_op jit(solution)/shard_map/all_gather | solution.py:37
  81.2 4.8 %convolution_convert_fusion = bf16[1024,1024]{1,0:T(8,128)(2,1)} fusion(bf16[256,1024]{1,0:T(8,128)(2,1)} %convolution_convert_fusion.1, bf16[1024,1024]{1,0:T(8,128)(2,1)} %all-gather.3.cloned.1.call-done, bf16[256,1024]{1,0:T(8,128)(2,1)S(1)} %gather_fusion, s32[256,1024]{1,0:T(8,128)S(1)} %fusion.30, s32[256,1024]{1,0:T(8,128)S(1)} %fusion.29, ...), kind=kOutput, calls=%fused_computation.2 | convolution fusion | flops 1081081856 | bytes 7345152 | tf_op jit(solution)/shard_map/dot_general | solution.py:61
  (6 shorter events, 0.0 us)
Async XLA Ops:
  6.5 51.5 %all-gather.5.cloned.1.call-start = ((), (), s32[]{:S(2)}) async-start(), calls=%async_computation.1 | async-start | bytes 2621440 | tf_op jit(solution)/shard_map/all_gather | solution.py:48
  7.3 73.9 %all-gather.3.cloned.1.call-start = ((), (), s32[]{:S(2)}) async-start(), calls=%async_computation | async-start | bytes 2621440 | tf_op jit(solution)/shard_map/all_gather | solution.py:37
  15.2 1.2 %copy-start.1 = (bf16[8,1024]{1,0:T(8,128)(2,1)S(1)}, bf16[8,1024]{1,0:T(8,128)(2,1)}, u32[]{:S(2)}) copy-start(bf16[8,1024]{1,0:T(8,128)(2,1)} %param.8) | copy-start | bytes 49156
  15.2 15.7 %copy-start.3 = (s32[256]{0:T(256)S(1)}, s32[256]{0:T(256)}, u32[]{:S(2)}) copy-start(s32[256]{0:T(256)} %param.12) | copy-start | bytes 3076
  30.8 1.2 %copy-start.2 = (s32[10]{0:T(128)S(1)}, s32[10]{0:T(128)}, u32[]{:S(2)}) copy-start(s32[10]{0:T(128)} %param.15) | copy-start | bytes 124
  30.9 1.2 %copy-start = (s32[256,10]{0,1:T(8,128)S(1)}, s32[256,10]{0,1:T(8,128)}, u32[]{:S(2)}) copy-start(s32[256,10]{0,1:T(8,128)} %param.14) | copy-start | bytes 30724
Sparse Core Ops, SparseCore 0:
  8.9 49.0 all-gather.4
  59.6 21.5 all-gather.2
where the time goes:
time: 93 us; the launch traced here: 92.8 us
  waiting for transfers between devices  43 us (46%)
  blocking collectives  20.9 us (22%)
  between operations  13.5 us (15%)
  matrix products  12.2 us (13%)
  local copies, waits for them, and re-layouts  2.36 us (3%)
    all_gather x1, waiting for transfers between devices, apply_right(): lax.all_gather(right_layer, 'path', axis=0, tiled=True)  22.1 us
    all_gather x1, waiting for transfers between devices, apply_left(): lax.all_gather(left_layer, ('half', 'tile'), axis=0, tiled=True)  19.5 us
    all_gather x1, blocking collectives, on_device(): left_rows = lax.all_gather(left_prefix, 'path', axis=0, tiled=True)  14.5 us
    all_gather x1, blocking collectives, on_device(): lax.all_gather(right_prefix, ('half', 'tile'), axis=0, tiled=True)  6.46 us
    dot_general x1, matrix products, on_device(): lax.dot_general(left_states, right_states, (((0,), (0,)), ((), ())), pref...  4.84 us
    dot_general x1, matrix products, columns(): lax.dot_general(projected, layer_piece, (((1,), (1,)), ((), ())), preferr...  3.64 us
    gather x2, local copies, waits for them, and re-layouts, project(): return prefix_rows[path_map] * factor  2.34 us
  transfers between devices with their start and end apart: 2, of which 2 were waited for; matrix products, arithmetic and copies ran while one was open for 11% of the time, Pallas kernels for 0%

commit v1 on v0

v1 whole, which is shorter than its diff:
```python
import functools

import jax
import jax.numpy as jnp
from jax import lax
from jax.experimental import pallas as pl
from jax.experimental.pallas import tpu as pltpu
from jax.sharding import PartitionSpec as P

DEVICE_AXES = ("path", "half", "tile")
CONTRACT_LAST = (((1,), (1,)), ((), ()))


def cut_factors(branch, cut_side, gate_count, on_left):
    cut_count = cut_side.shape[0]
    bit_place = lax.broadcasted_iota(jnp.int32, (cut_count, gate_count), 0)
    gate_code = lax.broadcasted_iota(jnp.int32, (cut_count, gate_count), 1)
    bit_table = jnp.right_shift(gate_code, bit_place) & 1
    projector = cut_side if on_left else 1 - cut_side
    phased = 1 - projector
    chosen = branch * projector[None, :]
    misses = (
        jnp.sum(chosen, axis=1, keepdims=True)
        + jnp.dot(projector, bit_table)[None, :]
        - 2 * jnp.dot(chosen, bit_table)
    )
    parity = jnp.dot(branch * phased[None, :], bit_table)
    sign_value = 1 - 2 * (parity % 2)
    return jnp.where(misses == 0, sign_value, 0).astype(jnp.bfloat16)


def gathered(
    left_prefix, right_prefix, left_layer, right_layer, left_map, right_map, branch_bits, cut_side
):
    def states(prefix, prefix_axes, layer, layer_axes, path_map, on_left):
        rows = lax.all_gather(prefix, prefix_axes, axis=0, tiled=True)
        factor = cut_factors(branch_bits, cut_side, rows.shape[1], on_left)
        whole_layer = lax.all_gather(layer, layer_axes, axis=0, tiled=True)
        applied = lax.dot_general(
            rows[path_map] * factor, whole_layer, CONTRACT_LAST, preferred_element_type=jnp.float32
        )
        return applied.astype(jnp.bfloat16)

    left_states = states(left_prefix, "path", left_layer, ("half", "tile"), left_map, True)
    right_states = states(right_prefix, ("half", "tile"), right_layer, "path", right_map, False)
    amplitude = lax.dot_general(
        left_states, right_states, (((0,), (0,)), ((), ())), preferred_element_type=jnp.float32
    )
    return amplitude.astype(jnp.bfloat16)


def whole_vmem(count):
    return [pl.BlockSpec(memory_space=pltpu.VMEM)] * count


def small(outs):
    return pltpu.CompilerParams(vmem_limit_bytes=outs)


def project_kernel(on_left, shard_axes, pieces, *refs):
    prefix_refs, (map_ref, branch_ref, side_ref), out_ref = refs[:-4], refs[-4:-1], refs[-1]
    cuts, paths = branch_ref.shape
    gates = out_ref.shape[0]
    shard, shards = jnp.int32(0), 1
    for axis in shard_axes:
        shard = shard * lax.axis_size(axis) + lax.axis_index(axis)
        shards *= lax.axis_size(axis)
    side = side_ref[...]
    projector = side if on_left else 1 - side
    weight = jnp.left_shift(1, lax.broadcasted_iota(jnp.int32, (cuts, 1), 0))
    branch = branch_ref[...]
    wanted = jnp.sum(branch * (projector * weight), axis=0, keepdims=True)
    phased = jnp.sum(branch * ((1 - projector) * weight), axis=0, keepdims=True)
    mask = jnp.sum(projector * weight, axis=0, keepdims=True)
    gate = lax.broadcasted_iota(jnp.int32, (gates, paths), 0)
    hit = (gate & mask) == wanted
    odd = (lax.population_count(gate & phased) & 1) == 1
    factor = jnp.where(hit, jnp.where(odd, -1.0, 1.0), 0.0)
    for block in range(2):
        rows = jnp.concatenate([r[...] for r in prefix_refs[block * pieces:][:pieces]], axis=0)
        depth = rows.shape[0] // shards
        wanted_row = map_ref[...]
        place = (lax.div(wanted_row, depth) ^ shard) * depth + lax.rem(wanted_row, depth)
        index = lax.broadcasted_iota(jnp.int32, (rows.shape[0], paths), 0)
        pick = jnp.where(index == place, 1.0, 0.0).astype(jnp.bfloat16)
        picked = lax.dot_general(
            rows, pick, (((0,), (0,)), ((), ())), preferred_element_type=jnp.float32
        )
        out_ref[:, pl.ds(block * paths, paths)] = (picked * factor).astype(jnp.bfloat16)


def project(blocks, path_map, branch_bits, cut_side, on_left, shard_axes):
    pieces = len(blocks[0])
    flat = [piece for block in blocks for piece in block]
    paths = path_map.shape[0]
    return pl.pallas_call(
        functools.partial(project_kernel, on_left, shard_axes, pieces),
        out_shape=jax.ShapeDtypeStruct((flat[0].shape[1], 2 * paths), jnp.bfloat16),
        in_specs=whole_vmem(len(flat) + 3),
        out_specs=pl.BlockSpec(memory_space=pltpu.VMEM),
        compiler_params=small(16 << 20),
    )(*flat, path_map[None, :], branch_bits.T, cut_side[:, None])


def apply_kernel(count, *refs):
    layer_refs, projected_ref, mine_ref, other_ref = refs[:count], refs[count], refs[-2], refs[-1]
    paths = mine_ref.shape[1]
    at = 0
    for layer_ref in layer_refs:
        rows = layer_ref.shape[0]
        states = jnp.dot(
            layer_ref[...], projected_ref[...], preferred_element_type=jnp.float32
        ).astype(jnp.bfloat16)
        mine_ref[pl.ds(at, rows), :] = states[:, :paths]
        other_ref[pl.ds(at, rows), :] = states[:, paths:]
        at += rows


def apply_rows(layers, projected):
    rows = sum(layer.shape[0] for layer in layers)
    shape = jax.ShapeDtypeStruct((rows, projected.shape[1] // 2), jnp.bfloat16)
    return pl.pallas_call(
        functools.partial(apply_kernel, len(layers)),
        out_shape=(shape, shape),
        in_specs=whole_vmem(len(layers) + 1),
        out_specs=(pl.BlockSpec(memory_space=pltpu.VMEM),) * 2,
        compiler_params=small(16 << 20),
    )(*layers, projected)


def amplitude_kernel(left_count, *refs):
    left_refs, right_refs = refs[:left_count], refs[left_count:-4]
    out_ref, right_ref, block_ref, sems = refs[-4:]
    path, half, tile = (lax.axis_index(axis) for axis in DEVICE_AXES)
    tiles = lax.axis_size("tile")
    spot = half * tiles + tile
    near = (0, 0, 1, 1, 0, 0, 1, 1)
    turn = (0, tiles, 0, tiles, 1, 1 + tiles, 1, 1 + tiles)
    rows = right_refs[0].shape[0] // 2
    chunk = rows * tiles * lax.axis_size("half")
    for ref, plane, spin in zip(right_refs, near, turn):
        for far in range(2):
            start = (path ^ (plane + 2 * far)) * chunk + (spot ^ spin) * rows
            right_ref[pl.ds(pl.multiple_of(start, rows), rows), :] = ref[pl.ds(far * rows, rows), :]
    right = right_ref[...]
    depth = left_refs[0].shape[0]
    copies = []
    for k, (ref, spin) in enumerate(zip(left_refs, (0, 1, tiles, 1 + tiles))):
        block_ref[k] = lax.dot_general(
            ref[...], right, CONTRACT_LAST, preferred_element_type=jnp.float32
        ).astype(jnp.bfloat16)
        start = pl.multiple_of((spot ^ spin) * depth, depth)
        copy = pltpu.make_async_copy(block_ref.at[k], out_ref.at[pl.ds(start, depth), :], sems.at[k])
        copy.start()
        copies.append(copy)
    for copy in copies:
        copy.wait()


def amplitude_of(left_pieces, right_pieces):
    depth, paths = left_pieces[0].shape
    count = len(left_pieces)
    width = sum(piece.shape[0] for piece in right_pieces)
    return pl.pallas_call(
        functools.partial(amplitude_kernel, count),
        out_shape=jax.ShapeDtypeStruct((count * depth, width), jnp.bfloat16),
        in_specs=whole_vmem(count + len(right_pieces)),
        out_specs=pl.BlockSpec(memory_space=pl.ANY),
        scratch_shapes=[
            pltpu.VMEM((width, paths), jnp.bfloat16),
            pltpu.VMEM((count, depth, width), jnp.bfloat16),
            pltpu.SemaphoreType.DMA((count,)),
        ],
        compiler_params=small(16 << 20),
    )(*left_pieces, *right_pieces)


def exchanged(
    left_prefix, right_prefix, left_layer, right_layer, left_map, right_map, branch_bits, cut_side
):
    sizes = [lax.axis_size(axis) for axis in DEVICE_AXES]

    def exchange(value, plane=0, half=0, tile=0):
        pairs = []
        for p in range(sizes[0]):
            for h in range(sizes[1]):
                for t in range(sizes[2]):
                    source = (p * sizes[1] + h) * sizes[2] + t
                    target = ((p ^ plane) * sizes[1] + (h ^ half)) * sizes[2] + (t ^ tile)
                    pairs.append((source, target))
        return lax.ppermute(value, DEVICE_AXES, pairs)

    spot = lax.axis_index("half") * sizes[2] + lax.axis_index("tile")
    share = right_layer.shape[0] // (sizes[1] * sizes[2])
    near_rows = lax.dynamic_slice_in_dim(right_layer, spot * share, share, axis=0)

    tile_prefix = exchange(right_prefix, tile=1)
    far_rows = exchange(near_rows, plane=2)
    pair = jnp.concatenate([right_prefix, tile_prefix], axis=0)
    pair_x = exchange(pair, half=1)
    pair_z = exchange(pair, plane=1)
    pair_xz = exchange(pair, plane=1, half=1)
    layer_x = exchange(left_layer, half=1)
    left_rows = jnp.concatenate(
        [left_prefix] + [exchange(left_prefix, plane=step) for step in (1, 2, 3)], axis=0
    )
    left_rows_t = exchange(left_rows, tile=1)

    right_projected = project(
        ((pair, pair_x), (pair_z, pair_xz)),
        right_map, branch_bits, cut_side, False, ("half", "tile"),
    )
    right_mine, right_near = apply_rows((near_rows, far_rows), right_projected)
    right_pieces = [
        right_mine,
        exchange(right_mine, half=1),
        exchange(right_near, plane=1),
        exchange(right_near, plane=1, half=1),
    ]
    right_pieces = right_pieces + [exchange(piece, tile=1) for piece in right_pieces]

    left_projected = project(
        ((left_rows,), (left_rows_t,)), left_map, branch_bits, cut_side, True, ("path",)
    )
    own_mine, own_other = apply_rows((left_layer,), left_projected)
    x_mine, x_other = apply_rows((layer_x,), left_projected)
    left_pieces = [own_mine, exchange(own_other, tile=1), x_mine, exchange(x_other, tile=1)]
    return amplitude_of(left_pieces, right_pieces)


def solution(mesh):
    in_specs = (
        P(("groups", "path"), ("half", "tile")),
        P(("groups", "half", "tile"), "path"),
        P(("groups", "half", "tile"), None),
        P(("groups", "path"), None),
        P("groups"),
        P("groups"),
        P("groups", None),
        P("groups"),
    )
    out_specs = P(("groups", "half", "tile"), "path")
    squares = (mesh.shape["path"], mesh.shape["half"], mesh.shape["tile"]) == (4, 2, 2)
    return jax.shard_map(
        exchanged if squares else gathered,
        mesh=mesh, in_specs=in_specs, out_specs=out_specs, check_vma=False,
    )
```

time: 93 us -> 36.6 us (0.39)
  waiting for transfers between devices: 43 us -> 10.4 us
  blocking collectives: 20.9 us -> 0 us
  starting transfers between devices: 0.04 us -> 17.6 us
  between operations: 13.5 us -> 0.11 us
  matrix products: 12.2 us -> 0 us
  Pallas kernels: 0 us -> 4.4 us
  local copies, waits for them, and re-layouts: 2.36 us -> 3.66 us
    all_gather x2 -> x0, waiting for transfers between devices: 41.6 us -> none  [the longest x1 22.1 us: apply_right(): lax.all_gather(right_layer, 'path', axis=0, tiled=True)]
    all_gather x2 -> x0, blocking collectives: 20.9 us -> none  [the longest x1 14.5 us: on_device(): left_rows = lax.all_gather(left_prefix, 'path', axis=0, tiled=True)]
    ppermute x0 -> x19, starting transfers between devices: none -> 17.6 us  [exchange(): return lax.ppermute(value, DEVICE_AXES, pairs)]
    dot_general x6 -> x0, matrix products: 12.2 us -> none  [the longest x1 4.84 us: on_device(): lax.dot_general(left_states, right_states, (((0,), (0,)), ((), ())), pref...]
    ppermute x0 -> x19, waiting for transfers between devices: none -> 10.4 us  [exchange(): return lax.ppermute(value, DEVICE_AXES, pairs)]
    pallas_call x0 -> x6, Pallas kernels: none -> 4.4 us  [the longest x1 1.72 us: amplitude_of(): pl.pallas_call(functools.partial(amplitude_kernel, count), out_shape=jax....]
    unnamed x8 -> x14, local copies, waits for them, and re-layouts: 0.02 us -> 2.91 us
    gather x2 -> x0, local copies, waits for them, and re-layouts: 2.34 us -> none  [project(): return prefix_rows[path_map] * factor]
  transfers between devices with their start and end apart: 2 -> 19, of which waited for: 2 -> 6; matrix products, arithmetic and copies ran while one was open for 11% -> 6% of each run, Pallas kernels for 0% -> 7%
where the time goes in v1:
time: 36.6 us; the launch traced here: 36.2 us
  starting transfers between devices  17.6 us (48%)
  waiting for transfers between devices  10.4 us (28%)
  Pallas kernels  4.4 us (12%)
  local copies, waits for them, and re-layouts  3.66 us (10%)
    ppermute x19, starting transfers between devices, exchange(): return lax.ppermute(value, DEVICE_AXES, pairs)  17.6 us
    ppermute x19, waiting for transfers between devices, exchange(): return lax.ppermute(value, DEVICE_AXES, pairs)  10.4 us
    unnamed x14, local copies, waits for them, and re-layouts  2.91 us
    pallas_call x1, Pallas kernels, amplitude_of(): pl.pallas_call(functools.partial(amplitude_kernel, count), out_shape=jax....  1.72 us
    pallas_call x2, Pallas kernels, project(): pl.pallas_call(functools.partial(project_kernel, on_left, shard_axes, pie...  1.34 us
    pallas_call x3, Pallas kernels, apply_rows(): pl.pallas_call(functools.partial(apply_kernel, len(layers)), out_shape=(s...  1.33 us
    broadcast_in_dim x1, local copies, waits for them, and re-layouts, project(): cut_side[:, None]  0.74 us
  transfers between devices with their start and end apart: 19, of which 6 were waited for; matrix products, arithmetic and copies ran while one was open for 6% of the time, Pallas kernels for 7%

profile of v1, /device:TPU:0, one launch (start us, length us, event | category | flops | bytes accessed | tf_op | source)
XLA Modules:
  0.0 36.2 jit_solution(13158621615396885351)
XLA Ops:
  0.0 4.1 %collective-permute-start.1 = (bf16[8,1024]{1,0:T(8,128)(2,1)}, bf16[8,1024]{1,0:T(8,128)(2,1)S(1)}, u32[]{:S(2)}, u32[]{:S(2)}) collective-permute-start(bf16[8,1024]{1,0:T(8,128)(2,1)} %param.8), channel_id=1, source_target_pairs={{0,8},{1,9},{2,10},{3,11},{4,12},{5,13},{6,14},{7,15},{8,0},{9,1},... | collective-permute-start | bytes 49160 | tf_op jit(solution)/shard_map/ppermute | solution.py:191
  4.1 1.6 %collective-permute-start = (bf16[8,1024]{1,0:T(8,128)(2,1)}, bf16[8,1024]{1,0:T(8,128)(2,1)S(1)}, u32[]{:S(2)}, u32[]{:S(2)}) collective-permute-start(bf16[8,1024]{1,0:T(8,128)(2,1)} %param.8), channel_id=1, source_target_pairs={{0,4},{1,5},{2,6},{3,7},{4,0},{5,1},{6,2},{7,3},{8,12},{9,13},{10,... | collective-permute-start | bytes 49160 | tf_op jit(solution)/shard_map/ppermute | solution.py:191
  5.7 1.7 %collective-permute-start.5 = (bf16[256,1024]{1,0:T(8,128)(2,1)}, bf16[256,1024]{1,0:T(8,128)(2,1)S(1)}, u32[]{:S(2)}, u32[]{:S(2)}) collective-permute-start(bf16[256,1024]{1,0:T(8,128)(2,1)} %refs_0_.1), channel_id=1, source_target_pairs={{0,2},{1,3},{2,0},{3,1},{4,6},{5,7},{6,4},{7,5},{8,10},{9,11},{10,... | collective-permute-start | bytes 1572872 | tf_op jit(solution)/shard_map/ppermute | solution.py:191
  7.4 0.7 %constant_dynamic-update-slice_fusion.5 = bf16[16,1024]{1,0:T(8,128)(2,1)S(1)} fusion(bf16[8,1024]{1,0:T(8,128)(2,1)} %param.9), kind=kLoop, calls=%fused_computation.5 | loop fusion | bytes 32768
  8.1 0.8 %constant_dynamic-update-slice_fusion.3 = bf16[32,1024]{1,0:T(8,128)(2,1)S(1)} fusion(bf16[8,1024]{1,0:T(8,128)(2,1)} %param.8), kind=kLoop, calls=%fused_computation.3 | loop fusion | bytes 32768
  8.9 1.7 %collective-permute-start.7 = (bf16[64,1024]{1,0:T(8,128)(2,1)S(1)}, bf16[64,1024]{1,0:T(8,128)(2,1)S(1)}, u32[]{:S(2)}, u32[]{:S(2)}) collective-permute-start(bf16[64,1024]{1,0:T(8,128)(2,1)S(1)} %constant_dynamic-slice_fusion.refs_0_), channel_id=1, source_target_pairs={{0,8},{1,9},{2,10},{3,11},{4,12},{5,13},{6,14},{7,15},{8,0},{9,1},... | collective-permute-start | bytes 393224 | tf_op jit(solution)/shard_map/ppermute | solution.py:191
  10.6 2.4 %collective-permute-start.11 = (bf16[16,1024]{1,0:T(8,128)(2,1)S(1)}, bf16[16,1024]{1,0:T(8,128)(2,1)S(1)}, u32[]{:S(2)}, u32[]{:S(2)}) collective-permute-start(bf16[16,1024]{1,0:T(8,128)(2,1)S(1)} %constant_dynamic-update-slice_fusion.4.refs_0_), channel_id=1, source_target_pairs={{0,6},{1,7},{2,4},{3,5},{4,2},{5,3},{6,0},{7,1},{8,14},{9,15},{10,... | collective-permute-start | bytes 98312 | tf_op jit(solution)/shard_map/ppermute | solution.py:191
  13.2 1.5 %collective-permute-start.9 = (bf16[16,1024]{1,0:T(8,128)(2,1)S(1)}, bf16[16,1024]{1,0:T(8,128)(2,1)S(1)}, u32[]{:S(2)}, u32[]{:S(2)}) collective-permute-start(bf16[16,1024]{1,0:T(8,128)(2,1)S(1)} %constant_dynamic-update-slice_fusion.4.refs_0_), channel_id=1, source_target_pairs={{0,2},{1,3},{2,0},{3,1},{4,6},{5,7},{6,4},{7,5},{8,10},{9,11},{10,... | collective-permute-start | bytes 98312 | tf_op jit(solution)/shard_map/ppermute | solution.py:191
  14.6 0.9 %collective-permute-done.11.refs_3_ = bf16[16,1024]{1,0:T(8,128)(2,1)S(1)} collective-permute-done((bf16[16,1024]{1,0:T(8,128)(2,1)S(1)}, bf16[16,1024]{1,0:T(8,128)(2,1)S(1)}, u32[]{:S(2)}, u32[]{:S(2)}) %collective-permute-start.11) | collective-permute-done | bytes 32800 | tf_op jit(solution)/shard_map/ppermute | solution.py:191
  15.5 0.7 %copy.9.refs_4_.refs_6_ = s32[10,1]{1,0:T(8,128)S(1)} copy(s32[10,1]{0,1:T(1,128)} %bitcast.8) | data formatting | bytes 80 | tf_op jit(solution)/shard_map/broadcast_in_dim | solution.py:102
  16.2 2.2 %collective-permute-done.10.refs_2_ = bf16[16,1024]{1,0:T(8,128)(2,1)S(1)} collective-permute-done((bf16[16,1024]{1,0:T(8,128)(2,1)S(1)}, bf16[16,1024]{1,0:T(8,128)(2,1)S(1)}, u32[]{:S(2)}, u32[]{:S(2)}) %collective-permute-start.10) | collective-permute-done | bytes 32800 | tf_op jit(solution)/shard_map/ppermute | solution.py:191
  18.4 3.2 %collective-permute-done.9.refs_1_ = bf16[16,1024]{1,0:T(8,128)(2,1)S(1)} collective-permute-done((bf16[16,1024]{1,0:T(8,128)(2,1)S(1)}, bf16[16,1024]{1,0:T(8,128)(2,1)S(1)}, u32[]{:S(2)}, u32[]{:S(2)}) %collective-permute-start.9) | collective-permute-done | bytes 32800 | tf_op jit(solution)/shard_map/ppermute | solution.py:191
  21.6 0.7 %copy-done.2 = s32[256,10]{0,1:T(8,128)S(1)} copy-done((s32[256,10]{0,1:T(8,128)S(1)}, s32[256,10]{0,1:T(8,128)}, u32[]{:S(2)}) %copy-start.2) | copy-done | bytes 10264
  22.3 0.7 %copy-done.3 = s32[256]{0:T(256)S(1)} copy-done((s32[256]{0:T(256)S(1)}, s32[256]{0:T(256)}, u32[]{:S(2)}) %copy-start.3) | copy-done | bytes 1048
  23.0 0.7 %shard_map.85.refs_2_ = bf16[1024,512]{1,0:T(8,128)(2,1)S(1)} custom-call(bf16[16,1024]{1,0:T(8,128)(2,1)S(1)} %constant_dynamic-update-slice_fusion.4.refs_0_, bf16[16,1024]{1,0:T(8,128)(2,1)S(1)} %collective-permute-done.9.refs_1_, bf16[16,1024]{1,0:T(8,128)(2,1)S(1)} %collective-permute-done.10.refs_2_, ...), custom_call_target="tpu_custom_call" | custom-call | tf_op jit(solution)/shard_map/pallas_call | solution.py:96
  23.7 0.5 %shard_map.86 = (bf16[128,256]{1,0:T(8,128)(2,1)S(1)}, bf16[128,256]{1,0:T(8,128)(2,1)S(1)}) custom-call(bf16[64,1024]{1,0:T(8,128)(2,1)S(1)} %constant_dynamic-slice_fusion.refs_0_, bf16[64,1024]{1,0:T(8,128)(2,1)S(1)} %collective-permute-done.7.refs_1_, bf16[1024,512]{1,0:T(8,128)(2,1)S(1)} %shard_map.85.refs_2_), custom_call_target="tpu_custom_call" | custom-call | tf_op jit(solution)/shard_map/pallas_call | solution.py:122
  24.2 1.9 %collective-permute-start.14 = (bf16[128,256]{1,0:T(8,128)(2,1)S(1)}, bf16[128,256]{1,0:T(8,128)(2,1)S(1)}, u32[]{:S(2)}, u32[]{:S(2)}) collective-permute-start(bf16[128,256]{1,0:T(8,128)(2,1)S(1)} %get-tuple-element.16), channel_id=1, source_target_pairs={{0,6},{1,7},{2,4},{3,5},{4,2},{5,3},{6,0},{7,1},{8,14},{9,15},{10,... | collective-permute-start | bytes 196616 | tf_op jit(solution)/shard_map/ppermute | solution.py:191
  26.1 0.7 %shard_map.82.refs_1_ = bf16[1024,512]{1,0:T(8,128)(2,1)S(1)} custom-call(bf16[32,1024]{1,0:T(8,128)(2,1)S(1)} %constant_dynamic-update-slice_fusion.refs_0_, bf16[32,1024]{1,0:T(8,128)(2,1)S(1)} %collective-permute-done.3.refs_1_, s32[1,256]{1,0:T(1,128)S(1)} %bitcast.7, s32[10,256]{1,0:T(8,128)S(1)} %bitcast.5, s32[10,1]{1,0:T(8,128)S(1)} %copy.9.refs_4_.refs_6_), custom_call_target="tpu_custom_call" | custom-call | tf_op jit(solution)/shard_map/pallas_call | solution.py:96
  27.3 1.4 %collective-permute-start.13 = (bf16[128,256]{1,0:T(8,128)(2,1)S(1)}, bf16[128,256]{1,0:T(8,128)(2,1)S(1)}, u32[]{:S(2)}, u32[]{:S(2)}) collective-permute-start(bf16[128,256]{1,0:T(8,128)(2,1)S(1)} %get-tuple-element.16), channel_id=1, source_target_pairs={{0,4},{1,5},{2,6},{3,7},{4,0},{5,1},{6,2},{7,3},{8,12},{9,13},{10,... | collective-permute-start | bytes 196616 | tf_op jit(solution)/shard_map/ppermute | solution.py:191
  29.8 2.0 %collective-permute-done.13.refs_6_ = bf16[128,256]{1,0:T(8,128)(2,1)S(1)} collective-permute-done((bf16[128,256]{1,0:T(8,128)(2,1)S(1)}, bf16[128,256]{1,0:T(8,128)(2,1)S(1)}, u32[]{:S(2)}, u32[]{:S(2)}) %collective-permute-start.13) | collective-permute-done | bytes 65568 | tf_op jit(solution)/shard_map/ppermute | solution.py:191
  31.8 0.5 %collective-permute-start.17 = (bf16[128,256]{1,0:T(8,128)(2,1)S(1)}, bf16[128,256]{1,0:T(8,128)(2,1)S(1)}, u32[]{:S(2)}, u32[]{:S(2)}) collective-permute-start(bf16[128,256]{1,0:T(8,128)(2,1)S(1)} %collective-permute-done.13.refs_6_), channel_id=1, source_target_pairs={{0,1},{1,0},{2,3},{3,2},{4,5},{5,4},{6,7},{7,6},{8,9},{9,8},{10,11... | collective-permute-start | bytes 196616 | tf_op jit(solution)/shard_map/ppermute | solution.py:191
  32.3 0.9 %collective-permute-done.12.refs_5_ = bf16[128,256]{1,0:T(8,128)(2,1)S(1)} collective-permute-done((bf16[128,256]{1,0:T(8,128)(2,1)S(1)}, bf16[128,256]{1,0:T(8,128)(2,1)S(1)}, u32[]{:S(2)}, u32[]{:S(2)}) %collective-permute-start.12) | collective-permute-done | bytes 65568 | tf_op jit(solution)/shard_map/ppermute | solution.py:191
  33.2 1.2 %collective-permute-done.16.refs_9_ = bf16[128,256]{1,0:T(8,128)(2,1)S(1)} collective-permute-done((bf16[128,256]{1,0:T(8,128)(2,1)S(1)}, bf16[128,256]{1,0:T(8,128)(2,1)S(1)}, u32[]{:S(2)}, u32[]{:S(2)}) %collective-permute-start.16) | collective-permute-done | bytes 65568 | tf_op jit(solution)/shard_map/ppermute | solution.py:191
  34.5 1.7 %shard_map.87 = bf16[1024,1024]{1,0:T(8,128)(2,1)} custom-call(bf16[256,256]{1,0:T(8,128)(2,1)S(1)} %get-tuple-element.11.refs_0_, bf16[256,256]{1,0:T(8,128)(2,1)S(1)} %collective-permute-done.4.refs_1_, bf16[256,256]{1,0:T(8,128)(2,1)S(1)} %get-tuple-element.13.refs_2_, bf16[256,256]{1,0:T(8,128)(2,1)S(1)} %collective-permute-done.6.refs_3_, ...), custom_call_target="tpu_custom_call" | custom-call | tf_op jit(solution)/shard_map/pallas_call | solution.py:164
  (38 shorter events, 1.7 us)
Async XLA Ops:
  0.0 8.1 %copy-start = (bf16[256,1024]{1,0:T(8,128)(2,1)S(1)}, bf16[256,1024]{1,0:T(8,128)(2,1)}, u32[]{:S(2)}) copy-start(bf16[256,1024]{1,0:T(8,128)(2,1)} %param.11) | copy-start | bytes 1572868
  0.0 26.1 %copy-start.4 = (s32[256]{0:T(256)S(1)}, s32[256]{0:T(256)}, u32[]{:S(2)}) copy-start(s32[256]{0:T(256)} %param.12) | copy-start | bytes 3076
  0.0 13.0 %collective-permute-start.1 = (bf16[8,1024]{1,0:T(8,128)(2,1)}, bf16[8,1024]{1,0:T(8,128)(2,1)S(1)}, u32[]{:S(2)}, u32[]{:S(2)}) collective-permute-start(bf16[8,1024]{1,0:T(8,128)(2,1)} %param.8), channel_id=1, source_target_pairs={{0,8},{1,9},{2,10},{3,11},{4,12},{5,13},{6,14},{7,15},{8,0},{9,1},... | collective-permute-start | bytes 49160 | tf_op jit(solution)/shard_map/ppermute | solution.py:191
  4.1 6.5 %collective-permute-start = (bf16[8,1024]{1,0:T(8,128)(2,1)}, bf16[8,1024]{1,0:T(8,128)(2,1)S(1)}, u32[]{:S(2)}, u32[]{:S(2)}) collective-permute-start(bf16[8,1024]{1,0:T(8,128)(2,1)} %param.8), channel_id=1, source_target_pairs={{0,4},{1,5},{2,6},{3,7},{4,0},{5,1},{6,2},{7,3},{8,12},{9,13},{10,... | collective-permute-start | bytes 49160 | tf_op jit(solution)/shard_map/ppermute | solution.py:191
  5.6 7.5 %collective-permute-start.2 = (bf16[8,1024]{1,0:T(8,128)(2,1)}, bf16[8,1024]{1,0:T(8,128)(2,1)S(1)}, u32[]{:S(2)}, u32[]{:S(2)}) collective-permute-start(bf16[8,1024]{1,0:T(8,128)(2,1)} %param.8), channel_id=1, source_target_pairs={{0,12},{1,13},{2,14},{3,15},{4,8},{5,9},{6,10},{7,11},{8,4},{9,5},... | collective-permute-start | bytes 49160 | tf_op jit(solution)/shard_map/ppermute | solution.py:191
  5.7 3.2 %collective-permute-start.8 = (bf16[8,1024]{1,0:T(8,128)(2,1)}, bf16[8,1024]{1,0:T(8,128)(2,1)S(1)}, u32[]{:S(2)}, u32[]{:S(2)}) collective-permute-start(bf16[8,1024]{1,0:T(8,128)(2,1)} %param.9), channel_id=1, source_target_pairs={{0,1},{1,0},{2,3},{3,2},{4,5},{5,4},{6,7},{7,6},{8,9},{9,8},{10,11... | collective-permute-start | bytes 49160 | tf_op jit(solution)/shard_map/ppermute | solution.py:191
  5.7 23.2 %collective-permute-start.5 = (bf16[256,1024]{1,0:T(8,128)(2,1)}, bf16[256,1024]{1,0:T(8,128)(2,1)S(1)}, u32[]{:S(2)}, u32[]{:S(2)}) collective-permute-start(bf16[256,1024]{1,0:T(8,128)(2,1)} %refs_0_.1), channel_id=1, source_target_pairs={{0,2},{1,3},{2,0},{3,1},{4,6},{5,7},{6,4},{7,5},{8,10},{9,11},{10,... | collective-permute-start | bytes 1572872 | tf_op jit(solution)/shard_map/ppermute | solution.py:191
  8.1 18.7 %copy-start.1 = (bf16[256,1024]{1,0:T(8,128)(2,1)S(1)}, bf16[256,1024]{1,0:T(8,128)(2,1)}, u32[]{:S(2)}) copy-start(bf16[256,1024]{1,0:T(8,128)(2,1)} %refs_0_.1) | copy-start | bytes 1572868
  8.9 14.8 %collective-permute-start.7 = (bf16[64,1024]{1,0:T(8,128)(2,1)S(1)}, bf16[64,1024]{1,0:T(8,128)(2,1)S(1)}, u32[]{:S(2)}, u32[]{:S(2)}) collective-permute-start(bf16[64,1024]{1,0:T(8,128)(2,1)S(1)} %constant_dynamic-slice_fusion.refs_0_), channel_id=1, source_target_pairs={{0,8},{1,9},{2,10},{3,11},{4,12},{5,13},{6,14},{7,15},{8,0},{9,1},... | collective-permute-start | bytes 393224 | tf_op jit(solution)/shard_map/ppermute | solution.py:191
  10.6 4.9 %collective-permute-start.11 = (bf16[16,1024]{1,0:T(8,128)(2,1)S(1)}, bf16[16,1024]{1,0:T(8,128)(2,1)S(1)}, u32[]{:S(2)}, u32[]{:S(2)}) collective-permute-start(bf16[16,1024]{1,0:T(8,128)(2,1)S(1)} %constant_dynamic-update-slice_fusion.4.refs_0_), channel_id=1, source_target_pairs={{0,6},{1,7},{2,4},{3,5},{4,2},{5,3},{6,0},{7,1},{8,14},{9,15},{10,... | collective-permute-start | bytes 98312 | tf_op jit(solution)/shard_map/ppermute | solution.py:191
  13.0 5.4 %collective-permute-start.10 = (bf16[16,1024]{1,0:T(8,128)(2,1)S(1)}, bf16[16,1024]{1,0:T(8,128)(2,1)S(1)}, u32[]{:S(2)}, u32[]{:S(2)}) collective-permute-start(bf16[16,1024]{1,0:T(8,128)(2,1)S(1)} %constant_dynamic-update-slice_fusion.4.refs_0_), channel_id=1, source_target_pairs={{0,4},{1,5},{2,6},{3,7},{4,0},{5,1},{6,2},{7,3},{8,12},{9,13},{10,... | collective-permute-start | bytes 98312 | tf_op jit(solution)/shard_map/ppermute | solution.py:191
  13.2 8.5 %collective-permute-start.9 = (bf16[16,1024]{1,0:T(8,128)(2,1)S(1)}, bf16[16,1024]{1,0:T(8,128)(2,1)S(1)}, u32[]{:S(2)}, u32[]{:S(2)}) collective-permute-start(bf16[16,1024]{1,0:T(8,128)(2,1)S(1)} %constant_dynamic-update-slice_fusion.4.refs_0_), channel_id=1, source_target_pairs={{0,2},{1,3},{2,0},{3,1},{4,6},{5,7},{6,4},{7,5},{8,10},{9,11},{10,... | collective-permute-start | bytes 98312 | tf_op jit(solution)/shard_map/ppermute | solution.py:191
  15.5 10.6 %collective-permute-start.3 = (bf16[32,1024]{1,0:T(8,128)(2,1)S(1)}, bf16[32,1024]{1,0:T(8,128)(2,1)S(1)}, u32[]{:S(2)}, u32[]{:S(2)}) collective-permute-start(bf16[32,1024]{1,0:T(8,128)(2,1)S(1)} %constant_dynamic-update-slice_fusion.refs_0_), channel_id=1, source_target_pairs={{0,1},{1,0},{2,3},{3,2},{4,5},{5,4},{6,7},{7,6},{8,9},{9,8},{10,11... | collective-permute-start | bytes 196616 | tf_op jit(solution)/shard_map/ppermute | solution.py:191
  21.6 0.7 %copy-start.2 = (s32[256,10]{0,1:T(8,128)S(1)}, s32[256,10]{0,1:T(8,128)}, u32[]{:S(2)}) copy-start(s32[256,10]{0,1:T(8,128)} %param.14) | copy-start | bytes 30724
  22.3 0.7 %copy-start.3 = (s32[256]{0:T(256)S(1)}, s32[256]{0:T(256)}, u32[]{:S(2)}) copy-start(s32[256]{0:T(256)} %param.13) | copy-start | bytes 3076
  24.2 5.4 %collective-permute-start.14 = (bf16[128,256]{1,0:T(8,128)(2,1)S(1)}, bf16[128,256]{1,0:T(8,128)(2,1)S(1)}, u32[]{:S(2)}, u32[]{:S(2)}) collective-permute-start(bf16[128,256]{1,0:T(8,128)(2,1)S(1)} %get-tuple-element.16), channel_id=1, source_target_pairs={{0,6},{1,7},{2,4},{3,5},{4,2},{5,3},{6,0},{7,1},{8,14},{9,15},{10,... | collective-permute-start | bytes 196616 | tf_op jit(solution)/shard_map/ppermute | solution.py:191
  27.2 6.0 %collective-permute-start.4 = (bf16[256,256]{1,0:T(8,128)(2,1)S(1)}, bf16[256,256]{1,0:T(8,128)(2,1)S(1)}, u32[]{:S(2)}, u32[]{:S(2)}) collective-permute-start(bf16[256,256]{1,0:T(8,128)(2,1)S(1)} %get-tuple-element.12), channel_id=1, source_target_pairs={{0,1},{1,0},{2,3},{3,2},{4,5},{5,4},{6,7},{7,6},{8,9},{9,8},{10,11... | collective-permute-start | bytes 393224 | tf_op jit(solution)/shard_map/ppermute | solution.py:191
  27.3 4.5 %collective-permute-start.13 = (bf16[128,256]{1,0:T(8,128)(2,1)S(1)}, bf16[128,256]{1,0:T(8,128)(2,1)S(1)}, u32[]{:S(2)}, u32[]{:S(2)}) collective-permute-start(bf16[128,256]{1,0:T(8,128)(2,1)S(1)} %get-tuple-element.16), channel_id=1, source_target_pairs={{0,4},{1,5},{2,6},{3,7},{4,0},{5,1},{6,2},{7,3},{8,12},{9,13},{10,... | collective-permute-start | bytes 196616 | tf_op jit(solution)/shard_map/ppermute | solution.py:191
  28.7 3.1 %collective-permute-start.15 = (bf16[128,256]{1,0:T(8,128)(2,1)S(1)}, bf16[128,256]{1,0:T(8,128)(2,1)S(1)}, u32[]{:S(2)}, u32[]{:S(2)}) collective-permute-start(bf16[128,256]{1,0:T(8,128)(2,1)S(1)} %get-tuple-element.15.refs_4_), channel_id=1, source_target_pairs={{0,1},{1,0},{2,3},{3,2},{4,5},{5,4},{6,7},{7,6},{8,9},{9,8},{10,11... | collective-permute-start | bytes 196616 | tf_op jit(solution)/shard_map/ppermute | solution.py:191
  28.8 4.4 %collective-permute-start.12 = (bf16[128,256]{1,0:T(8,128)(2,1)S(1)}, bf16[128,256]{1,0:T(8,128)(2,1)S(1)}, u32[]{:S(2)}, u32[]{:S(2)}) collective-permute-start(bf16[128,256]{1,0:T(8,128)(2,1)S(1)} %get-tuple-element.15.refs_4_), channel_id=1, source_target_pairs={{0,2},{1,3},{2,0},{3,1},{4,6},{5,7},{6,4},{7,5},{8,10},{9,11},{10,... | collective-permute-start | bytes 196616 | tf_op jit(solution)/shard_map/ppermute | solution.py:191
  29.6 4.8 %collective-permute-start.6 = (bf16[256,256]{1,0:T(8,128)(2,1)S(1)}, bf16[256,256]{1,0:T(8,128)(2,1)S(1)}, u32[]{:S(2)}, u32[]{:S(2)}) collective-permute-start(bf16[256,256]{1,0:T(8,128)(2,1)S(1)} %get-tuple-element.14), channel_id=1, source_target_pairs={{0,1},{1,0},{2,3},{3,2},{4,5},{5,4},{6,7},{7,6},{8,9},{9,8},{10,11... | collective-permute-start | bytes 393224 | tf_op jit(solution)/shard_map/ppermute | solution.py:191
  31.8 1.4 %collective-permute-start.18 = (bf16[128,256]{1,0:T(8,128)(2,1)S(1)}, bf16[128,256]{1,0:T(8,128)(2,1)S(1)}, u32[]{:S(2)}, u32[]{:S(2)}) collective-permute-start(bf16[128,256]{1,0:T(8,128)(2,1)S(1)} %collective-permute-done.14.refs_7_), channel_id=1, source_target_pairs={{0,1},{1,0},{2,3},{3,2},{4,5},{5,4},{6,7},{7,6},{8,9},{9,8},{10,11... | collective-permute-start | bytes 196616 | tf_op jit(solution)/shard_map/ppermute | solution.py:191
  31.8 1.4 %collective-permute-start.17 = (bf16[128,256]{1,0:T(8,128)(2,1)S(1)}, bf16[128,256]{1,0:T(8,128)(2,1)S(1)}, u32[]{:S(2)}, u32[]{:S(2)}) collective-permute-start(bf16[128,256]{1,0:T(8,128)(2,1)S(1)} %collective-permute-done.13.refs_6_), channel_id=1, source_target_pairs={{0,1},{1,0},{2,3},{3,2},{4,5},{5,4},{6,7},{7,6},{8,9},{9,8},{10,11... | collective-permute-start | bytes 196616 | tf_op jit(solution)/shard_map/ppermute | solution.py:191
  33.2 1.3 %collective-permute-start.16 = (bf16[128,256]{1,0:T(8,128)(2,1)S(1)}, bf16[128,256]{1,0:T(8,128)(2,1)S(1)}, u32[]{:S(2)}, u32[]{:S(2)}) collective-permute-start(bf16[128,256]{1,0:T(8,128)(2,1)S(1)} %collective-permute-done.12.refs_5_), channel_id=1, source_target_pairs={{0,1},{1,0},{2,3},{3,2},{4,5},{5,4},{6,7},{7,6},{8,9},{9,8},{10,11... | collective-permute-start | bytes 196616 | tf_op jit(solution)/shard_map/ppermute | solution.py:191

commit v2 on v0

v2 whole, which is shorter than its diff:
```python
import functools

import jax
import jax.numpy as jnp
from jax import lax
from jax.experimental import pallas as pl
from jax.experimental.pallas import tpu as pltpu
from jax.sharding import PartitionSpec as P


DEVICE_AXES = ("path", "half", "tile")
CONTRACT_LAST = (((1,), (1,)), ((), ()))


def cut_factors(branch, cut_side, gate_count, on_left):
    cut_count = cut_side.shape[0]
    bit_place = lax.broadcasted_iota(jnp.int32, (cut_count, gate_count), 0)
    gate_code = lax.broadcasted_iota(jnp.int32, (cut_count, gate_count), 1)
    bit_table = jnp.right_shift(gate_code, bit_place) & 1
    projector = cut_side if on_left else 1 - cut_side
    phased = 1 - projector
    chosen = branch * projector[None, :]
    misses = (
        jnp.sum(chosen, axis=1, keepdims=True)
        + jnp.dot(projector, bit_table)[None, :]
        - 2 * jnp.dot(chosen, bit_table)
    )
    parity = jnp.dot(branch * phased[None, :], bit_table)
    sign_value = 1 - 2 * (parity % 2)
    return jnp.where(misses == 0, sign_value, 0).astype(jnp.bfloat16)


def gathered(
    left_prefix, right_prefix, left_layer, right_layer, left_map, right_map, branch_bits, cut_side
):
    def states(prefix, prefix_axes, layer, layer_axes, path_map, on_left):
        rows = lax.all_gather(prefix, prefix_axes, axis=0, tiled=True)
        factor = cut_factors(branch_bits, cut_side, rows.shape[1], on_left)
        whole_layer = lax.all_gather(layer, layer_axes, axis=0, tiled=True)
        applied = lax.dot_general(
            rows[path_map] * factor, whole_layer, CONTRACT_LAST, preferred_element_type=jnp.float32
        )
        return applied.astype(jnp.bfloat16)

    left_states = states(left_prefix, "path", left_layer, ("half", "tile"), left_map, True)
    right_states = states(right_prefix, ("half", "tile"), right_layer, "path", right_map, False)
    amplitude = lax.dot_general(
        left_states, right_states, (((0,), (0,)), ((), ())), preferred_element_type=jnp.float32
    )
    return amplitude.astype(jnp.bfloat16)


def call(kernel, outs, *operands, in_space=pltpu.VMEM, scratch=(), out_space=pltpu.VMEM):
    shapes = [jax.ShapeDtypeStruct(shape, jnp.bfloat16) for shape in outs]
    spaces = [in_space] * len(operands)
    if in_space == pltpu.HBM:
        operands = [pltpu.with_memory_space_constraint(x, in_space) for x in operands]
    return pl.pallas_call(
        kernel,
        out_shape=shapes,
        in_specs=[pl.BlockSpec(memory_space=space) for space in spaces],
        out_specs=[pl.BlockSpec(memory_space=out_space)] * len(shapes),
        scratch_shapes=list(scratch),
        compiler_params=pltpu.CompilerParams(vmem_limit_bytes=16 << 20),
    )(*operands)


def spot_of():
    return lax.axis_index("half") * lax.axis_size("tile") + lax.axis_index("tile")


def stage_kernel(*refs):
    sources, (outs, held, sems) = refs[:7], (refs[7:14], refs[14:18], refs[18])
    share = outs[2].shape[0]
    start = pl.multiple_of(spot_of() * share, share)
    copies = []
    for k, source in enumerate(sources):
        if k == 2:
            source = source.at[pl.ds(start, share), :]
        target = outs[k] if k < 3 else held[k - 3]
        copies.append(pltpu.make_async_copy(source, target, sems.at[k]))
        copies[-1].start()
    for copy in copies[3:]:
        copy.wait()
    side_ref, branch_ref, left_map_ref, right_map_ref = held
    out_refs = outs[3:]
    cuts, paths = branch_ref.shape
    tiles = lax.axis_size("half") * lax.axis_size("tile")
    for on_left, map_ref, shard, shards, (factor_ref, pick_ref) in (
        (True, left_map_ref, lax.axis_index("path"), lax.axis_size("path"), out_refs[:2]),
        (False, right_map_ref, spot_of(), tiles, out_refs[2:]),
    ):
        wanted = jnp.zeros((1, paths), jnp.int32)
        phased = jnp.zeros((1, paths), jnp.int32)
        mask = jnp.int32(0)
        for cut in range(cuts):
            projector = side_ref[cut] if on_left else 1 - side_ref[cut]
            bits = branch_ref[pl.ds(cut, 1), :]
            wanted += bits * (projector << cut)
            phased += bits * ((1 - projector) << cut)
            mask += projector << cut
        gate = lax.broadcasted_iota(jnp.int32, factor_ref.shape, 0)
        hit = (gate & mask) == wanted
        odd = (lax.population_count(gate & phased) & 1) == 1
        factor = jnp.where(hit, jnp.where(odd, -1.0, 1.0), 0.0)
        factor_ref[...] = factor.astype(jnp.bfloat16)
        rows = pick_ref.shape[0]
        depth = rows // shards
        row = map_ref[...]
        place = (lax.div(row, depth) ^ shard) * depth + lax.rem(row, depth)
        index = lax.broadcasted_iota(jnp.int32, pick_ref.shape, 0)
        pick_ref[...] = jnp.where(index == place, 1.0, 0.0).astype(jnp.bfloat16)
    for copy in copies[:3]:
        copy.wait()


def pack_kernel(right_ref, right_t_ref, left_ref, left_t_ref, rows_ref, pair_ref, near_ref, far_ref):
    depth = right_ref.shape[0]
    pair = jnp.concatenate([right_ref[...], right_t_ref[...]], axis=0)
    left = jnp.concatenate([left_ref[...], left_t_ref[...]], axis=0)
    pair_ref[...] = pair
    near_ref[pl.ds(0, 2 * depth), :] = pair
    near_ref[pl.ds(2 * depth, 2 * depth), :] = left
    share = rows_ref.shape[0]
    far_ref[pl.ds(0, share), :] = rows_ref[...]
    far_ref[pl.ds(share, 2 * depth), :] = left


def project_kernel(pieces, factor_ref, pick_ref, *refs):
    prefix_refs, out_ref = refs[:-1], refs[-1]
    paths = pick_ref.shape[1]
    factor = factor_ref[...].astype(jnp.float32)
    for block, sources in enumerate(pieces):
        rows = jnp.concatenate(
            [prefix_refs[k][pl.ds(first, count), :] for k, first, count in sources], axis=0
        )
        picked = lax.dot_general(
            rows, pick_ref[...], (((0,), (0,)), ((), ())), preferred_element_type=jnp.float32
        )
        out_ref[:, pl.ds(block * paths, paths)] = (picked * factor).astype(jnp.bfloat16)


def right_own_kernel(layer_ref, projected_ref, out_ref):
    paths = out_ref.shape[1]
    out_ref[...] = jnp.dot(
        layer_ref[...], projected_ref[:, :paths], preferred_element_type=jnp.float32
    ).astype(jnp.bfloat16)


def right_far_kernel(layer_ref, far_ref, projected_ref, mine_ref, near_ref, cross_ref):
    share, paths = mine_ref.shape
    half = near_ref.shape[0] - share
    start = pl.multiple_of(lax.axis_index("tile") * half, half)
    far = jnp.dot(
        far_ref[pl.ds(0, share), :], projected_ref[...], preferred_element_type=jnp.float32
    ).astype(jnp.bfloat16)
    mine_ref[...] = far[:, :paths]
    cross_ref[...] = far[:, paths:]
    near_ref[pl.ds(half, share), :] = far[:, paths:]
    near_ref[pl.ds(0, half), :] = jnp.dot(
        layer_ref[pl.ds(start, half), :],
        projected_ref[:, paths:],
        preferred_element_type=jnp.float32,
    ).astype(jnp.bfloat16)


def left_kernel(layer_ref, projected_ref, mine_ref, other_ref):
    paths = mine_ref.shape[1]
    states = jnp.dot(
        layer_ref[...], projected_ref[...], preferred_element_type=jnp.float32
    ).astype(jnp.bfloat16)
    mine_ref[...] = states[:, :paths]
    other_ref[...] = states[:, paths:]


def amplitude_kernel(left_count, *refs):
    left_refs, right_refs = refs[:left_count], refs[left_count:-4]
    out_ref, right_ref, block_ref, sems = refs[-4:]
    own_ref, mine_ref, x_ref, z_ref, xz_ref, mine_t_ref, x_t_ref, z_t_ref, xz_t_ref = right_refs
    path, tile, spot = lax.axis_index("path"), lax.axis_index("tile"), spot_of()
    tiles = lax.axis_size("tile")
    chunk, share = own_ref.shape[0], mine_ref.shape[0]
    half = z_ref.shape[0] - share

    def place(ref, first, count, plane, offset):
        start = pl.multiple_of((path ^ plane) * chunk + offset, count)
        right_ref[pl.ds(start, count), :] = ref[pl.ds(first, count), :]

    place(own_ref, 0, chunk, 0, 0)
    place(z_ref, 0, half, 1, tile * half)
    place(z_t_ref, 0, half, 1, (tile ^ 1) * half)
    for spin, (near_ref, x_piece, z_piece, xz_piece) in enumerate(
        ((mine_ref, x_ref, z_ref, xz_ref), (mine_t_ref, x_t_ref, z_t_ref, xz_t_ref))
    ):
        place(near_ref, 0, share, 2, (spot ^ spin) * share)
        place(x_piece, 0, share, 2, (spot ^ (spin + tiles)) * share)
        place(z_piece, half, share, 3, (spot ^ spin) * share)
        place(xz_piece, 0, share, 3, (spot ^ (spin + tiles)) * share)
    right = right_ref[...]
    depth = left_refs[0].shape[0]
    copies = []
    for k, (ref, spin) in enumerate(zip(left_refs, (0, 1, tiles, 1 + tiles))):
        block_ref[k] = lax.dot_general(
            ref[...], right, CONTRACT_LAST, preferred_element_type=jnp.float32
        ).astype(jnp.bfloat16)
        start = pl.multiple_of((spot ^ spin) * depth, depth)
        copy = pltpu.make_async_copy(block_ref.at[k], out_ref.at[pl.ds(start, depth), :], sems.at[k])
        copy.start()
        copies.append(copy)
    for copy in copies:
        copy.wait()


def exchanged(
    left_prefix, right_prefix, left_layer, right_layer, left_map, right_map, branch_bits, cut_side
):
    sizes = [lax.axis_size(axis) for axis in DEVICE_AXES]

    def exchange(value, plane=0, half=0, tile=0):
        pairs = []
        for p in range(sizes[0]):
            for h in range(sizes[1]):
                for t in range(sizes[2]):
                    source = (p * sizes[1] + h) * sizes[2] + t
                    target = ((p ^ plane) * sizes[1] + (h ^ half)) * sizes[2] + (t ^ tile)
                    pairs.append((source, target))
        return lax.ppermute(value, DEVICE_AXES, pairs)

    paths = left_map.shape[0]
    depth, gates = right_prefix.shape
    chunk = right_layer.shape[0]
    spots = sizes[1] * sizes[2]
    share = chunk // spots

    right_t = exchange(right_prefix, tile=1)
    left_t = exchange(left_prefix, tile=1)
    bits = branch_bits.T
    prefix_rows = [(sizes[0] * depth, paths), (spots * depth, paths)]
    right_own, left_own, near_rows, left_factor, left_pick, right_factor, right_pick = call(
        stage_kernel,
        [
            (depth, gates), (depth, gates), (share, gates),
            (gates, paths), prefix_rows[0], (gates, paths), prefix_rows[1],
        ],
        right_prefix, left_prefix, right_layer,
        cut_side, bits, left_map[None, :], right_map[None, :],
        in_space=pltpu.HBM,
        scratch=(
            pltpu.SMEM(cut_side.shape, jnp.int32),
            pltpu.VMEM(bits.shape, jnp.int32),
            pltpu.VMEM((1, paths), jnp.int32),
            pltpu.VMEM((1, paths), jnp.int32),
            pltpu.SemaphoreType.DMA((7,)),
        ),
    )
    pair, near_pack, far_pack = call(
        pack_kernel,
        [(2 * depth, gates), (4 * depth, gates), (share + 2 * depth, gates)],
        right_own, right_t, left_own, left_t, near_rows,
    )
    pair_x = exchange(pair, half=1)
    layer_x = exchange(left_layer, half=1)
    far = exchange(far_pack, plane=2)
    pair_xz = exchange(pair, plane=1, half=1)
    near = exchange(near_pack, plane=1)
    left_far = exchange(far_pack[share:], plane=3)

    (right_projected,) = call(
        functools.partial(
            project_kernel,
            (((0, 0, 2 * depth), (1, 0, 2 * depth)), ((2, 0, 2 * depth), (3, 0, 2 * depth))),
        ),
        [(gates, 2 * paths)],
        right_factor, right_pick, pair, pair_x, near, pair_xz,
    )
    (right_near,) = call(right_own_kernel, [(chunk, paths)], right_layer, right_projected)
    mine, for_near, cross = call(
        right_far_kernel,
        [(share, paths), (chunk // sizes[2] + share, paths), (share, paths)],
        right_layer, far, right_projected,
    )
    right_pieces = [
        mine, exchange(mine, half=1), exchange(for_near, plane=1), exchange(cross, plane=1, half=1)
    ]
    right_pieces = right_pieces + [exchange(piece, tile=1) for piece in right_pieces]

    (left_projected,) = call(
        functools.partial(
            project_kernel,
            tuple(
                (
                    (0, share + k * depth, depth),
                    (1, (2 + k) * depth, depth),
                    (2, share + k * depth, depth),
                    (3, k * depth, depth),
                )
                for k in range(2)
            ),
        ),
        [(gates, 2 * paths)],
        left_factor, left_pick, far_pack, near, far, left_far,
    )
    rows = left_layer.shape[0]
    own_mine, own_other = call(left_kernel, [(rows, paths)] * 2, left_layer, left_projected)
    x_mine, x_other = call(left_kernel, [(rows, paths)] * 2, layer_x, left_projected)
    left_pieces = [own_mine, exchange(own_other, tile=1), x_mine, exchange(x_other, tile=1)]
    (amplitude,) = call(
        functools.partial(amplitude_kernel, len(left_pieces)),
        [(spots * rows, sizes[0] * chunk)],
        *left_pieces, right_near, *right_pieces,
        scratch=(
            pltpu.VMEM((sizes[0] * chunk, paths), jnp.bfloat16),
            pltpu.VMEM((len(left_pieces), rows, sizes[0] * chunk), jnp.bfloat16),
            pltpu.SemaphoreType.DMA((len(left_pieces),)),
        ),
        out_space=pl.ANY,
    )
    return amplitude


def solution(mesh):
    in_specs = (
        P(("groups", "path"), ("half", "tile")),
        P(("groups", "half", "tile"), "path"),
        P(("groups", "half", "tile"), None),
        P(("groups", "path"), None),
        P("groups"),
        P("groups"),
        P("groups", None),
        P("groups"),
    )
    out_specs = P(("groups", "half", "tile"), "path")
    squares = (mesh.shape["path"], mesh.shape["half"], mesh.shape["tile"]) == (4, 2, 2)

    def on_device(*arrays):
        return (exchanged if squares else gathered)(*arrays)

    return jax.shard_map(
        on_device, mesh=mesh, in_specs=in_specs, out_specs=out_specs, check_vma=False
    )
```

time: 93 us -> 36.6 us (0.39)
  waiting for transfers between devices: 43 us -> 13.9 us
  blocking collectives: 20.9 us -> 0 us
  starting transfers between devices: 0.04 us -> 16.6 us
  between operations: 13.5 us -> 0.15 us
  matrix products: 12.2 us -> 0 us
  Pallas kernels: 0 us -> 5.77 us
  local copies, waits for them, and re-layouts: 2.36 us -> 0.01 us
    all_gather x2 -> x0, waiting for transfers between devices: 41.6 us -> none  [the longest x1 22.1 us: apply_right(): lax.all_gather(right_layer, 'path', axis=0, tiled=True)]
    all_gather x2 -> x0, blocking collectives: 20.9 us -> none  [the longest x1 14.5 us: on_device(): left_rows = lax.all_gather(left_prefix, 'path', axis=0, tiled=True)]
    ppermute x0 -> x17, starting transfers between devices: none -> 16.6 us  [exchange(): return lax.ppermute(value, DEVICE_AXES, pairs)]
    ppermute x0 -> x17, waiting for transfers between devices: none -> 13.9 us  [exchange(): return lax.ppermute(value, DEVICE_AXES, pairs)]
    dot_general x6 -> x0, matrix products: 12.2 us -> none  [the longest x1 4.84 us: on_device(): lax.dot_general(left_states, right_states, (((0,), (0,)), ((), ())), pref...]
    pallas_call x0 -> x9, Pallas kernels: none -> 5.77 us  [call(): pl.pallas_call(kernel, out_shape=shapes, in_specs=[pl.BlockSpec(memory_sp...]
    gather x2 -> x0, local copies, waits for them, and re-layouts: 2.34 us -> none  [project(): return prefix_rows[path_map] * factor]
    unnamed x2 -> x0, waiting for transfers between devices: 1.41 us -> none
  transfers between devices with their start and end apart: 2 -> 17, of which waited for: 2 -> 6; matrix products, arithmetic and copies ran while one was open for 11% -> 0% of each run, Pallas kernels for 0% -> 11%
where the time goes in v2:
time: 36.6 us; the launch traced here: 36.5 us
  starting transfers between devices  16.6 us (45%)
  waiting for transfers between devices  13.9 us (38%)
  Pallas kernels  5.77 us (16%)
    ppermute x17, starting transfers between devices, exchange(): return lax.ppermute(value, DEVICE_AXES, pairs)  16.6 us
    ppermute x17, waiting for transfers between devices, exchange(): return lax.ppermute(value, DEVICE_AXES, pairs)  13.9 us
    pallas_call x9, Pallas kernels, call(): pl.pallas_call(kernel, out_shape=shapes, in_specs=[pl.BlockSpec(memory_sp...  5.77 us
  transfers between devices with their start and end apart: 17, of which 6 were waited for; matrix products, arithmetic and copies ran while one was open for 0% of the time, Pallas kernels for 11%

profile of v2, /device:TPU:0, one launch (start us, length us, event | category | flops | bytes accessed | tf_op | source)
XLA Modules:
  0.0 36.5 jit_solution(4257240733612324218)
XLA Ops:
  0.0 3.0 %collective-permute-start.6 = (bf16[256,1024]{1,0:T(8,128)(2,1)}, bf16[256,1024]{1,0:T(8,128)(2,1)S(1)}, u32[]{:S(2)}, u32[]{:S(2)}) collective-permute-start(bf16[256,1024]{1,0:T(8,128)(2,1)} %layer_ref.3), channel_id=1, source_target_pairs={{0,2},{1,3},{2,0},{3,1},{4,6},{5,7},{6,4},{7,5},{8,10},{9,11},{10,... | collective-permute-start | bytes 1572872 | tf_op jit(solution)/shard_map/ppermute | solution.py:227
  3.0 0.5 %collective-permute-start.1 = (bf16[8,1024]{1,0:T(8,128)(2,1)}, bf16[8,1024]{1,0:T(8,128)(2,1)S(1)}, u32[]{:S(2)}, u32[]{:S(2)}) collective-permute-start(bf16[8,1024]{1,0:T(8,128)(2,1)} %refs_1_.1), channel_id=1, source_target_pairs={{0,1},{1,0},{2,3},{3,2},{4,5},{5,4},{6,7},{7,6},{8,9},{9,8},{10,11... | collective-permute-start | bytes 49160 | tf_op jit(solution)/shard_map/ppermute | solution.py:227
  3.5 1.5 %shard_map.82 = (bf16[8,1024]{1,0:T(8,128)(2,1)S(1)}, bf16[8,1024]{1,0:T(8,128)(2,1)S(1)}, bf16[64,1024]{1,0:T(8,128)(2,1)S(1)}, bf16[1024,256]{1,0:T(8,128)(2,1...) custom-call(bf16[8,1024]{1,0:T(8,128)(2,1)} %refs_0_.1, ...), custom_call_target="tpu_custom_call" | custom-call | tf_op jit(solution)/shard_map/pallas_call | solution.py:58
  5.1 2.7 %collective-permute-start.3 = (bf16[80,1024]{1,0:T(8,128)(2,1)S(1)}, bf16[80,1024]{1,0:T(8,128)(2,1)S(1)}, u32[]{:S(2)}, u32[]{:S(2)}) collective-permute-start(bf16[80,1024]{1,0:T(8,128)(2,1)S(1)} %get-tuple-element.27.refs_0_), channel_id=1, source_target_pairs={{0,8},{1,9},{2,10},{3,11},{4,12},{5,13},{6,14},{7,15},{8,0},{9,1},... | collective-permute-start | bytes 491528 | tf_op jit(solution)/shard_map/ppermute | solution.py:227
  7.7 1.6 %collective-permute-start.2 = (bf16[32,1024]{1,0:T(8,128)(2,1)S(1)}, bf16[32,1024]{1,0:T(8,128)(2,1)S(1)}, u32[]{:S(2)}, u32[]{:S(2)}) collective-permute-start(bf16[32,1024]{1,0:T(8,128)(2,1)S(1)} %get-tuple-element.28), channel_id=1, source_target_pairs={{0,4},{1,5},{2,6},{3,7},{4,0},{5,1},{6,2},{7,3},{8,12},{9,13},{10,... | collective-permute-start | bytes 196616 | tf_op jit(solution)/shard_map/ppermute | solution.py:227
  9.3 0.5 %collective-permute-start.8 = (bf16[16,1024]{1,0:T(8,128)(2,1)S(1)}, bf16[16,1024]{1,0:T(8,128)(2,1)S(1)}, u32[]{:S(2)}, u32[]{:S(2)}) collective-permute-start(bf16[16,1024]{1,0:T(8,128)(2,1)S(1)} %get-tuple-element.35.refs_0_), channel_id=1, source_target_pairs={{0,2},{1,3},{2,0},{3,1},{4,6},{5,7},{6,4},{7,5},{8,10},{9,11},{10,... | collective-permute-start | bytes 98312 | tf_op jit(solution)/shard_map/ppermute | solution.py:227
  9.8 1.4 %collective-permute-start.9 = (bf16[16,1024]{1,0:T(8,128)(2,1)S(1)}, bf16[16,1024]{1,0:T(8,128)(2,1)S(1)}, u32[]{:S(2)}, u32[]{:S(2)}) collective-permute-start(bf16[16,1024]{1,0:T(8,128)(2,1)S(1)} %get-tuple-element.35.refs_0_), channel_id=1, source_target_pairs={{0,6},{1,7},{2,4},{3,5},{4,2},{5,3},{6,0},{7,1},{8,14},{9,15},{10,... | collective-permute-start | bytes 98312 | tf_op jit(solution)/shard_map/ppermute | solution.py:227
  11.2 5.3 %collective-permute-done.8.refs_1_ = bf16[16,1024]{1,0:T(8,128)(2,1)S(1)} collective-permute-done((bf16[16,1024]{1,0:T(8,128)(2,1)S(1)}, bf16[16,1024]{1,0:T(8,128)(2,1)S(1)}, u32[]{:S(2)}, u32[]{:S(2)}) %collective-permute-start.8) | collective-permute-done | bytes 32800 | tf_op jit(solution)/shard_map/ppermute | solution.py:227
  16.5 0.5 %shard_map.87.projected_ref = bf16[1024,512]{1,0:T(8,128)(2,1)S(1)} custom-call(bf16[1024,256]{1,0:T(8,128)(2,1)S(1)} %get-tuple-element.33.factor_ref, bf16[32,256]{1,0:T(8,128)(2,1)S(1)} %get-tuple-element.34.pick_ref, bf16[16,1024]{1,0:T(8,128)(2,1)S(1)} %get-tuple-element.35.refs_0_, bf16[16,1024]{1,0:T(8,128)(2,1)S(1)} %collective-permute-done.8.refs_1_, ...), custom_call_target="tpu_custom_call" | custom-call | tf_op jit(solution)/shard_map/pallas_call | solution.py:58
  17.0 0.4 %shard_map.89 = (bf16[64,256]{1,0:T(8,128)(2,1)S(1)}, bf16[192,256]{1,0:T(8,128)(2,1)S(1)}, bf16[64,256]{1,0:T(8,128)(2,1)S(1)}) custom-call(bf16[256,1024]{1,0:T(8,128)(2,1)S(1)} %copy-done, bf16[80,1024]{1,0:T(8,128)(2,1)S(1)} %collective-permute-done.3.refs_2_.far_ref, bf16[1024,512]{1,0:T(8,128)(2,1)S(1)} %shard_map.87.projected_ref), custom_call_target="tpu_custom_call" | custom-call | tf_op jit(solution)/shard_map/pallas_call | solution.py:58
  17.4 1.9 %collective-permute-start.11 = (bf16[192,256]{1,0:T(8,128)(2,1)S(1)}, bf16[192,256]{1,0:T(8,128)(2,1)S(1)}, u32[]{:S(2)}, u32[]{:S(2)}) collective-permute-start(bf16[192,256]{1,0:T(8,128)(2,1)S(1)} %get-tuple-element.37), channel_id=1, source_target_pairs={{0,4},{1,5},{2,6},{3,7},{4,0},{5,1},{6,2},{7,3},{8,12},{9,13},{10,... | collective-permute-start | bytes 294920 | tf_op jit(solution)/shard_map/ppermute | solution.py:227
  19.3 2.5 %collective-permute-start.4 = (bf16[16,1024]{1,0:T(8,128)(2,1)S(1)}, bf16[16,1024]{1,0:T(8,128)(2,1)S(1)}, u32[]{:S(2)}, u32[]{:S(2)}) collective-permute-start(bf16[16,1024]{1,0:T(8,128)(2,1)S(1)} %slice.3), channel_id=1, source_target_pairs={{0,12},{1,13},{2,14},{3,15},{4,8},{5,9},{6,10},{7,11},{8,4},{9,5},... | collective-permute-start | bytes 98312 | tf_op jit(solution)/shard_map/ppermute | solution.py:227
  21.8 3.2 %collective-permute-done.4.refs_3_ = bf16[16,1024]{1,0:T(8,128)(2,1)S(1)} collective-permute-done((bf16[16,1024]{1,0:T(8,128)(2,1)S(1)}, bf16[16,1024]{1,0:T(8,128)(2,1)S(1)}, u32[]{:S(2)}, u32[]{:S(2)}) %collective-permute-start.4) | collective-permute-done | bytes 32800 | tf_op jit(solution)/shard_map/ppermute | solution.py:227
  25.0 0.5 %shard_map.84.projected_ref = bf16[1024,512]{1,0:T(8,128)(2,1)S(1)} custom-call(bf16[1024,256]{1,0:T(8,128)(2,1)S(1)} %get-tuple-element.22.factor_ref, bf16[32,256]{1,0:T(8,128)(2,1)S(1)} %get-tuple-element.23.pick_ref, bf16[80,1024]{1,0:T(8,128)(2,1)S(1)} %get-tuple-element.27.refs_0_, bf16[32,1024]{1,0:T(8,128)(2,1)S(1)} %collective-permute-done.2.refs_1_.refs_2_, ...), custom_call_target="tpu_custom_call" | custom-call | tf_op jit(solution)/shard_map/pallas_call | solution.py:58
  25.5 0.4 %shard_map.85 = (bf16[256,256]{1,0:T(8,128)(2,1)S(1)}, bf16[256,256]{1,0:T(8,128)(2,1)S(1)}) custom-call(bf16[256,1024]{1,0:T(8,128)(2,1)S(1)} %copy-done.1, bf16[1024,512]{1,0:T(8,128)(2,1)S(1)} %shard_map.84.projected_ref), custom_call_target="tpu_custom_call" | custom-call | tf_op jit(solution)/shard_map/pallas_call | solution.py:58
  26.1 0.4 %shard_map.86 = (bf16[256,256]{1,0:T(8,128)(2,1)S(1)}, bf16[256,256]{1,0:T(8,128)(2,1)S(1)}) custom-call(bf16[256,1024]{1,0:T(8,128)(2,1)S(1)} %collective-permute-done.6.layer_ref, bf16[1024,512]{1,0:T(8,128)(2,1)S(1)} %shard_map.84.projected_ref), custom_call_target="tpu_custom_call" | custom-call | tf_op jit(solution)/shard_map/pallas_call | solution.py:58
  26.5 0.6 %collective-permute-start.7 = (bf16[256,256]{1,0:T(8,128)(2,1)S(1)}, bf16[256,256]{1,0:T(8,128)(2,1)S(1)}, u32[]{:S(2)}, u32[]{:S(2)}) collective-permute-start(bf16[256,256]{1,0:T(8,128)(2,1)S(1)} %get-tuple-element.32), channel_id=1, source_target_pairs={{0,1},{1,0},{2,3},{3,2},{4,5},{5,4},{6,7},{7,6},{8,9},{9,8},{10,11... | collective-permute-start | bytes 393224 | tf_op jit(solution)/shard_map/ppermute | solution.py:227
  27.0 1.5 %collective-permute-start.10 = (bf16[64,256]{1,0:T(8,128)(2,1)S(1)}, bf16[64,256]{1,0:T(8,128)(2,1)S(1)}, u32[]{:S(2)}, u32[]{:S(2)}) collective-permute-start(bf16[64,256]{1,0:T(8,128)(2,1)S(1)} %get-tuple-element.36.refs_5_), channel_id=1, source_target_pairs={{0,2},{1,3},{2,0},{3,1},{4,6},{5,7},{6,4},{7,5},{8,10},{9,11},{10,... | collective-permute-start | bytes 98312 | tf_op jit(solution)/shard_map/ppermute | solution.py:227
  28.6 2.4 %collective-permute-done.10.refs_6_ = bf16[64,256]{1,0:T(8,128)(2,1)S(1)} collective-permute-done((bf16[64,256]{1,0:T(8,128)(2,1)S(1)}, bf16[64,256]{1,0:T(8,128)(2,1)S(1)}, u32[]{:S(2)}, u32[]{:S(2)}) %collective-permute-start.10) | collective-permute-done | bytes 32800 | tf_op jit(solution)/shard_map/ppermute | solution.py:227
  31.0 2.4 %collective-permute-done.12.refs_8_ = bf16[64,256]{1,0:T(8,128)(2,1)S(1)} collective-permute-done((bf16[64,256]{1,0:T(8,128)(2,1)S(1)}, bf16[64,256]{1,0:T(8,128)(2,1)S(1)}, u32[]{:S(2)}, u32[]{:S(2)}) %collective-permute-start.12) | collective-permute-done | bytes 32800 | tf_op jit(solution)/shard_map/ppermute | solution.py:227
  33.4 0.5 %collective-permute-start.16 = (bf16[64,256]{1,0:T(8,128)(2,1)S(1)}, bf16[64,256]{1,0:T(8,128)(2,1)S(1)}, u32[]{:S(2)}, u32[]{:S(2)}) collective-permute-start(bf16[64,256]{1,0:T(8,128)(2,1)S(1)} %collective-permute-done.12.refs_8_), channel_id=1, source_target_pairs={{0,1},{1,0},{2,3},{3,2},{4,5},{5,4},{6,7},{7,6},{8,9},{9,8},{10,11... | collective-permute-start | bytes 98312 | tf_op jit(solution)/shard_map/ppermute | solution.py:227
  33.9 0.3 shard_map.88.refs_4_
  34.2 0.4 %collective-permute-done.14.refs_10_ = bf16[64,256]{1,0:T(8,128)(2,1)S(1)} collective-permute-done((bf16[64,256]{1,0:T(8,128)(2,1)S(1)}, bf16[64,256]{1,0:T(8,128)(2,1)S(1)}, u32[]{:S(2)}, u32[]{:S(2)}) %collective-permute-start.14) | collective-permute-done | bytes 32800 | tf_op jit(solution)/shard_map/ppermute | solution.py:227
  34.8 1.7 %shard_map.90 = bf16[1024,1024]{1,0:T(8,128)(2,1)} custom-call(bf16[256,256]{1,0:T(8,128)(2,1)S(1)} %get-tuple-element.29.refs_0_, bf16[256,256]{1,0:T(8,128)(2,1)S(1)} %collective-permute-done.5.refs_1_, bf16[256,256]{1,0:T(8,128)(2,1)S(1)} %get-tuple-element.31.refs_2_, bf16[256,256]{1,0:T(8,128)(2,1)S(1)} %collective-permute-done.7.refs_3_, ...), custom_call_target="tpu_custom_call" | custom-call | tf_op jit(solution)/shard_map/pallas_call | solution.py:58
  (24 shorter events, 0.3 us)
Async XLA Ops:
  0.0 17.0 %copy-start = (bf16[256,1024]{1,0:T(8,128)(2,1)S(1)}, bf16[256,1024]{1,0:T(8,128)(2,1)}, u32[]{:S(2)}) copy-start(bf16[256,1024]{1,0:T(8,128)(2,1)} %layer_ref.5) | copy-start | bytes 1572868
  0.0 26.0 %collective-permute-start.6 = (bf16[256,1024]{1,0:T(8,128)(2,1)}, bf16[256,1024]{1,0:T(8,128)(2,1)S(1)}, u32[]{:S(2)}, u32[]{:S(2)}) collective-permute-start(bf16[256,1024]{1,0:T(8,128)(2,1)} %layer_ref.3), channel_id=1, source_target_pairs={{0,2},{1,3},{2,0},{3,1},{4,6},{5,7},{6,4},{7,5},{8,10},{9,11},{10,... | collective-permute-start | bytes 1572872 | tf_op jit(solution)/shard_map/ppermute | solution.py:227
  3.0 2.0 %collective-permute-start = (bf16[8,1024]{1,0:T(8,128)(2,1)}, bf16[8,1024]{1,0:T(8,128)(2,1)S(1)}, u32[]{:S(2)}, u32[]{:S(2)}) collective-permute-start(bf16[8,1024]{1,0:T(8,128)(2,1)} %refs_0_.1), channel_id=1, source_target_pairs={{0,1},{1,0},{2,3},{3,2},{4,5},{5,4},{6,7},{7,6},{8,9},{9,8},{10,11... | collective-permute-start | bytes 49160 | tf_op jit(solution)/shard_map/ppermute | solution.py:227
  3.0 2.0 %collective-permute-start.1 = (bf16[8,1024]{1,0:T(8,128)(2,1)}, bf16[8,1024]{1,0:T(8,128)(2,1)S(1)}, u32[]{:S(2)}, u32[]{:S(2)}) collective-permute-start(bf16[8,1024]{1,0:T(8,128)(2,1)} %refs_1_.1), channel_id=1, source_target_pairs={{0,1},{1,0},{2,3},{3,2},{4,5},{5,4},{6,7},{7,6},{8,9},{9,8},{10,11... | collective-permute-start | bytes 49160 | tf_op jit(solution)/shard_map/ppermute | solution.py:227
  5.1 11.9 %collective-permute-start.3 = (bf16[80,1024]{1,0:T(8,128)(2,1)S(1)}, bf16[80,1024]{1,0:T(8,128)(2,1)S(1)}, u32[]{:S(2)}, u32[]{:S(2)}) collective-permute-start(bf16[80,1024]{1,0:T(8,128)(2,1)S(1)} %get-tuple-element.27.refs_0_), channel_id=1, source_target_pairs={{0,8},{1,9},{2,10},{3,11},{4,12},{5,13},{6,14},{7,15},{8,0},{9,1},... | collective-permute-start | bytes 491528 | tf_op jit(solution)/shard_map/ppermute | solution.py:227
  7.7 8.8 %collective-permute-start.2 = (bf16[32,1024]{1,0:T(8,128)(2,1)S(1)}, bf16[32,1024]{1,0:T(8,128)(2,1)S(1)}, u32[]{:S(2)}, u32[]{:S(2)}) collective-permute-start(bf16[32,1024]{1,0:T(8,128)(2,1)S(1)} %get-tuple-element.28), channel_id=1, source_target_pairs={{0,4},{1,5},{2,6},{3,7},{4,0},{5,1},{6,2},{7,3},{8,12},{9,13},{10,... | collective-permute-start | bytes 196616 | tf_op jit(solution)/shard_map/ppermute | solution.py:227
  9.3 7.2 %collective-permute-start.8 = (bf16[16,1024]{1,0:T(8,128)(2,1)S(1)}, bf16[16,1024]{1,0:T(8,128)(2,1)S(1)}, u32[]{:S(2)}, u32[]{:S(2)}) collective-permute-start(bf16[16,1024]{1,0:T(8,128)(2,1)S(1)} %get-tuple-element.35.refs_0_), channel_id=1, source_target_pairs={{0,2},{1,3},{2,0},{3,1},{4,6},{5,7},{6,4},{7,5},{8,10},{9,11},{10,... | collective-permute-start | bytes 98312 | tf_op jit(solution)/shard_map/ppermute | solution.py:227
  9.8 6.7 %collective-permute-start.9 = (bf16[16,1024]{1,0:T(8,128)(2,1)S(1)}, bf16[16,1024]{1,0:T(8,128)(2,1)S(1)}, u32[]{:S(2)}, u32[]{:S(2)}) collective-permute-start(bf16[16,1024]{1,0:T(8,128)(2,1)S(1)} %get-tuple-element.35.refs_0_), channel_id=1, source_target_pairs={{0,6},{1,7},{2,4},{3,5},{4,2},{5,3},{6,0},{7,1},{8,14},{9,15},{10,... | collective-permute-start | bytes 98312 | tf_op jit(solution)/shard_map/ppermute | solution.py:227
  17.0 8.5 %copy-start.1 = (bf16[256,1024]{1,0:T(8,128)(2,1)S(1)}, bf16[256,1024]{1,0:T(8,128)(2,1)}, u32[]{:S(2)}) copy-start(bf16[256,1024]{1,0:T(8,128)(2,1)} %layer_ref.3) | copy-start | bytes 1572868
  17.4 11.1 %collective-permute-start.11 = (bf16[192,256]{1,0:T(8,128)(2,1)S(1)}, bf16[192,256]{1,0:T(8,128)(2,1)S(1)}, u32[]{:S(2)}, u32[]{:S(2)}) collective-permute-start(bf16[192,256]{1,0:T(8,128)(2,1)S(1)} %get-tuple-element.37), channel_id=1, source_target_pairs={{0,4},{1,5},{2,6},{3,7},{4,0},{5,1},{6,2},{7,3},{8,12},{9,13},{10,... | collective-permute-start | bytes 294920 | tf_op jit(solution)/shard_map/ppermute | solution.py:227
  19.3 5.7 %collective-permute-start.4 = (bf16[16,1024]{1,0:T(8,128)(2,1)S(1)}, bf16[16,1024]{1,0:T(8,128)(2,1)S(1)}, u32[]{:S(2)}, u32[]{:S(2)}) collective-permute-start(bf16[16,1024]{1,0:T(8,128)(2,1)S(1)} %slice.3), channel_id=1, source_target_pairs={{0,12},{1,13},{2,14},{3,15},{4,8},{5,9},{6,10},{7,11},{8,4},{9,5},... | collective-permute-start | bytes 98312 | tf_op jit(solution)/shard_map/ppermute | solution.py:227
  26.0 8.8 %collective-permute-start.5 = (bf16[256,256]{1,0:T(8,128)(2,1)S(1)}, bf16[256,256]{1,0:T(8,128)(2,1)S(1)}, u32[]{:S(2)}, u32[]{:S(2)}) collective-permute-start(bf16[256,256]{1,0:T(8,128)(2,1)S(1)} %get-tuple-element.30), channel_id=1, source_target_pairs={{0,1},{1,0},{2,3},{3,2},{4,5},{5,4},{6,7},{7,6},{8,9},{9,8},{10,11... | collective-permute-start | bytes 393224 | tf_op jit(solution)/shard_map/ppermute | solution.py:227
  26.5 8.3 %collective-permute-start.7 = (bf16[256,256]{1,0:T(8,128)(2,1)S(1)}, bf16[256,256]{1,0:T(8,128)(2,1)S(1)}, u32[]{:S(2)}, u32[]{:S(2)}) collective-permute-start(bf16[256,256]{1,0:T(8,128)(2,1)S(1)} %get-tuple-element.32), channel_id=1, source_target_pairs={{0,1},{1,0},{2,3},{3,2},{4,5},{5,4},{6,7},{7,6},{8,9},{9,8},{10,11... | collective-permute-start | bytes 393224 | tf_op jit(solution)/shard_map/ppermute | solution.py:227
  27.0 3.9 %collective-permute-start.10 = (bf16[64,256]{1,0:T(8,128)(2,1)S(1)}, bf16[64,256]{1,0:T(8,128)(2,1)S(1)}, u32[]{:S(2)}, u32[]{:S(2)}) collective-permute-start(bf16[64,256]{1,0:T(8,128)(2,1)S(1)} %get-tuple-element.36.refs_5_), channel_id=1, source_target_pairs={{0,2},{1,3},{2,0},{3,1},{4,6},{5,7},{6,4},{7,5},{8,10},{9,11},{10,... | collective-permute-start | bytes 98312 | tf_op jit(solution)/shard_map/ppermute | solution.py:227
  28.5 6.2 %collective-permute-start.15 = (bf16[192,256]{1,0:T(8,128)(2,1)S(1)}, bf16[192,256]{1,0:T(8,128)(2,1)S(1)}, u32[]{:S(2)}, u32[]{:S(2)}) collective-permute-start(bf16[192,256]{1,0:T(8,128)(2,1)S(1)} %collective-permute-done.11.refs_7_), channel_id=1, source_target_pairs={{0,1},{1,0},{2,3},{3,2},{4,5},{5,4},{6,7},{7,6},{8,9},{9,8},{10,11... | collective-permute-start | bytes 294920 | tf_op jit(solution)/shard_map/ppermute | solution.py:227
  28.5 4.8 %collective-permute-start.12 = (bf16[64,256]{1,0:T(8,128)(2,1)S(1)}, bf16[64,256]{1,0:T(8,128)(2,1)S(1)}, u32[]{:S(2)}, u32[]{:S(2)}) collective-permute-start(bf16[64,256]{1,0:T(8,128)(2,1)S(1)} %get-tuple-element.38), channel_id=1, source_target_pairs={{0,6},{1,7},{2,4},{3,5},{4,2},{5,3},{6,0},{7,1},{8,14},{9,15},{10,... | collective-permute-start | bytes 98312 | tf_op jit(solution)/shard_map/ppermute | solution.py:227
  31.0 2.4 %collective-permute-start.13 = (bf16[64,256]{1,0:T(8,128)(2,1)S(1)}, bf16[64,256]{1,0:T(8,128)(2,1)S(1)}, u32[]{:S(2)}, u32[]{:S(2)}) collective-permute-start(bf16[64,256]{1,0:T(8,128)(2,1)S(1)} %get-tuple-element.36.refs_5_), channel_id=1, source_target_pairs={{0,1},{1,0},{2,3},{3,2},{4,5},{5,4},{6,7},{7,6},{8,9},{9,8},{10,11... | collective-permute-start | bytes 98312 | tf_op jit(solution)/shard_map/ppermute | solution.py:227
  33.4 1.2 %collective-permute-start.14 = (bf16[64,256]{1,0:T(8,128)(2,1)S(1)}, bf16[64,256]{1,0:T(8,128)(2,1)S(1)}, u32[]{:S(2)}, u32[]{:S(2)}) collective-permute-start(bf16[64,256]{1,0:T(8,128)(2,1)S(1)} %collective-permute-done.10.refs_6_), channel_id=1, source_target_pairs={{0,1},{1,0},{2,3},{3,2},{4,5},{5,4},{6,7},{7,6},{8,9},{9,8},{10,11... | collective-permute-start | bytes 98312 | tf_op jit(solution)/shard_map/ppermute | solution.py:227
  33.4 1.4 %collective-permute-start.16 = (bf16[64,256]{1,0:T(8,128)(2,1)S(1)}, bf16[64,256]{1,0:T(8,128)(2,1)S(1)}, u32[]{:S(2)}, u32[]{:S(2)}) collective-permute-start(bf16[64,256]{1,0:T(8,128)(2,1)S(1)} %collective-permute-done.12.refs_8_), channel_id=1, source_target_pairs={{0,1},{1,0},{2,3},{3,2},{4,5},{5,4},{6,7},{7,6},{8,9},{9,8},{10,11... | collective-permute-start | bytes 98312 | tf_op jit(solution)/shard_map/ppermute | solution.py:227

commit v3 on v2

--- a/solution.py
+++ b/solution.py
@@ -51,7 +51,9 @@
 
 
 def call(kernel, outs, *operands, in_space=pltpu.VMEM, scratch=(), out_space=pltpu.VMEM):
-    shapes = [jax.ShapeDtypeStruct(shape, jnp.bfloat16) for shape in outs]
+    shapes = [
+        jax.ShapeDtypeStruct(out, jnp.bfloat16) if isinstance(out, tuple) else out for out in outs
+    ]
     spaces = [in_space] * len(operands)
     if in_space == pltpu.HBM:
         operands = [pltpu.with_memory_space_constraint(x, in_space) for x in operands]
@@ -69,61 +71,75 @@
     return lax.axis_index("half") * lax.axis_size("tile") + lax.axis_index("tile")
 
 
-def stage_kernel(*refs):
-    sources, (outs, held, sems) = refs[:7], (refs[7:14], refs[14:18], refs[18])
-    share = outs[2].shape[0]
+def stage_kernel(
+    prefix_ref, left_ref, layer_ref, side_ref, branch_ref, left_map_ref, right_map_ref,
+    own_ref, far_ref, codes_ref, side, branch, left_map, right_map, sems,
+):
+    depth = prefix_ref.shape[0]
+    share = far_ref.shape[0] - depth
     start = pl.multiple_of(spot_of() * share, share)
-    copies = []
-    for k, source in enumerate(sources):
-        if k == 2:
-            source = source.at[pl.ds(start, share), :]
-        target = outs[k] if k < 3 else held[k - 3]
-        copies.append(pltpu.make_async_copy(source, target, sems.at[k]))
-        copies[-1].start()
-    for copy in copies[3:]:
+    copies = [
+        pltpu.make_async_copy(source, target, sems.at[k])
+        for k, (source, target) in enumerate(
+            (
+                (side_ref, side), (branch_ref, branch),
+                (left_map_ref, left_map), (right_map_ref, right_map),
+                (layer_ref.at[pl.ds(start, share), :], far_ref.at[pl.ds(0, share), :]),
+                (left_ref, far_ref.at[pl.ds(share, depth), :]),
+                (prefix_ref, own_ref),
+            )
+        )
+    ]
+    for copy in copies:
+        copy.start()
+    for copy in copies[:4]:
         copy.wait()
-    side_ref, branch_ref, left_map_ref, right_map_ref = held
-    out_refs = outs[3:]
-    cuts, paths = branch_ref.shape
-    tiles = lax.axis_size("half") * lax.axis_size("tile")
-    for on_left, map_ref, shard, shards, (factor_ref, pick_ref) in (
-        (True, left_map_ref, lax.axis_index("path"), lax.axis_size("path"), out_refs[:2]),
-        (False, right_map_ref, spot_of(), tiles, out_refs[2:]),
+    cuts, paths = branch.shape
+    for half, (map_ref, shard) in enumerate(
+        ((left_map, lax.axis_index("path")), (right_map, spot_of()))
     ):
         wanted = jnp.zeros((1, paths), jnp.int32)
         phased = jnp.zeros((1, paths), jnp.int32)
         mask = jnp.int32(0)
         for cut in range(cuts):
-            projector = side_ref[cut] if on_left else 1 - side_ref[cut]
-            bits = branch_ref[pl.ds(cut, 1), :]
+            projector = 1 - side[cut] if half else side[cut]
+            bits = branch[pl.ds(cut, 1), :]
             wanted += bits * (projector << cut)
             phased += bits * ((1 - projector) << cut)
             mask += projector << cut
+        row = map_ref[...]
+        place = (lax.div(row, depth) ^ shard) * depth + lax.rem(row, depth)
+        for k, code in enumerate((wanted, phased, place, jnp.full((1, paths), mask))):
+            codes_ref[pl.ds(4 * half + k, 1), :] = code
+    for copy in copies[4:]:
+        copy.wait()
+
+
+def mask_kernel(codes_ref, *out_refs):
+    for half in range(2):
+        factor_ref, pick_ref = out_refs[2 * half:][:2]
+        wanted, phased, place, mask = (codes_ref[pl.ds(4 * half + k, 1), :] for k in range(4))
         gate = lax.broadcasted_iota(jnp.int32, factor_ref.shape, 0)
         hit = (gate & mask) == wanted
         odd = (lax.population_count(gate & phased) & 1) == 1
         factor = jnp.where(hit, jnp.where(odd, -1.0, 1.0), 0.0)
         factor_ref[...] = factor.astype(jnp.bfloat16)
-        rows = pick_ref.shape[0]
-        depth = rows // shards
-        row = map_ref[...]
-        place = (lax.div(row, depth) ^ shard) * depth + lax.rem(row, depth)
         index = lax.broadcasted_iota(jnp.int32, pick_ref.shape, 0)
         pick_ref[...] = jnp.where(index == place, 1.0, 0.0).astype(jnp.bfloat16)
-    for copy in copies[:3]:
-        copy.wait()
-
-
-def pack_kernel(right_ref, right_t_ref, left_ref, left_t_ref, rows_ref, pair_ref, near_ref, far_ref):
-    depth = right_ref.shape[0]
-    pair = jnp.concatenate([right_ref[...], right_t_ref[...]], axis=0)
-    left = jnp.concatenate([left_ref[...], left_t_ref[...]], axis=0)
+
+
+def pack_kernel(own_ref, own_t_ref, far_ref, pair_ref, near_ref):
+    depth = own_ref.shape[0]
+    pair = jnp.concatenate([own_ref[...], own_t_ref[...]], axis=0)
     pair_ref[...] = pair
     near_ref[pl.ds(0, 2 * depth), :] = pair
-    near_ref[pl.ds(2 * depth, 2 * depth), :] = left
-    share = rows_ref.shape[0]
-    far_ref[pl.ds(0, share), :] = rows_ref[...]
-    far_ref[pl.ds(share, 2 * depth), :] = left
+    near_ref[pl.ds(2 * depth, depth), :] = far_ref[pl.ds(far_ref.shape[0] - depth, depth), :]
+
+
+def left_pack_kernel(own_ref, near_ref, far_ref, cross_ref, out_ref):
+    depth = cross_ref.shape[0]
+    for k, ref in enumerate((own_ref, near_ref, far_ref, cross_ref)):
+        out_ref[pl.ds(k * depth, depth), :] = ref[pl.ds(ref.shape[0] - depth, depth), :]
 
 
 def project_kernel(pieces, factor_ref, pick_ref, *refs):
@@ -232,16 +248,10 @@
     spots = sizes[1] * sizes[2]
     share = chunk // spots
 
-    right_t = exchange(right_prefix, tile=1)
-    left_t = exchange(left_prefix, tile=1)
     bits = branch_bits.T
-    prefix_rows = [(sizes[0] * depth, paths), (spots * depth, paths)]
-    right_own, left_own, near_rows, left_factor, left_pick, right_factor, right_pick = call(
+    own, far_pack, codes = call(
         stage_kernel,
-        [
-            (depth, gates), (depth, gates), (share, gates),
-            (gates, paths), prefix_rows[0], (gates, paths), prefix_rows[1],
-        ],
+        [(depth, gates), (share + depth, gates), jax.ShapeDtypeStruct((8, paths), jnp.int32)],
         right_prefix, left_prefix, right_layer,
         cut_side, bits, left_map[None, :], right_map[None, :],
         in_space=pltpu.HBM,
@@ -253,27 +263,34 @@
             pltpu.SemaphoreType.DMA((7,)),
         ),
     )
-    pair, near_pack, far_pack = call(
-        pack_kernel,
-        [(2 * depth, gates), (4 * depth, gates), (share + 2 * depth, gates)],
-        right_own, right_t, left_own, left_t, near_rows,
-    )
-    pair_x = exchange(pair, half=1)
+    far = exchange(far_pack, plane=2)
+    prefix_x = exchange(right_prefix, half=1)
     layer_x = exchange(left_layer, half=1)
-    far = exchange(far_pack, plane=2)
+    own_t = exchange(own, tile=1)
+    left_factor, left_pick, right_factor, right_pick = call(
+        mask_kernel,
+        [(gates, paths), (sizes[0] * depth, paths), (gates, paths), (spots * depth, paths)],
+        codes,
+    )
+    pair, near_pack = call(
+        pack_kernel, [(2 * depth, gates), (3 * depth, gates)], own, own_t, far_pack
+    )
+    near = exchange(near_pack, plane=1)
     pair_xz = exchange(pair, plane=1, half=1)
-    near = exchange(near_pack, plane=1)
-    left_far = exchange(far_pack[share:], plane=3)
+    left_cross = exchange(left_prefix, plane=3)
+    prefix_xt = exchange(prefix_x, tile=1)
 
     (right_projected,) = call(
         functools.partial(
             project_kernel,
-            (((0, 0, 2 * depth), (1, 0, 2 * depth)), ((2, 0, 2 * depth), (3, 0, 2 * depth))),
+            (
+                ((0, 0, 2 * depth), (1, 0, depth), (2, 0, depth)),
+                ((3, 0, 2 * depth), (4, 0, 2 * depth)),
+            ),
         ),
         [(gates, 2 * paths)],
-        right_factor, right_pick, pair, pair_x, near, pair_xz,
-    )
-    (right_near,) = call(right_own_kernel, [(chunk, paths)], right_layer, right_projected)
+        right_factor, right_pick, pair, prefix_x, prefix_xt, near, pair_xz,
+    )
     mine, for_near, cross = call(
         right_far_kernel,
         [(share, paths), (chunk // sizes[2] + share, paths), (share, paths)],
@@ -283,22 +300,18 @@
         mine, exchange(mine, half=1), exchange(for_near, plane=1), exchange(cross, plane=1, half=1)
     ]
     right_pieces = right_pieces + [exchange(piece, tile=1) for piece in right_pieces]
-
+    (right_near,) = call(right_own_kernel, [(chunk, paths)], right_layer, right_projected)
+
+    (left_rows,) = call(
+        left_pack_kernel, [(sizes[0] * depth, gates)], far_pack, near, far, left_cross
+    )
+    left_rows_t = exchange(left_rows, tile=1)
     (left_projected,) = call(
         functools.partial(
-            project_kernel,
-            tuple(
-                (
-                    (0, share + k * depth, depth),
-                    (1, (2 + k) * depth, depth),
-                    (2, share + k * depth, depth),
-                    (3, k * depth, depth),
-                )
-                for k in range(2)
-            ),
+            project_kernel, tuple(((k, 0, sizes[0] * depth),) for k in range(2))
         ),
         [(gates, 2 * paths)],
-        left_factor, left_pick, far_pack, near, far, left_far,
+        left_factor, left_pick, left_rows, left_rows_t,
     )
     rows = left_layer.shape[0]
     own_mine, own_other = call(left_kernel, [(rows, paths)] * 2, left_layer, left_projected)

time: 36.6 us -> 35 us (0.956)
  starting transfers between devices: 16.6 us -> 12 us
  waiting for transfers between devices: 13.9 us -> 16.6 us
    ppermute x17 -> x18, starting transfers between devices: 16.6 us -> 12 us  [exchange(): return lax.ppermute(value, DEVICE_AXES, pairs)]
    ppermute x17 -> x18, waiting for transfers between devices: 13.9 us -> 16.6 us  [exchange(): return lax.ppermute(value, DEVICE_AXES, pairs)]
    pallas_call x9 -> x11, Pallas kernels: 5.77 us -> 5.91 us  [call(): pl.pallas_call(kernel, out_shape=shapes, in_specs=[pl.BlockSpec(memory_sp...]
  transfers between devices with their start and end apart: 17 -> 18, of which waited for: 6 -> 8; matrix products, arithmetic and copies ran while one was open for 0% -> 0% of each run, Pallas kernels for 11% -> 12%
where the time goes in v3:
time: 35 us; the launch traced here: 34.8 us
  waiting for transfers between devices  16.6 us (47%)
  starting transfers between devices  12 us (34%)
  Pallas kernels  5.91 us (17%)
    ppermute x18, waiting for transfers between devices, exchange(): return lax.ppermute(value, DEVICE_AXES, pairs)  16.6 us
    ppermute x18, starting transfers between devices, exchange(): return lax.ppermute(value, DEVICE_AXES, pairs)  12 us
    pallas_call x11, Pallas kernels, call(): pl.pallas_call(kernel, out_shape=shapes, in_specs=[pl.BlockSpec(memory_sp...  5.91 us
  transfers between devices with their start and end apart: 18, of which 8 were waited for; matrix products, arithmetic and copies ran while one was open for 0% of the time, Pallas kernels for 12%

profile of v3, /device:TPU:0, one launch (start us, length us, event | category | flops | bytes accessed | tf_op | source)
XLA Modules:
  0.0 34.8 jit_solution(12712592228500808849)
XLA Ops:
  0.0 3.0 %collective-permute-start.6 = (bf16[256,1024]{1,0:T(8,128)(2,1)}, bf16[256,1024]{1,0:T(8,128)(2,1)S(1)}, u32[]{:S(2)}, u32[]{:S(2)}) collective-permute-start(bf16[256,1024]{1,0:T(8,128)(2,1)} %layer_ref.5), channel_id=1, source_target_pairs={{0,2},{1,3},{2,0},{3,1},{4,6},{5,7},{6,4},{7,5},{8,10},{9,11},{10,... | collective-permute-start | bytes 1572872 | tf_op jit(solution)/shard_map/ppermute | solution.py:243
  3.0 1.0 %shard_map.82 = (bf16[8,1024]{1,0:T(8,128)(2,1)S(1)}, bf16[72,1024]{1,0:T(8,128)(2,1)S(1)}, s32[8,256]{1,0:T(8,128)S(1)}) custom-call(bf16[8,1024]{1,0:T(8,128)(2,1)} %prefix_ref.1, bf16[8,1024]{1,0:T(8,128)(2,1)} %left_ref.1, bf16[256,1024]{1,0:T(8,128)(2,1)} %layer_ref.7, s32[10]{0:T(128)} %side_ref.1, s32[10,256]{1,0:T(8,128)} %bitcast.3, ...), custom_call_target="tpu_custom_call" | custom-call | tf_op jit(solution)/shard_map/pallas_call | solution.py:60
  4.0 2.7 %collective-permute-start.2 = (bf16[72,1024]{1,0:T(8,128)(2,1)S(1)}, bf16[72,1024]{1,0:T(8,128)(2,1)S(1)}, u32[]{:S(2)}, u32[]{:S(2)}) collective-permute-start(bf16[72,1024]{1,0:T(8,128)(2,1)S(1)} %get-tuple-element.24.far_ref.own_ref), channel_id=1, source_target_pairs={{0,8},{1,9},{2,10},{3,11},{4,12},{5,13},{6,14},{7,15},{8,0},{9,1},... | collective-permute-start | bytes 442376 | tf_op jit(solution)/shard_map/ppermute | solution.py:243
  6.7 1.2 %collective-permute-done.own_t_ref = bf16[8,1024]{1,0:T(8,128)(2,1)S(1)} collective-permute-done((bf16[8,1024]{1,0:T(8,128)(2,1)S(1)}, bf16[8,1024]{1,0:T(8,128)(2,1)S(1)}, u32[]{:S(2)}, u32[]{:S(2)}) %collective-permute-start) | collective-permute-done | bytes 16416 | tf_op jit(solution)/shard_map/ppermute | solution.py:243
  7.8 1.6 %collective-permute-start.1 = (bf16[24,1024]{1,0:T(8,128)(2,1)S(1)}, bf16[24,1024]{1,0:T(8,128)(2,1)S(1)}, u32[]{:S(2)}, u32[]{:S(2)}) collective-permute-start(bf16[24,1024]{1,0:T(8,128)(2,1)S(1)} %get-tuple-element.26), channel_id=1, source_target_pairs={{0,4},{1,5},{2,6},{3,7},{4,0},{5,1},{6,2},{7,3},{8,12},{9,13},{10,... | collective-permute-start | bytes 147464 | tf_op jit(solution)/shard_map/ppermute | solution.py:243
  9.7 0.3 collective-permute-start.8
  10.0 5.2 %collective-permute-done.3.cross_ref = bf16[8,1024]{1,0:T(8,128)(2,1)S(1)} collective-permute-done((bf16[8,1024]{1,0:T(8,128)(2,1)}, bf16[8,1024]{1,0:T(8,128)(2,1)S(1)}, u32[]{:S(2)}, u32[]{:S(2)}) %collective-permute-start.3) | collective-permute-done | bytes 16416 | tf_op jit(solution)/shard_map/ppermute | solution.py:243
  15.5 0.6 %shard_map.83 = (bf16[1024,256]{1,0:T(8,128)(2,1)S(1)}, bf16[32,256]{1,0:T(8,128)(2,1)S(1)}, bf16[1024,256]{1,0:T(8,128)(2,1)S(1)}, bf16[32,256]{1,0:T(8,128)(2,1)S(1)}) custom-call(s32[8,256]{1,0:T(8,128)S(1)} %get-tuple-element.21.codes_ref), custom_call_target="tpu_custom_call" | custom-call | tf_op jit(solution)/shard_map/pallas_call | solution.py:60
  16.1 0.6 %collective-permute-start.4 = (bf16[32,1024]{1,0:T(8,128)(2,1)S(1)}, bf16[32,1024]{1,0:T(8,128)(2,1)S(1)}, u32[]{:S(2)}, u32[]{:S(2)}) collective-permute-start(bf16[32,1024]{1,0:T(8,128)(2,1)S(1)} %shard_map.85.refs_0_), channel_id=1, source_target_pairs={{0,1},{1,0},{2,3},{3,2},{4,5},{5,4},{6,7},{7,6},{8,9},{9,8},{10,11... | collective-permute-start | bytes 196616 | tf_op jit(solution)/shard_map/ppermute | solution.py:243
  16.7 3.3 %collective-permute-done.10.refs_4_ = bf16[16,1024]{1,0:T(8,128)(2,1)S(1)} collective-permute-done((bf16[16,1024]{1,0:T(8,128)(2,1)S(1)}, bf16[16,1024]{1,0:T(8,128)(2,1)S(1)}, u32[]{:S(2)}, u32[]{:S(2)}) %collective-permute-start.10) | collective-permute-done | bytes 32800 | tf_op jit(solution)/shard_map/ppermute | solution.py:243
  20.1 0.5 %shard_map.89.projected_ref = bf16[1024,512]{1,0:T(8,128)(2,1)S(1)} custom-call(bf16[1024,256]{1,0:T(8,128)(2,1)S(1)} %get-tuple-element.31.factor_ref, bf16[32,256]{1,0:T(8,128)(2,1)S(1)} %get-tuple-element.32.pick_ref, bf16[16,1024]{1,0:T(8,128)(2,1)S(1)} %get-tuple-element.33.refs_0_, bf16[8,1024]{1,0:T(8,128)(2,1)S(1)} %collective-permute-done.8.refs_1_, ...), custom_call_target="tpu_custom_call" | custom-call | tf_op jit(solution)/shard_map/pallas_call | solution.py:60
  20.6 0.4 %shard_map.91 = (bf16[64,256]{1,0:T(8,128)(2,1)S(1)}, bf16[192,256]{1,0:T(8,128)(2,1)S(1)}, bf16[64,256]{1,0:T(8,128)(2,1)S(1)}) custom-call(bf16[256,1024]{1,0:T(8,128)(2,1)S(1)} %copy-done, bf16[72,1024]{1,0:T(8,128)(2,1)S(1)} %collective-permute-done.2.far_ref, bf16[1024,512]{1,0:T(8,128)(2,1)S(1)} %shard_map.89.projected_ref), custom_call_target="tpu_custom_call" | custom-call | tf_op jit(solution)/shard_map/pallas_call | solution.py:60
  21.0 0.5 %shard_map.86.projected_ref = bf16[1024,512]{1,0:T(8,128)(2,1)S(1)} custom-call(bf16[1024,256]{1,0:T(8,128)(2,1)S(1)} %get-tuple-element.22.factor_ref, bf16[32,256]{1,0:T(8,128)(2,1)S(1)} %get-tuple-element.23.pick_ref, bf16[32,1024]{1,0:T(8,128)(2,1)S(1)} %shard_map.85.refs_0_, bf16[32,1024]{1,0:T(8,128)(2,1)S(1)} %collective-permute-done.4.refs_1_), custom_call_target="tpu_custom_call" | custom-call | tf_op jit(solution)/shard_map/pallas_call | solution.py:60
  21.6 0.4 %shard_map.87 = (bf16[256,256]{1,0:T(8,128)(2,1)S(1)}, bf16[256,256]{1,0:T(8,128)(2,1)S(1)}) custom-call(bf16[256,1024]{1,0:T(8,128)(2,1)S(1)} %copy-done.1, bf16[1024,512]{1,0:T(8,128)(2,1)S(1)} %shard_map.86.projected_ref), custom_call_target="tpu_custom_call" | custom-call | tf_op jit(solution)/shard_map/pallas_call | solution.py:60
  22.1 0.4 %shard_map.88 = (bf16[256,256]{1,0:T(8,128)(2,1)S(1)}, bf16[256,256]{1,0:T(8,128)(2,1)S(1)}) custom-call(bf16[256,1024]{1,0:T(8,128)(2,1)S(1)} %collective-permute-done.6.layer_ref, bf16[1024,512]{1,0:T(8,128)(2,1)S(1)} %shard_map.86.projected_ref), custom_call_target="tpu_custom_call" | custom-call | tf_op jit(solution)/shard_map/pallas_call | solution.py:60
  22.6 0.6 %collective-permute-start.7 = (bf16[256,256]{1,0:T(8,128)(2,1)S(1)}, bf16[256,256]{1,0:T(8,128)(2,1)S(1)}, u32[]{:S(2)}, u32[]{:S(2)}) collective-permute-start(bf16[256,256]{1,0:T(8,128)(2,1)S(1)} %get-tuple-element.30), channel_id=1, source_target_pairs={{0,1},{1,0},{2,3},{3,2},{4,5},{5,4},{6,7},{7,6},{8,9},{9,8},{10,11... | collective-permute-start | bytes 393224 | tf_op jit(solution)/shard_map/ppermute | solution.py:243
  23.1 1.9 %collective-permute-start.13 = (bf16[64,256]{1,0:T(8,128)(2,1)S(1)}, bf16[64,256]{1,0:T(8,128)(2,1)S(1)}, u32[]{:S(2)}, u32[]{:S(2)}) collective-permute-start(bf16[64,256]{1,0:T(8,128)(2,1)S(1)} %get-tuple-element.36), channel_id=1, source_target_pairs={{0,6},{1,7},{2,4},{3,5},{4,2},{5,3},{6,0},{7,1},{8,14},{9,15},{10,... | collective-permute-start | bytes 98312 | tf_op jit(solution)/shard_map/ppermute | solution.py:243
  25.0 0.6 %collective-permute-done.12.refs_7_ = bf16[192,256]{1,0:T(8,128)(2,1)S(1)} collective-permute-done((bf16[192,256]{1,0:T(8,128)(2,1)S(1)}, bf16[192,256]{1,0:T(8,128)(2,1)S(1)}, u32[]{:S(2)}, u32[]{:S(2)}) %collective-permute-start.12) | collective-permute-done | bytes 98336 | tf_op jit(solution)/shard_map/ppermute | solution.py:243
  25.6 0.5 %collective-permute-start.14 = (bf16[64,256]{1,0:T(8,128)(2,1)S(1)}, bf16[64,256]{1,0:T(8,128)(2,1)S(1)}, u32[]{:S(2)}, u32[]{:S(2)}) collective-permute-start(bf16[64,256]{1,0:T(8,128)(2,1)S(1)} %get-tuple-element.34.refs_5_), channel_id=1, source_target_pairs={{0,1},{1,0},{2,3},{3,2},{4,5},{5,4},{6,7},{7,6},{8,9},{9,8},{10,11... | collective-permute-start | bytes 98312 | tf_op jit(solution)/shard_map/ppermute | solution.py:243
  26.1 1.8 %collective-permute-done.13.refs_8_ = bf16[64,256]{1,0:T(8,128)(2,1)S(1)} collective-permute-done((bf16[64,256]{1,0:T(8,128)(2,1)S(1)}, bf16[64,256]{1,0:T(8,128)(2,1)S(1)}, u32[]{:S(2)}, u32[]{:S(2)}) %collective-permute-start.13) | collective-permute-done | bytes 32800 | tf_op jit(solution)/shard_map/ppermute | solution.py:243
  27.9 0.5 %collective-permute-start.11 = (bf16[64,256]{1,0:T(8,128)(2,1)S(1)}, bf16[64,256]{1,0:T(8,128)(2,1)S(1)}, u32[]{:S(2)}, u32[]{:S(2)}) collective-permute-start(bf16[64,256]{1,0:T(8,128)(2,1)S(1)} %get-tuple-element.34.refs_5_), channel_id=1, source_target_pairs={{0,2},{1,3},{2,0},{3,1},{4,6},{5,7},{6,4},{7,5},{8,10},{9,11},{10,... | collective-permute-start | bytes 98312 | tf_op jit(solution)/shard_map/ppermute | solution.py:243
  28.5 3.4 %collective-permute-done.11.refs_6_ = bf16[64,256]{1,0:T(8,128)(2,1)S(1)} collective-permute-done((bf16[64,256]{1,0:T(8,128)(2,1)S(1)}, bf16[64,256]{1,0:T(8,128)(2,1)S(1)}, u32[]{:S(2)}, u32[]{:S(2)}) %collective-permute-start.11) | collective-permute-done | bytes 32800 | tf_op jit(solution)/shard_map/ppermute | solution.py:243
  32.2 0.9 %collective-permute-done.15.refs_10_ = bf16[64,256]{1,0:T(8,128)(2,1)S(1)} collective-permute-done((bf16[64,256]{1,0:T(8,128)(2,1)S(1)}, bf16[64,256]{1,0:T(8,128)(2,1)S(1)}, u32[]{:S(2)}, u32[]{:S(2)}) %collective-permute-start.15) | collective-permute-done | bytes 32800 | tf_op jit(solution)/shard_map/ppermute | solution.py:243
  33.1 1.7 %shard_map.92 = bf16[1024,1024]{1,0:T(8,128)(2,1)} custom-call(bf16[256,256]{1,0:T(8,128)(2,1)S(1)} %get-tuple-element.27.refs_0_, bf16[256,256]{1,0:T(8,128)(2,1)S(1)} %collective-permute-done.5.refs_1_, bf16[256,256]{1,0:T(8,128)(2,1)S(1)} %get-tuple-element.29.refs_2_, bf16[256,256]{1,0:T(8,128)(2,1)S(1)} %collective-permute-done.7.refs_3_, ...), custom_call_target="tpu_custom_call" | custom-call | tf_op jit(solution)/shard_map/pallas_call | solution.py:60
  (27 shorter events, 1.0 us)
Async XLA Ops:
  0.0 20.5 %copy-start = (bf16[256,1024]{1,0:T(8,128)(2,1)S(1)}, bf16[256,1024]{1,0:T(8,128)(2,1)}, u32[]{:S(2)}) copy-start(bf16[256,1024]{1,0:T(8,128)(2,1)} %layer_ref.7) | copy-start | bytes 1572868
  0.0 22.1 %collective-permute-start.6 = (bf16[256,1024]{1,0:T(8,128)(2,1)}, bf16[256,1024]{1,0:T(8,128)(2,1)S(1)}, u32[]{:S(2)}, u32[]{:S(2)}) collective-permute-start(bf16[256,1024]{1,0:T(8,128)(2,1)} %layer_ref.5), channel_id=1, source_target_pairs={{0,2},{1,3},{2,0},{3,1},{4,6},{5,7},{6,4},{7,5},{8,10},{9,11},{10,... | collective-permute-start | bytes 1572872 | tf_op jit(solution)/shard_map/ppermute | solution.py:243
  4.0 12.1 %collective-permute-start.2 = (bf16[72,1024]{1,0:T(8,128)(2,1)S(1)}, bf16[72,1024]{1,0:T(8,128)(2,1)S(1)}, u32[]{:S(2)}, u32[]{:S(2)}) collective-permute-start(bf16[72,1024]{1,0:T(8,128)(2,1)S(1)} %get-tuple-element.24.far_ref.own_ref), channel_id=1, source_target_pairs={{0,8},{1,9},{2,10},{3,11},{4,12},{5,13},{6,14},{7,15},{8,0},{9,1},... | collective-permute-start | bytes 442376 | tf_op jit(solution)/shard_map/ppermute | solution.py:243
  6.7 1.2 %collective-permute-start = (bf16[8,1024]{1,0:T(8,128)(2,1)S(1)}, bf16[8,1024]{1,0:T(8,128)(2,1)S(1)}, u32[]{:S(2)}, u32[]{:S(2)}) collective-permute-start(bf16[8,1024]{1,0:T(8,128)(2,1)S(1)} %get-tuple-element.25.own_ref), channel_id=1, source_target_pairs={{0,1},{1,0},{2,3},{3,2},{4,5},{5,4},{6,7},{7,6},{8,9},{9,8},{10,11... | collective-permute-start | bytes 49160 | tf_op jit(solution)/shard_map/ppermute | solution.py:243
  7.8 8.3 %collective-permute-start.1 = (bf16[24,1024]{1,0:T(8,128)(2,1)S(1)}, bf16[24,1024]{1,0:T(8,128)(2,1)S(1)}, u32[]{:S(2)}, u32[]{:S(2)}) collective-permute-start(bf16[24,1024]{1,0:T(8,128)(2,1)S(1)} %get-tuple-element.26), channel_id=1, source_target_pairs={{0,4},{1,5},{2,6},{3,7},{4,0},{5,1},{6,2},{7,3},{8,12},{9,13},{10,... | collective-permute-start | bytes 147464 | tf_op jit(solution)/shard_map/ppermute | solution.py:243
  9.5 5.7 %collective-permute-start.3 = (bf16[8,1024]{1,0:T(8,128)(2,1)}, bf16[8,1024]{1,0:T(8,128)(2,1)S(1)}, u32[]{:S(2)}, u32[]{:S(2)}) collective-permute-start(bf16[8,1024]{1,0:T(8,128)(2,1)} %left_ref.1), channel_id=1, source_target_pairs={{0,12},{1,13},{2,14},{3,15},{4,8},{5,9},{6,10},{7,11},{8,4},{9,5},... | collective-permute-start | bytes 49160 | tf_op jit(solution)/shard_map/ppermute | solution.py:243
  9.7 5.7 %collective-permute-start.8 = (bf16[8,1024]{1,0:T(8,128)(2,1)}, bf16[8,1024]{1,0:T(8,128)(2,1)S(1)}, u32[]{:S(2)}, u32[]{:S(2)}) collective-permute-start(bf16[8,1024]{1,0:T(8,128)(2,1)} %prefix_ref.1), channel_id=1, source_target_pairs={{0,2},{1,3},{2,0},{3,1},{4,6},{5,7},{6,4},{7,5},{8,10},{9,11},{10,... | collective-permute-start | bytes 49160 | tf_op jit(solution)/shard_map/ppermute | solution.py:243
  15.2 4.8 %collective-permute-start.10 = (bf16[16,1024]{1,0:T(8,128)(2,1)S(1)}, bf16[16,1024]{1,0:T(8,128)(2,1)S(1)}, u32[]{:S(2)}, u32[]{:S(2)}) collective-permute-start(bf16[16,1024]{1,0:T(8,128)(2,1)S(1)} %get-tuple-element.33.refs_0_), channel_id=1, source_target_pairs={{0,6},{1,7},{2,4},{3,5},{4,2},{5,3},{6,0},{7,1},{8,14},{9,15},{10,... | collective-permute-start | bytes 98312 | tf_op jit(solution)/shard_map/ppermute | solution.py:243
  15.5 1.3 %collective-permute-start.9 = (bf16[8,1024]{1,0:T(8,128)(2,1)S(1)}, bf16[8,1024]{1,0:T(8,128)(2,1)S(1)}, u32[]{:S(2)}, u32[]{:S(2)}) collective-permute-start(bf16[8,1024]{1,0:T(8,128)(2,1)S(1)} %collective-permute-done.8.refs_1_), channel_id=1, source_target_pairs={{0,1},{1,0},{2,3},{3,2},{4,5},{5,4},{6,7},{7,6},{8,9},{9,8},{10,11... | collective-permute-start | bytes 49160 | tf_op jit(solution)/shard_map/ppermute | solution.py:243
  16.1 4.9 %collective-permute-start.4 = (bf16[32,1024]{1,0:T(8,128)(2,1)S(1)}, bf16[32,1024]{1,0:T(8,128)(2,1)S(1)}, u32[]{:S(2)}, u32[]{:S(2)}) collective-permute-start(bf16[32,1024]{1,0:T(8,128)(2,1)S(1)} %shard_map.85.refs_0_), channel_id=1, source_target_pairs={{0,1},{1,0},{2,3},{3,2},{4,5},{5,4},{6,7},{7,6},{8,9},{9,8},{10,11... | collective-permute-start | bytes 196616 | tf_op jit(solution)/shard_map/ppermute | solution.py:243
  20.5 1.0 %copy-start.1 = (bf16[256,1024]{1,0:T(8,128)(2,1)S(1)}, bf16[256,1024]{1,0:T(8,128)(2,1)}, u32[]{:S(2)}) copy-start(bf16[256,1024]{1,0:T(8,128)(2,1)} %layer_ref.5) | copy-start | bytes 1572868
  21.0 4.7 %collective-permute-start.12 = (bf16[192,256]{1,0:T(8,128)(2,1)S(1)}, bf16[192,256]{1,0:T(8,128)(2,1)S(1)}, u32[]{:S(2)}, u32[]{:S(2)}) collective-permute-start(bf16[192,256]{1,0:T(8,128)(2,1)S(1)} %get-tuple-element.35), channel_id=1, source_target_pairs={{0,4},{1,5},{2,6},{3,7},{4,0},{5,1},{6,2},{7,3},{8,12},{9,13},{10,... | collective-permute-start | bytes 294920 | tf_op jit(solution)/shard_map/ppermute | solution.py:243
  22.0 11.0 %collective-permute-start.5 = (bf16[256,256]{1,0:T(8,128)(2,1)S(1)}, bf16[256,256]{1,0:T(8,128)(2,1)S(1)}, u32[]{:S(2)}, u32[]{:S(2)}) collective-permute-start(bf16[256,256]{1,0:T(8,128)(2,1)S(1)} %get-tuple-element.28), channel_id=1, source_target_pairs={{0,1},{1,0},{2,3},{3,2},{4,5},{5,4},{6,7},{7,6},{8,9},{9,8},{10,11... | collective-permute-start | bytes 393224 | tf_op jit(solution)/shard_map/ppermute | solution.py:243
  22.6 10.5 %collective-permute-start.7 = (bf16[256,256]{1,0:T(8,128)(2,1)S(1)}, bf16[256,256]{1,0:T(8,128)(2,1)S(1)}, u32[]{:S(2)}, u32[]{:S(2)}) collective-permute-start(bf16[256,256]{1,0:T(8,128)(2,1)S(1)} %get-tuple-element.30), channel_id=1, source_target_pairs={{0,1},{1,0},{2,3},{3,2},{4,5},{5,4},{6,7},{7,6},{8,9},{9,8},{10,11... | collective-permute-start | bytes 393224 | tf_op jit(solution)/shard_map/ppermute | solution.py:243
  23.1 4.8 %collective-permute-start.13 = (bf16[64,256]{1,0:T(8,128)(2,1)S(1)}, bf16[64,256]{1,0:T(8,128)(2,1)S(1)}, u32[]{:S(2)}, u32[]{:S(2)}) collective-permute-start(bf16[64,256]{1,0:T(8,128)(2,1)S(1)} %get-tuple-element.36), channel_id=1, source_target_pairs={{0,6},{1,7},{2,4},{3,5},{4,2},{5,3},{6,0},{7,1},{8,14},{9,15},{10,... | collective-permute-start | bytes 98312 | tf_op jit(solution)/shard_map/ppermute | solution.py:243
  25.6 7.4 %collective-permute-start.16 = (bf16[192,256]{1,0:T(8,128)(2,1)S(1)}, bf16[192,256]{1,0:T(8,128)(2,1)S(1)}, u32[]{:S(2)}, u32[]{:S(2)}) collective-permute-start(bf16[192,256]{1,0:T(8,128)(2,1)S(1)} %collective-permute-done.12.refs_7_), channel_id=1, source_target_pairs={{0,1},{1,0},{2,3},{3,2},{4,5},{5,4},{6,7},{7,6},{8,9},{9,8},{10,11... | collective-permute-start | bytes 294920 | tf_op jit(solution)/shard_map/ppermute | solution.py:243
  25.6 2.8 %collective-permute-start.14 = (bf16[64,256]{1,0:T(8,128)(2,1)S(1)}, bf16[64,256]{1,0:T(8,128)(2,1)S(1)}, u32[]{:S(2)}, u32[]{:S(2)}) collective-permute-start(bf16[64,256]{1,0:T(8,128)(2,1)S(1)} %get-tuple-element.34.refs_5_), channel_id=1, source_target_pairs={{0,1},{1,0},{2,3},{3,2},{4,5},{5,4},{6,7},{7,6},{8,9},{9,8},{10,11... | collective-permute-start | bytes 98312 | tf_op jit(solution)/shard_map/ppermute | solution.py:243
  27.9 3.9 %collective-permute-start.11 = (bf16[64,256]{1,0:T(8,128)(2,1)S(1)}, bf16[64,256]{1,0:T(8,128)(2,1)S(1)}, u32[]{:S(2)}, u32[]{:S(2)}) collective-permute-start(bf16[64,256]{1,0:T(8,128)(2,1)S(1)} %get-tuple-element.34.refs_5_), channel_id=1, source_target_pairs={{0,2},{1,3},{2,0},{3,1},{4,6},{5,7},{6,4},{7,5},{8,10},{9,11},{10,... | collective-permute-start | bytes 98312 | tf_op jit(solution)/shard_map/ppermute | solution.py:243
  28.5 3.7 %collective-permute-start.17 = (bf16[64,256]{1,0:T(8,128)(2,1)S(1)}, bf16[64,256]{1,0:T(8,128)(2,1)S(1)}, u32[]{:S(2)}, u32[]{:S(2)}) collective-permute-start(bf16[64,256]{1,0:T(8,128)(2,1)S(1)} %collective-permute-done.13.refs_8_), channel_id=1, source_target_pairs={{0,1},{1,0},{2,3},{3,2},{4,5},{5,4},{6,7},{7,6},{8,9},{9,8},{10,11... | collective-permute-start | bytes 98312 | tf_op jit(solution)/shard_map/ppermute | solution.py:243
  31.8 1.2 %collective-permute-start.15 = (bf16[64,256]{1,0:T(8,128)(2,1)S(1)}, bf16[64,256]{1,0:T(8,128)(2,1)S(1)}, u32[]{:S(2)}, u32[]{:S(2)}) collective-permute-start(bf16[64,256]{1,0:T(8,128)(2,1)S(1)} %collective-permute-done.11.refs_6_), channel_id=1, source_target_pairs={{0,1},{1,0},{2,3},{3,2},{4,5},{5,4},{6,7},{7,6},{8,9},{9,8},{10,11... | collective-permute-start | bytes 98312 | tf_op jit(solution)/shard_map/ppermute | solution.py:243

commit v4 on v3

--- a/solution.py
+++ b/solution.py
@@ -73,10 +73,9 @@
 
 def stage_kernel(
     prefix_ref, left_ref, layer_ref, side_ref, branch_ref, left_map_ref, right_map_ref,
-    own_ref, far_ref, codes_ref, side, branch, left_map, right_map, sems,
+    own_ref, left_own_ref, far_ref, codes_ref, side, branch, left_map, right_map, sems,
 ):
-    depth = prefix_ref.shape[0]
-    share = far_ref.shape[0] - depth
+    depth, share = prefix_ref.shape[0], far_ref.shape[0]
     start = pl.multiple_of(spot_of() * share, share)
     copies = [
         pltpu.make_async_copy(source, target, sems.at[k])
@@ -84,8 +83,8 @@
             (
                 (side_ref, side), (branch_ref, branch),
                 (left_map_ref, left_map), (right_map_ref, right_map),
-                (layer_ref.at[pl.ds(start, share), :], far_ref.at[pl.ds(0, share), :]),
-                (left_ref, far_ref.at[pl.ds(share, depth), :]),
+                (layer_ref.at[pl.ds(start, share), :], far_ref),
+                (left_ref, left_own_ref),
                 (prefix_ref, own_ref),
             )
         )
@@ -128,18 +127,11 @@
         pick_ref[...] = jnp.where(index == place, 1.0, 0.0).astype(jnp.bfloat16)
 
 
-def pack_kernel(own_ref, own_t_ref, far_ref, pair_ref, near_ref):
-    depth = own_ref.shape[0]
-    pair = jnp.concatenate([own_ref[...], own_t_ref[...]], axis=0)
-    pair_ref[...] = pair
-    near_ref[pl.ds(0, 2 * depth), :] = pair
-    near_ref[pl.ds(2 * depth, depth), :] = far_ref[pl.ds(far_ref.shape[0] - depth, depth), :]
-
-
-def left_pack_kernel(own_ref, near_ref, far_ref, cross_ref, out_ref):
-    depth = cross_ref.shape[0]
-    for k, ref in enumerate((own_ref, near_ref, far_ref, cross_ref)):
-        out_ref[pl.ds(k * depth, depth), :] = ref[pl.ds(ref.shape[0] - depth, depth), :]
+def join_kernel(sources, *refs):
+    out_ref, at = refs[-1], 0
+    for k, first, count in sources:
+        out_ref[pl.ds(at, count), :] = refs[k][pl.ds(first, count), :]
+        at += count
 
 
 def project_kernel(pieces, factor_ref, pick_ref, *refs):
@@ -157,26 +149,24 @@
 
 
 def right_own_kernel(layer_ref, projected_ref, out_ref):
-    paths = out_ref.shape[1]
     out_ref[...] = jnp.dot(
-        layer_ref[...], projected_ref[:, :paths], preferred_element_type=jnp.float32
+        layer_ref[...], projected_ref[...], preferred_element_type=jnp.float32
     ).astype(jnp.bfloat16)
 
 
-def right_far_kernel(layer_ref, far_ref, projected_ref, mine_ref, near_ref, cross_ref):
-    share, paths = mine_ref.shape
+def right_far_kernel(layer_ref, far_ref, here_ref, there_ref, mine_ref, near_ref, cross_ref):
+    share, _ = mine_ref.shape
     half = near_ref.shape[0] - share
     start = pl.multiple_of(lax.axis_index("tile") * half, half)
-    far = jnp.dot(
-        far_ref[pl.ds(0, share), :], projected_ref[...], preferred_element_type=jnp.float32
+    far = far_ref[...]
+    mine_ref[...] = jnp.dot(
+        far, here_ref[...], preferred_element_type=jnp.float32
     ).astype(jnp.bfloat16)
-    mine_ref[...] = far[:, :paths]
-    cross_ref[...] = far[:, paths:]
-    near_ref[pl.ds(half, share), :] = far[:, paths:]
+    cross = jnp.dot(far, there_ref[...], preferred_element_type=jnp.float32).astype(jnp.bfloat16)
+    cross_ref[...] = cross
+    near_ref[pl.ds(half, share), :] = cross
     near_ref[pl.ds(0, half), :] = jnp.dot(
-        layer_ref[pl.ds(start, half), :],
-        projected_ref[:, paths:],
-        preferred_element_type=jnp.float32,
+        layer_ref[pl.ds(start, half), :], there_ref[...], preferred_element_type=jnp.float32
     ).astype(jnp.bfloat16)
 
 
@@ -189,7 +179,7 @@
     other_ref[...] = states[:, paths:]
 
 
-def amplitude_kernel(left_count, *refs):
+def amplitude_kernel(left_pieces, left_count, *refs):
     left_refs, right_refs = refs[:left_count], refs[left_count:-4]
     out_ref, right_ref, block_ref, sems = refs[-4:]
     own_ref, mine_ref, x_ref, z_ref, xz_ref, mine_t_ref, x_t_ref, z_t_ref, xz_t_ref = right_refs
@@ -213,14 +203,18 @@
         place(z_piece, half, share, 3, (spot ^ spin) * share)
         place(xz_piece, 0, share, 3, (spot ^ (spin + tiles)) * share)
     right = right_ref[...]
-    depth = left_refs[0].shape[0]
     copies = []
-    for k, (ref, spin) in enumerate(zip(left_refs, (0, 1, tiles, 1 + tiles))):
-        block_ref[k] = lax.dot_general(
-            ref[...], right, CONTRACT_LAST, preferred_element_type=jnp.float32
+    for k, (source, first, count, spin, offset) in enumerate(left_pieces):
+        block_ref[k, pl.ds(0, count), :] = lax.dot_general(
+            left_refs[source][pl.ds(first, count), :],
+            right,
+            CONTRACT_LAST,
+            preferred_element_type=jnp.float32,
         ).astype(jnp.bfloat16)
-        start = pl.multiple_of((spot ^ spin) * depth, depth)
-        copy = pltpu.make_async_copy(block_ref.at[k], out_ref.at[pl.ds(start, depth), :], sems.at[k])
+        start = pl.multiple_of((spot ^ spin) * chunk + offset, count)
+        copy = pltpu.make_async_copy(
+            block_ref.at[k, pl.ds(0, count), :], out_ref.at[pl.ds(start, count), :], sems.at[k]
+        )
         copy.start()
         copies.append(copy)
     for copy in copies:
@@ -248,10 +242,14 @@
     spots = sizes[1] * sizes[2]
     share = chunk // spots
 
+    prefix_x = exchange(right_prefix, half=1)
     bits = branch_bits.T
-    own, far_pack, codes = call(
+    own, left_own, far_pack, codes = call(
         stage_kernel,
-        [(depth, gates), (share + depth, gates), jax.ShapeDtypeStruct((8, paths), jnp.int32)],
+        [
+            (depth, gates), (depth, gates), (share, gates),
+            jax.ShapeDtypeStruct((8, paths), jnp.int32),
+        ],
         right_prefix, left_prefix, right_layer,
         cut_side, bits, left_map[None, :], right_map[None, :],
         in_space=pltpu.HBM,
@@ -263,64 +261,65 @@
             pltpu.SemaphoreType.DMA((7,)),
         ),
     )
+    layer_x = exchange(left_layer, half=1)
     far = exchange(far_pack, plane=2)
-    prefix_x = exchange(right_prefix, half=1)
-    layer_x = exchange(left_layer, half=1)
-    own_t = exchange(own, tile=1)
+
+    def join(sources, *arrays):
+        count = sum(source[2] for source in sources)
+        kernel = functools.partial(join_kernel, sources)
+        return call(kernel, [(count, arrays[0].shape[1])], *arrays)[0]
+
+    pair = join(((0, 0, depth), (1, 0, depth), (2, 0, depth)), own, prefix_x, left_own)
+    near = exchange(pair, plane=1)
+    pair_t = exchange(pair, tile=1)
+    near_t = exchange(near, tile=1)
     left_factor, left_pick, right_factor, right_pick = call(
         mask_kernel,
         [(gates, paths), (sizes[0] * depth, paths), (gates, paths), (spots * depth, paths)],
         codes,
     )
-    pair, near_pack = call(
-        pack_kernel, [(2 * depth, gates), (3 * depth, gates)], own, own_t, far_pack
-    )
-    near = exchange(near_pack, plane=1)
-    pair_xz = exchange(pair, plane=1, half=1)
-    left_cross = exchange(left_prefix, plane=3)
-    prefix_xt = exchange(prefix_x, tile=1)
-
-    (right_projected,) = call(
-        functools.partial(
-            project_kernel,
-            (
-                ((0, 0, 2 * depth), (1, 0, depth), (2, 0, depth)),
-                ((3, 0, 2 * depth), (4, 0, 2 * depth)),
-            ),
-        ),
-        [(gates, 2 * paths)],
-        right_factor, right_pick, pair, prefix_x, prefix_xt, near, pair_xz,
+    left_pair = join(((0, 2 * depth, depth), (1, 2 * depth, depth)), pair, near)
+    left_far = exchange(left_pair, plane=2)
+    left_far_t = exchange(left_far, tile=1)
+
+    def project(sources, factor, pick, *arrays):
+        kernel = functools.partial(project_kernel, sources)
+        return call(kernel, [(gates, len(sources) * paths)], factor, pick, *arrays)[0]
+
+    here = project(
+        (((0, 0, depth), (1, 0, depth), (0, depth, depth), (1, depth, depth)),),
+        right_factor, right_pick, pair, pair_t,
+    )
+    (right_near,) = call(right_own_kernel, [(chunk, paths)], right_layer, here)
+    there = project(
+        (((0, 0, depth), (1, 0, depth), (0, depth, depth), (1, depth, depth)),),
+        right_factor, right_pick, near, near_t,
     )
     mine, for_near, cross = call(
         right_far_kernel,
         [(share, paths), (chunk // sizes[2] + share, paths), (share, paths)],
-        right_layer, far, right_projected,
+        right_layer, far, here, there,
     )
     right_pieces = [
         mine, exchange(mine, half=1), exchange(for_near, plane=1), exchange(cross, plane=1, half=1)
     ]
-    right_pieces = right_pieces + [exchange(piece, tile=1) for piece in right_pieces]
-    (right_near,) = call(right_own_kernel, [(chunk, paths)], right_layer, right_projected)
-
-    (left_rows,) = call(
-        left_pack_kernel, [(sizes[0] * depth, gates)], far_pack, near, far, left_cross
-    )
-    left_rows_t = exchange(left_rows, tile=1)
-    (left_projected,) = call(
-        functools.partial(
-            project_kernel, tuple(((k, 0, sizes[0] * depth),) for k in range(2))
+    right_pieces = right_pieces + [exchange(value, tile=1) for value in right_pieces]
+    left_projected = project(
+        (
+            ((0, 0, 2 * depth), (1, 0, 2 * depth)),
+            ((2, 2 * depth, depth), (3, 2 * depth, depth), (4, 0, 2 * depth)),
         ),
-        [(gates, 2 * paths)],
-        left_factor, left_pick, left_rows, left_rows_t,
+        left_factor, left_pick, left_pair, left_far, pair_t, near_t, left_far_t,
     )
     rows = left_layer.shape[0]
     own_mine, own_other = call(left_kernel, [(rows, paths)] * 2, left_layer, left_projected)
     x_mine, x_other = call(left_kernel, [(rows, paths)] * 2, layer_x, left_projected)
-    left_pieces = [own_mine, exchange(own_other, tile=1), x_mine, exchange(x_other, tile=1)]
+    left_states = [own_mine, exchange(own_other, tile=1), x_mine, exchange(x_other, tile=1)]
+    left_pieces = tuple((k, 0, rows, spin, 0) for k, spin in enumerate((0, 1, 2, 3)))
     (amplitude,) = call(
-        functools.partial(amplitude_kernel, len(left_pieces)),
+        functools.partial(amplitude_kernel, left_pieces, len(left_states)),
         [(spots * rows, sizes[0] * chunk)],
-        *left_pieces, right_near, *right_pieces,
+        *left_states, right_near, *right_pieces,
         scratch=(
             pltpu.VMEM((sizes[0] * chunk, paths), jnp.bfloat16),
             pltpu.VMEM((len(left_pieces), rows, sizes[0] * chunk), jnp.bfloat16),

time: 35 us -> 40.9 us (1.17)
  starting transfers between devices: 12 us -> 17.2 us
  waiting for transfers between devices: 16.6 us -> 17.4 us
    ppermute x18 -> x17, starting transfers between devices: 12 us -> 17.2 us  [exchange(): return lax.ppermute(value, DEVICE_AXES, pairs)]
    ppermute x18 -> x17, waiting for transfers between devices: 16.6 us -> 17.4 us  [exchange(): return lax.ppermute(value, DEVICE_AXES, pairs)]
    pallas_call x11 -> x12, Pallas kernels: 5.91 us -> 6.07 us  [call(): pl.pallas_call(kernel, out_shape=shapes, in_specs=[pl.BlockSpec(memory_sp...]
  transfers between devices with their start and end apart: 18 -> 17, of which waited for: 8 -> 6; matrix products, arithmetic and copies ran while one was open for 0% -> 0% of each run, Pallas kernels for 12% -> 11%
where the time goes in v4:
time: 40.9 us; the launch traced here: 40.8 us
  waiting for transfers between devices  17.4 us (43%)
  starting transfers between devices  17.2 us (42%)
  Pallas kernels  6.07 us (15%)
    ppermute x17, waiting for transfers between devices, exchange(): return lax.ppermute(value, DEVICE_AXES, pairs)  17.4 us
    ppermute x17, starting transfers between devices, exchange(): return lax.ppermute(value, DEVICE_AXES, pairs)  17.2 us
    pallas_call x12, Pallas kernels, call(): pl.pallas_call(kernel, out_shape=shapes, in_specs=[pl.BlockSpec(memory_sp...  6.07 us
  transfers between devices with their start and end apart: 17, of which 6 were waited for; matrix products, arithmetic and copies ran while one was open for 0% of the time, Pallas kernels for 11%

profile of v4, /device:TPU:0, one launch (start us, length us, event | category | flops | bytes accessed | tf_op | source)
XLA Modules:
  0.0 40.8 jit_solution(14437037040564174730)
XLA Ops:
  0.0 3.0 %collective-permute-start.7 = (bf16[256,1024]{1,0:T(8,128)(2,1)}, bf16[256,1024]{1,0:T(8,128)(2,1)S(1)}, u32[]{:S(2)}, u32[]{:S(2)}) collective-permute-start(bf16[256,1024]{1,0:T(8,128)(2,1)} %layer_ref.5), channel_id=1, source_target_pairs={{0,2},{1,3},{2,0},{3,1},{4,6},{5,7},{6,4},{7,5},{8,10},{9,11},{10,... | collective-permute-start | bytes 1572872 | tf_op jit(solution)/shard_map/ppermute | solution.py:237
  3.0 1.0 %shard_map.82 = (bf16[8,1024]{1,0:T(8,128)(2,1)S(1)}, bf16[8,1024]{1,0:T(8,128)(2,1)S(1)}, bf16[64,1024]{1,0:T(8,128)(2,1)S(1)}, s32[8,256]{1,0:T(8,128)S(1)}) custom-call(bf16[8,1024]{1,0:T(8,128)(2,1)} %prefix_ref.1, bf16[8,1024]{1,0:T(8,128)(2,1)} %left_ref.1, bf16[256,1024]{1,0:T(8,128)(2,1)} %layer_ref.7, s32[10]{0:T(128)} %side_ref.1, ...), custom_call_target="tpu_custom_call" | custom-call | tf_op jit(solution)/shard_map/pallas_call | solution.py:60
  4.0 2.7 %collective-permute-start.9 = (bf16[64,1024]{1,0:T(8,128)(2,1)S(1)}, bf16[64,1024]{1,0:T(8,128)(2,1)S(1)}, u32[]{:S(2)}, u32[]{:S(2)}) collective-permute-start(bf16[64,1024]{1,0:T(8,128)(2,1)S(1)} %get-tuple-element.31), channel_id=1, source_target_pairs={{0,8},{1,9},{2,10},{3,11},{4,12},{5,13},{6,14},{7,15},{8,0},{9,1},... | collective-permute-start | bytes 393224 | tf_op jit(solution)/shard_map/ppermute | solution.py:237
  6.7 0.5 %collective-permute-start = (bf16[8,1024]{1,0:T(8,128)(2,1)}, bf16[8,1024]{1,0:T(8,128)(2,1)S(1)}, u32[]{:S(2)}, u32[]{:S(2)}) collective-permute-start(bf16[8,1024]{1,0:T(8,128)(2,1)} %prefix_ref.1), channel_id=1, source_target_pairs={{0,2},{1,3},{2,0},{3,1},{4,6},{5,7},{6,4},{7,5},{8,10},{9,11},{10,... | collective-permute-start | bytes 49160 | tf_op jit(solution)/shard_map/ppermute | solution.py:237
  7.2 8.3 %collective-permute-done.refs_1_ = bf16[8,1024]{1,0:T(8,128)(2,1)S(1)} collective-permute-done((bf16[8,1024]{1,0:T(8,128)(2,1)}, bf16[8,1024]{1,0:T(8,128)(2,1)S(1)}, u32[]{:S(2)}, u32[]{:S(2)}) %collective-permute-start) | collective-permute-done | bytes 16416 | tf_op jit(solution)/shard_map/ppermute | solution.py:237
  15.5 1.8 %collective-permute-start.1 = (bf16[24,1024]{1,0:T(8,128)(2,1)S(1)}, bf16[24,1024]{1,0:T(8,128)(2,1)S(1)}, u32[]{:S(2)}, u32[]{:S(2)}) collective-permute-start(bf16[24,1024]{1,0:T(8,128)(2,1)S(1)} %shard_map.84.refs_0_), channel_id=1, source_target_pairs={{0,4},{1,5},{2,6},{3,7},{4,0},{5,1},{6,2},{7,3},{8,12},{9,13},{10,... | collective-permute-start | bytes 147464 | tf_op jit(solution)/shard_map/ppermute | solution.py:237
  17.3 2.3 %collective-permute-done.1.refs_1_.refs_0_ = bf16[24,1024]{1,0:T(8,128)(2,1)S(1)} collective-permute-done((bf16[24,1024]{1,0:T(8,128)(2,1)S(1)}, bf16[24,1024]{1,0:T(8,128)(2,1)S(1)}, u32[]{:S(2)}, u32[]{:S(2)}) %collective-permute-start.1) | collective-permute-done | bytes 49184 | tf_op jit(solution)/shard_map/ppermute | solution.py:237
  19.6 0.6 %shard_map.83 = (bf16[1024,256]{1,0:T(8,128)(2,1)S(1)}, bf16[32,256]{1,0:T(8,128)(2,1)S(1)}, bf16[1024,256]{1,0:T(8,128)(2,1)S(1)}, bf16[32,256]{1,0:T(8,128)(2,1)S(1)}) custom-call(s32[8,256]{1,0:T(8,128)S(1)} %get-tuple-element.20.codes_ref), custom_call_target="tpu_custom_call" | custom-call | tf_op jit(solution)/shard_map/pallas_call | solution.py:60
  20.2 2.9 %collective-permute-start.2 = (bf16[16,1024]{1,0:T(8,128)(2,1)S(1)}, bf16[16,1024]{1,0:T(8,128)(2,1)S(1)}, u32[]{:S(2)}, u32[]{:S(2)}) collective-permute-start(bf16[16,1024]{1,0:T(8,128)(2,1)S(1)} %shard_map.85.refs_0_), channel_id=1, source_target_pairs={{0,8},{1,9},{2,10},{3,11},{4,12},{5,13},{6,14},{7,15},{8,0},{9,1},... | collective-permute-start | bytes 98312 | tf_op jit(solution)/shard_map/ppermute | solution.py:237
  23.5 0.3 shard_map.91.there_ref
  23.8 0.4 shard_map.92
  24.2 1.6 %collective-permute-start.11 = (bf16[192,256]{1,0:T(8,128)(2,1)S(1)}, bf16[192,256]{1,0:T(8,128)(2,1)S(1)}, u32[]{:S(2)}, u32[]{:S(2)}) collective-permute-start(bf16[192,256]{1,0:T(8,128)(2,1)S(1)} %get-tuple-element.33), channel_id=1, source_target_pairs={{0,4},{1,5},{2,6},{3,7},{4,0},{5,1},{6,2},{7,3},{8,12},{9,13},{10,... | collective-permute-start | bytes 294920 | tf_op jit(solution)/shard_map/ppermute | solution.py:237
  25.9 1.2 %collective-permute-done.5.refs_4_ = bf16[16,1024]{1,0:T(8,128)(2,1)S(1)} collective-permute-done((bf16[16,1024]{1,0:T(8,128)(2,1)S(1)}, bf16[16,1024]{1,0:T(8,128)(2,1)S(1)}, u32[]{:S(2)}, u32[]{:S(2)}) %collective-permute-start.5) | collective-permute-done | bytes 32800 | tf_op jit(solution)/shard_map/ppermute | solution.py:237
  27.1 0.5 %shard_map.86.projected_ref = bf16[1024,512]{1,0:T(8,128)(2,1)S(1)} custom-call(bf16[1024,256]{1,0:T(8,128)(2,1)S(1)} %get-tuple-element.21.factor_ref, bf16[32,256]{1,0:T(8,128)(2,1)S(1)} %get-tuple-element.22.pick_ref, bf16[16,1024]{1,0:T(8,128)(2,1)S(1)} %shard_map.85.refs_0_, bf16[16,1024]{1,0:T(8,128)(2,1)S(1)} %collective-permute-done.2.refs_1_, ...), custom_call_target="tpu_custom_call" | custom-call | tf_op jit(solution)/shard_map/pallas_call | solution.py:60
  27.6 0.4 %shard_map.87 = (bf16[256,256]{1,0:T(8,128)(2,1)S(1)}, bf16[256,256]{1,0:T(8,128)(2,1)S(1)}) custom-call(bf16[256,1024]{1,0:T(8,128)(2,1)S(1)} %copy-done.1, bf16[1024,512]{1,0:T(8,128)(2,1)S(1)} %shard_map.86.projected_ref), custom_call_target="tpu_custom_call" | custom-call | tf_op jit(solution)/shard_map/pallas_call | solution.py:60
  28.2 0.4 %shard_map.88 = (bf16[256,256]{1,0:T(8,128)(2,1)S(1)}, bf16[256,256]{1,0:T(8,128)(2,1)S(1)}) custom-call(bf16[256,1024]{1,0:T(8,128)(2,1)S(1)} %collective-permute-done.7.layer_ref, bf16[1024,512]{1,0:T(8,128)(2,1)S(1)} %shard_map.86.projected_ref), custom_call_target="tpu_custom_call" | custom-call | tf_op jit(solution)/shard_map/pallas_call | solution.py:60
  28.7 0.4 %collective-permute-start.8 = (bf16[256,256]{1,0:T(8,128)(2,1)S(1)}, bf16[256,256]{1,0:T(8,128)(2,1)S(1)}, u32[]{:S(2)}, u32[]{:S(2)}) collective-permute-start(bf16[256,256]{1,0:T(8,128)(2,1)S(1)} %get-tuple-element.28), channel_id=1, source_target_pairs={{0,1},{1,0},{2,3},{3,2},{4,5},{5,4},{6,7},{7,6},{8,9},{9,8},{10,11... | collective-permute-start | bytes 393224 | tf_op jit(solution)/shard_map/ppermute | solution.py:237
  29.1 2.0 %collective-permute-start.12 = (bf16[64,256]{1,0:T(8,128)(2,1)S(1)}, bf16[64,256]{1,0:T(8,128)(2,1)S(1)}, u32[]{:S(2)}, u32[]{:S(2)}) collective-permute-start(bf16[64,256]{1,0:T(8,128)(2,1)S(1)} %get-tuple-element.34), channel_id=1, source_target_pairs={{0,6},{1,7},{2,4},{3,5},{4,2},{5,3},{6,0},{7,1},{8,14},{9,15},{10,... | collective-permute-start | bytes 98312 | tf_op jit(solution)/shard_map/ppermute | solution.py:237
  31.1 0.5 %collective-permute-start.13 = (bf16[64,256]{1,0:T(8,128)(2,1)S(1)}, bf16[64,256]{1,0:T(8,128)(2,1)S(1)}, u32[]{:S(2)}, u32[]{:S(2)}) collective-permute-start(bf16[64,256]{1,0:T(8,128)(2,1)S(1)} %get-tuple-element.32.refs_5_), channel_id=1, source_target_pairs={{0,1},{1,0},{2,3},{3,2},{4,5},{5,4},{6,7},{7,6},{8,9},{9,8},{10,11... | collective-permute-start | bytes 98312 | tf_op jit(solution)/shard_map/ppermute | solution.py:237
  31.6 2.3 %collective-permute-done.12.refs_8_ = bf16[64,256]{1,0:T(8,128)(2,1)S(1)} collective-permute-done((bf16[64,256]{1,0:T(8,128)(2,1)S(1)}, bf16[64,256]{1,0:T(8,128)(2,1)S(1)}, u32[]{:S(2)}, u32[]{:S(2)}) %collective-permute-start.12) | collective-permute-done | bytes 32800 | tf_op jit(solution)/shard_map/ppermute | solution.py:237
  33.9 1.5 %collective-permute-start.10 = (bf16[64,256]{1,0:T(8,128)(2,1)S(1)}, bf16[64,256]{1,0:T(8,128)(2,1)S(1)}, u32[]{:S(2)}, u32[]{:S(2)}) collective-permute-start(bf16[64,256]{1,0:T(8,128)(2,1)S(1)} %get-tuple-element.32.refs_5_), channel_id=1, source_target_pairs={{0,2},{1,3},{2,0},{3,1},{4,6},{5,7},{6,4},{7,5},{8,10},{9,11},{10,... | collective-permute-start | bytes 98312 | tf_op jit(solution)/shard_map/ppermute | solution.py:237
  35.4 2.4 %collective-permute-done.10.refs_6_ = bf16[64,256]{1,0:T(8,128)(2,1)S(1)} collective-permute-done((bf16[64,256]{1,0:T(8,128)(2,1)S(1)}, bf16[64,256]{1,0:T(8,128)(2,1)S(1)}, u32[]{:S(2)}, u32[]{:S(2)}) %collective-permute-start.10) | collective-permute-done | bytes 32800 | tf_op jit(solution)/shard_map/ppermute | solution.py:237
  38.1 0.9 %collective-permute-done.14.refs_10_ = bf16[64,256]{1,0:T(8,128)(2,1)S(1)} collective-permute-done((bf16[64,256]{1,0:T(8,128)(2,1)S(1)}, bf16[64,256]{1,0:T(8,128)(2,1)S(1)}, u32[]{:S(2)}, u32[]{:S(2)}) %collective-permute-start.14) | collective-permute-done | bytes 32800 | tf_op jit(solution)/shard_map/ppermute | solution.py:237
  39.0 1.7 %shard_map.93 = bf16[1024,1024]{1,0:T(8,128)(2,1)} custom-call(bf16[256,256]{1,0:T(8,128)(2,1)S(1)} %get-tuple-element.25.refs_0_, bf16[256,256]{1,0:T(8,128)(2,1)S(1)} %collective-permute-done.6.refs_1_, bf16[256,256]{1,0:T(8,128)(2,1)S(1)} %get-tuple-element.27.refs_2_, bf16[256,256]{1,0:T(8,128)(2,1)S(1)} %collective-permute-done.8.refs_3_, ...), custom_call_target="tpu_custom_call" | custom-call | tf_op jit(solution)/shard_map/pallas_call | solution.py:60
  (26 shorter events, 0.9 us)
Async XLA Ops:
  0.0 23.8 %copy-start = (bf16[256,1024]{1,0:T(8,128)(2,1)S(1)}, bf16[256,1024]{1,0:T(8,128)(2,1)}, u32[]{:S(2)}) copy-start(bf16[256,1024]{1,0:T(8,128)(2,1)} %layer_ref.7) | copy-start | bytes 1572868
  0.0 28.2 %collective-permute-start.7 = (bf16[256,1024]{1,0:T(8,128)(2,1)}, bf16[256,1024]{1,0:T(8,128)(2,1)S(1)}, u32[]{:S(2)}, u32[]{:S(2)}) collective-permute-start(bf16[256,1024]{1,0:T(8,128)(2,1)} %layer_ref.5), channel_id=1, source_target_pairs={{0,2},{1,3},{2,0},{3,1},{4,6},{5,7},{6,4},{7,5},{8,10},{9,11},{10,... | collective-permute-start | bytes 1572872 | tf_op jit(solution)/shard_map/ppermute | solution.py:237
  4.0 19.8 %collective-permute-start.9 = (bf16[64,1024]{1,0:T(8,128)(2,1)S(1)}, bf16[64,1024]{1,0:T(8,128)(2,1)S(1)}, u32[]{:S(2)}, u32[]{:S(2)}) collective-permute-start(bf16[64,1024]{1,0:T(8,128)(2,1)S(1)} %get-tuple-element.31), channel_id=1, source_target_pairs={{0,8},{1,9},{2,10},{3,11},{4,12},{5,13},{6,14},{7,15},{8,0},{9,1},... | collective-permute-start | bytes 393224 | tf_op jit(solution)/shard_map/ppermute | solution.py:237
  6.7 8.8 %collective-permute-start = (bf16[8,1024]{1,0:T(8,128)(2,1)}, bf16[8,1024]{1,0:T(8,128)(2,1)S(1)}, u32[]{:S(2)}, u32[]{:S(2)}) collective-permute-start(bf16[8,1024]{1,0:T(8,128)(2,1)} %prefix_ref.1), channel_id=1, source_target_pairs={{0,2},{1,3},{2,0},{3,1},{4,6},{5,7},{6,4},{7,5},{8,10},{9,11},{10,... | collective-permute-start | bytes 49160 | tf_op jit(solution)/shard_map/ppermute | solution.py:237
  15.5 4.1 %collective-permute-start.1 = (bf16[24,1024]{1,0:T(8,128)(2,1)S(1)}, bf16[24,1024]{1,0:T(8,128)(2,1)S(1)}, u32[]{:S(2)}, u32[]{:S(2)}) collective-permute-start(bf16[24,1024]{1,0:T(8,128)(2,1)S(1)} %shard_map.84.refs_0_), channel_id=1, source_target_pairs={{0,4},{1,5},{2,6},{3,7},{4,0},{5,1},{6,2},{7,3},{8,12},{9,13},{10,... | collective-permute-start | bytes 147464 | tf_op jit(solution)/shard_map/ppermute | solution.py:237
  17.3 5.8 %collective-permute-start.3 = (bf16[24,1024]{1,0:T(8,128)(2,1)S(1)}, bf16[24,1024]{1,0:T(8,128)(2,1)S(1)}, u32[]{:S(2)}, u32[]{:S(2)}) collective-permute-start(bf16[24,1024]{1,0:T(8,128)(2,1)S(1)} %shard_map.84.refs_0_), channel_id=1, source_target_pairs={{0,1},{1,0},{2,3},{3,2},{4,5},{5,4},{6,7},{7,6},{8,9},{9,8},{10,11... | collective-permute-start | bytes 147464 | tf_op jit(solution)/shard_map/ppermute | solution.py:237
  19.5 3.9 %collective-permute-start.4 = (bf16[24,1024]{1,0:T(8,128)(2,1)S(1)}, bf16[24,1024]{1,0:T(8,128)(2,1)S(1)}, u32[]{:S(2)}, u32[]{:S(2)}) collective-permute-start(bf16[24,1024]{1,0:T(8,128)(2,1)S(1)} %collective-permute-done.1.refs_1_.refs_0_), channel_id=1, source_target_pairs={{0,1},{1,0},{2,3},{3,2},{4,5},{5,4},{6,7},{7,6},{8,9},{9,8},{10,11... | collective-permute-start | bytes 147464 | tf_op jit(solution)/shard_map/ppermute | solution.py:237
  20.2 5.7 %collective-permute-start.2 = (bf16[16,1024]{1,0:T(8,128)(2,1)S(1)}, bf16[16,1024]{1,0:T(8,128)(2,1)S(1)}, u32[]{:S(2)}, u32[]{:S(2)}) collective-permute-start(bf16[16,1024]{1,0:T(8,128)(2,1)S(1)} %shard_map.85.refs_0_), channel_id=1, source_target_pairs={{0,8},{1,9},{2,10},{3,11},{4,12},{5,13},{6,14},{7,15},{8,0},{9,1},... | collective-permute-start | bytes 98312 | tf_op jit(solution)/shard_map/ppermute | solution.py:237
  23.5 4.1 %copy-start.1 = (bf16[256,1024]{1,0:T(8,128)(2,1)S(1)}, bf16[256,1024]{1,0:T(8,128)(2,1)}, u32[]{:S(2)}) copy-start(bf16[256,1024]{1,0:T(8,128)(2,1)} %layer_ref.5) | copy-start | bytes 1572868
  24.2 6.8 %collective-permute-start.11 = (bf16[192,256]{1,0:T(8,128)(2,1)S(1)}, bf16[192,256]{1,0:T(8,128)(2,1)S(1)}, u32[]{:S(2)}, u32[]{:S(2)}) collective-permute-start(bf16[192,256]{1,0:T(8,128)(2,1)S(1)} %get-tuple-element.33), channel_id=1, source_target_pairs={{0,4},{1,5},{2,6},{3,7},{4,0},{5,1},{6,2},{7,3},{8,12},{9,13},{10,... | collective-permute-start | bytes 294920 | tf_op jit(solution)/shard_map/ppermute | solution.py:237
  25.9 1.2 %collective-permute-start.5 = (bf16[16,1024]{1,0:T(8,128)(2,1)S(1)}, bf16[16,1024]{1,0:T(8,128)(2,1)S(1)}, u32[]{:S(2)}, u32[]{:S(2)}) collective-permute-start(bf16[16,1024]{1,0:T(8,128)(2,1)S(1)} %collective-permute-done.2.refs_1_), channel_id=1, source_target_pairs={{0,1},{1,0},{2,3},{3,2},{4,5},{5,4},{6,7},{7,6},{8,9},{9,8},{10,11... | collective-permute-start | bytes 98312 | tf_op jit(solution)/shard_map/ppermute | solution.py:237
  28.0 11.0 %collective-permute-start.6 = (bf16[256,256]{1,0:T(8,128)(2,1)S(1)}, bf16[256,256]{1,0:T(8,128)(2,1)S(1)}, u32[]{:S(2)}, u32[]{:S(2)}) collective-permute-start(bf16[256,256]{1,0:T(8,128)(2,1)S(1)} %get-tuple-element.26), channel_id=1, source_target_pairs={{0,1},{1,0},{2,3},{3,2},{4,5},{5,4},{6,7},{7,6},{8,9},{9,8},{10,11... | collective-permute-start | bytes 393224 | tf_op jit(solution)/shard_map/ppermute | solution.py:237
  28.7 10.4 %collective-permute-start.8 = (bf16[256,256]{1,0:T(8,128)(2,1)S(1)}, bf16[256,256]{1,0:T(8,128)(2,1)S(1)}, u32[]{:S(2)}, u32[]{:S(2)}) collective-permute-start(bf16[256,256]{1,0:T(8,128)(2,1)S(1)} %get-tuple-element.28), channel_id=1, source_target_pairs={{0,1},{1,0},{2,3},{3,2},{4,5},{5,4},{6,7},{7,6},{8,9},{9,8},{10,11... | collective-permute-start | bytes 393224 | tf_op jit(solution)/shard_map/ppermute | solution.py:237
  29.1 4.8 %collective-permute-start.12 = (bf16[64,256]{1,0:T(8,128)(2,1)S(1)}, bf16[64,256]{1,0:T(8,128)(2,1)S(1)}, u32[]{:S(2)}, u32[]{:S(2)}) collective-permute-start(bf16[64,256]{1,0:T(8,128)(2,1)S(1)} %get-tuple-element.34), channel_id=1, source_target_pairs={{0,6},{1,7},{2,4},{3,5},{4,2},{5,3},{6,0},{7,1},{8,14},{9,15},{10,... | collective-permute-start | bytes 98312 | tf_op jit(solution)/shard_map/ppermute | solution.py:237
  31.1 8.0 %collective-permute-start.15 = (bf16[192,256]{1,0:T(8,128)(2,1)S(1)}, bf16[192,256]{1,0:T(8,128)(2,1)S(1)}, u32[]{:S(2)}, u32[]{:S(2)}) collective-permute-start(bf16[192,256]{1,0:T(8,128)(2,1)S(1)} %collective-permute-done.11.refs_7_), channel_id=1, source_target_pairs={{0,1},{1,0},{2,3},{3,2},{4,5},{5,4},{6,7},{7,6},{8,9},{9,8},{10,11... | collective-permute-start | bytes 294920 | tf_op jit(solution)/shard_map/ppermute | solution.py:237
  31.1 4.3 %collective-permute-start.13 = (bf16[64,256]{1,0:T(8,128)(2,1)S(1)}, bf16[64,256]{1,0:T(8,128)(2,1)S(1)}, u32[]{:S(2)}, u32[]{:S(2)}) collective-permute-start(bf16[64,256]{1,0:T(8,128)(2,1)S(1)} %get-tuple-element.32.refs_5_), channel_id=1, source_target_pairs={{0,1},{1,0},{2,3},{3,2},{4,5},{5,4},{6,7},{7,6},{8,9},{9,8},{10,11... | collective-permute-start | bytes 98312 | tf_op jit(solution)/shard_map/ppermute | solution.py:237
  33.9 3.9 %collective-permute-start.10 = (bf16[64,256]{1,0:T(8,128)(2,1)S(1)}, bf16[64,256]{1,0:T(8,128)(2,1)S(1)}, u32[]{:S(2)}, u32[]{:S(2)}) collective-permute-start(bf16[64,256]{1,0:T(8,128)(2,1)S(1)} %get-tuple-element.32.refs_5_), channel_id=1, source_target_pairs={{0,2},{1,3},{2,0},{3,1},{4,6},{5,7},{6,4},{7,5},{8,10},{9,11},{10,... | collective-permute-start | bytes 98312 | tf_op jit(solution)/shard_map/ppermute | solution.py:237
  35.4 2.7 %collective-permute-start.16 = (bf16[64,256]{1,0:T(8,128)(2,1)S(1)}, bf16[64,256]{1,0:T(8,128)(2,1)S(1)}, u32[]{:S(2)}, u32[]{:S(2)}) collective-permute-start(bf16[64,256]{1,0:T(8,128)(2,1)S(1)} %collective-permute-done.12.refs_8_), channel_id=1, source_target_pairs={{0,1},{1,0},{2,3},{3,2},{4,5},{5,4},{6,7},{7,6},{8,9},{9,8},{10,11... | collective-permute-start | bytes 98312 | tf_op jit(solution)/shard_map/ppermute | solution.py:237
  37.8 1.2 %collective-permute-start.14 = (bf16[64,256]{1,0:T(8,128)(2,1)S(1)}, bf16[64,256]{1,0:T(8,128)(2,1)S(1)}, u32[]{:S(2)}, u32[]{:S(2)}) collective-permute-start(bf16[64,256]{1,0:T(8,128)(2,1)S(1)} %collective-permute-done.10.refs_6_), channel_id=1, source_target_pairs={{0,1},{1,0},{2,3},{3,2},{4,5},{5,4},{6,7},{7,6},{8,9},{9,8},{10,11... | collective-permute-start | bytes 98312 | tf_op jit(solution)/shard_map/ppermute | solution.py:237

commit v5 on v4

--- a/solution.py
+++ b/solution.py
@@ -52,7 +52,7 @@
 
 def call(kernel, outs, *operands, in_space=pltpu.VMEM, scratch=(), out_space=pltpu.VMEM):
     shapes = [
-        jax.ShapeDtypeStruct(out, jnp.bfloat16) if isinstance(out, tuple) else out for out in outs
+        out_space(out, jnp.bfloat16) if isinstance(out, tuple) else out for out in outs
     ]
     spaces = [in_space] * len(operands)
     if in_space == pltpu.HBM:
@@ -71,53 +71,43 @@
     return lax.axis_index("half") * lax.axis_size("tile") + lax.axis_index("tile")
 
 
-def stage_kernel(
-    prefix_ref, left_ref, layer_ref, side_ref, branch_ref, left_map_ref, right_map_ref,
-    own_ref, left_own_ref, far_ref, codes_ref, side, branch, left_map, right_map, sems,
-):
-    depth, share = prefix_ref.shape[0], far_ref.shape[0]
-    start = pl.multiple_of(spot_of() * share, share)
-    copies = [
-        pltpu.make_async_copy(source, target, sems.at[k])
-        for k, (source, target) in enumerate(
-            (
-                (side_ref, side), (branch_ref, branch),
-                (left_map_ref, left_map), (right_map_ref, right_map),
-                (layer_ref.at[pl.ds(start, share), :], far_ref),
-                (left_ref, left_own_ref),
-                (prefix_ref, own_ref),
-            )
-        )
-    ]
+def stage_kernel(*refs):
+    layer_ref, sources, targets, sems = refs[0], refs[1:7], refs[8:14], refs[14]
+    far_ref = refs[7]
+    share = far_ref.shape[0]
+    order = lax.axis_index("tile") * lax.axis_size("half") + lax.axis_index("half")
+    start = pl.multiple_of(order * share, share)
+    copies = [pltpu.make_async_copy(layer_ref.at[pl.ds(start, share), :], far_ref, sems.at[0])]
+    for k, (source, target) in enumerate(zip(sources, targets)):
+        copies.append(pltpu.make_async_copy(source, target, sems.at[k + 1]))
     for copy in copies:
         copy.start()
-    for copy in copies[:4]:
+    for copy in copies:
         copy.wait()
-    cuts, paths = branch.shape
-    for half, (map_ref, shard) in enumerate(
-        ((left_map, lax.axis_index("path")), (right_map, spot_of()))
+
+
+def mask_kernel(side_ref, branch_ref, left_map_ref, right_map_ref, *out_refs):
+    cuts, paths = branch_ref.shape
+    for half, (map_ref, shard, shards) in enumerate(
+        (
+            (left_map_ref, lax.axis_index("path"), lax.axis_size("path")),
+            (right_map_ref, spot_of(), lax.axis_size("half") * lax.axis_size("tile")),
+        )
     ):
+        factor_ref, pick_ref = out_refs[2 * half:][:2]
         wanted = jnp.zeros((1, paths), jnp.int32)
         phased = jnp.zeros((1, paths), jnp.int32)
-        mask = jnp.int32(0)
+        mask = jnp.zeros((1, 1), jnp.int32)
         for cut in range(cuts):
-            projector = 1 - side[cut] if half else side[cut]
-            bits = branch[pl.ds(cut, 1), :]
+            side = side_ref[:, pl.ds(cut, 1)]
+            projector = 1 - side if half else side
+            bits = branch_ref[pl.ds(cut, 1), :]
             wanted += bits * (projector << cut)
             phased += bits * ((1 - projector) << cut)
             mask += projector << cut
+        depth = pick_ref.shape[0] // shards
         row = map_ref[...]
         place = (lax.div(row, depth) ^ shard) * depth + lax.rem(row, depth)
-        for k, code in enumerate((wanted, phased, place, jnp.full((1, paths), mask))):
-            codes_ref[pl.ds(4 * half + k, 1), :] = code
-    for copy in copies[4:]:
-        copy.wait()
-
-
-def mask_kernel(codes_ref, *out_refs):
-    for half in range(2):
-        factor_ref, pick_ref = out_refs[2 * half:][:2]
-        wanted, phased, place, mask = (codes_ref[pl.ds(4 * half + k, 1), :] for k in range(4))
         gate = lax.broadcasted_iota(jnp.int32, factor_ref.shape, 0)
         hit = (gate & mask) == wanted
         odd = (lax.population_count(gate & phased) & 1) == 1
@@ -170,53 +160,77 @@
     ).astype(jnp.bfloat16)
 
 
-def left_kernel(layer_ref, projected_ref, mine_ref, other_ref):
-    paths = mine_ref.shape[1]
-    states = jnp.dot(
-        layer_ref[...], projected_ref[...], preferred_element_type=jnp.float32
-    ).astype(jnp.bfloat16)
-    mine_ref[...] = states[:, :paths]
-    other_ref[...] = states[:, paths:]
-
-
-def amplitude_kernel(left_pieces, left_count, *refs):
+def left_kernel(own_ref, x_ref, projected_ref, mine_ref, other_ref):
+    rows, paths = own_ref.shape[0], mine_ref.shape[1]
+    for k, layer_ref in enumerate((own_ref, x_ref)):
+        states = jnp.dot(
+            layer_ref[...], projected_ref[...], preferred_element_type=jnp.float32
+        ).astype(jnp.bfloat16)
+        mine_ref[pl.ds(k * rows, rows), :] = states[:, :paths]
+        other_ref[pl.ds(k * rows, rows), :] = states[:, paths:]
+
+
+def join_right(right_ref, at, mine_ref, x_ref, z_ref, xz_ref):
+    half, share = lax.axis_index("half"), mine_ref.shape[0]
+    side = z_ref.shape[0] - share
+    right_ref[pl.ds(at, side), :] = z_ref[pl.ds(0, side), :]
+    for plane, near_ref, first, far_ref in ((2, mine_ref, 0, x_ref), (3, z_ref, side, xz_ref)):
+        base = at + (plane - 1) * side
+        right_ref[pl.ds(pl.multiple_of(base + half * share, share), share), :] = near_ref[
+            pl.ds(first, share), :
+        ]
+        right_ref[pl.ds(pl.multiple_of(base + (half ^ 1) * share, share), share), :] = far_ref[...]
+
+
+def left_blocks(left_refs):
+    for tile, ref in enumerate(left_refs):
+        rows = ref.shape[0] // 2
+        for half in range(2):
+            spin = half * lax.axis_size("tile") + tile
+            row = pl.multiple_of((spot_of() ^ spin) * rows, rows)
+            yield ref[pl.ds(half * rows, rows), :], rows, row
+
+
+def amplitude_near_kernel(left_count, *refs):
+    left_refs, right_refs, (out_ref, right_ref) = refs[:left_count], refs[left_count:-2], refs[-2:]
+    chunk = right_refs[0].shape[0]
+    right_ref[pl.ds(0, chunk), :] = right_refs[0][...]
+    join_right(right_ref, chunk, *right_refs[1:])
+    right = right_ref[...]
+    for left, rows, row in left_blocks(left_refs):
+        out_ref[pl.ds(row, rows), :] = lax.dot_general(
+            left, right, CONTRACT_LAST, preferred_element_type=jnp.float32
+        ).astype(jnp.bfloat16)
+
+
+def amplitude_rest_kernel(left_count, near_ref, *refs):
     left_refs, right_refs = refs[:left_count], refs[left_count:-4]
     out_ref, right_ref, block_ref, sems = refs[-4:]
-    own_ref, mine_ref, x_ref, z_ref, xz_ref, mine_t_ref, x_t_ref, z_t_ref, xz_t_ref = right_refs
-    path, tile, spot = lax.axis_index("path"), lax.axis_index("tile"), spot_of()
-    tiles = lax.axis_size("tile")
-    chunk, share = own_ref.shape[0], mine_ref.shape[0]
-    half = z_ref.shape[0] - share
-
-    def place(ref, first, count, plane, offset):
-        start = pl.multiple_of((path ^ plane) * chunk + offset, count)
-        right_ref[pl.ds(start, count), :] = ref[pl.ds(first, count), :]
-
-    place(own_ref, 0, chunk, 0, 0)
-    place(z_ref, 0, half, 1, tile * half)
-    place(z_t_ref, 0, half, 1, (tile ^ 1) * half)
-    for spin, (near_ref, x_piece, z_piece, xz_piece) in enumerate(
-        ((mine_ref, x_ref, z_ref, xz_ref), (mine_t_ref, x_t_ref, z_t_ref, xz_t_ref))
-    ):
-        place(near_ref, 0, share, 2, (spot ^ spin) * share)
-        place(x_piece, 0, share, 2, (spot ^ (spin + tiles)) * share)
-        place(z_piece, half, share, 3, (spot ^ spin) * share)
-        place(xz_piece, 0, share, 3, (spot ^ (spin + tiles)) * share)
+    path, tile = lax.axis_index("path"), lax.axis_index("tile")
+    side = right_ref.shape[0] // 3
+    chunk = side * lax.axis_size("tile")
+    copies = []
+
+    def send(source, row, rows, column, width):
+        place = pl.ds(row, rows), pl.ds(pl.multiple_of(column, side), width)
+        copy = pltpu.make_async_copy(source, out_ref.at[place], sems.at[len(copies)])
+        copies.append(copy)
+        copy.start()
+
+    height = near_ref.shape[0]
+    send(near_ref.at[:, pl.ds(0, chunk)], 0, height, path * chunk, chunk)
+    for plane in range(1, 4):
+        source = near_ref.at[:, pl.ds(chunk + (plane - 1) * side, side)]
+        send(source, 0, height, (path ^ plane) * chunk + tile * side, side)
+    join_right(right_ref, 0, *right_refs)
     right = right_ref[...]
-    copies = []
-    for k, (source, first, count, spin, offset) in enumerate(left_pieces):
-        block_ref[k, pl.ds(0, count), :] = lax.dot_general(
-            left_refs[source][pl.ds(first, count), :],
-            right,
-            CONTRACT_LAST,
-            preferred_element_type=jnp.float32,
+    for k, (left, rows, row) in enumerate(left_blocks(left_refs)):
+        block_ref[k] = lax.dot_general(
+            left, right, CONTRACT_LAST, preferred_element_type=jnp.float32
         ).astype(jnp.bfloat16)
-        start = pl.multiple_of((spot ^ spin) * chunk + offset, count)
-        copy = pltpu.make_async_copy(
-            block_ref.at[k, pl.ds(0, count), :], out_ref.at[pl.ds(start, count), :], sems.at[k]
-        )
-        copy.start()
-        copies.append(copy)
+        for plane in range(1, 4):
+            source = block_ref.at[k, :, pl.ds((plane - 1) * side, side)]
+            send(source, row, rows, (path ^ plane) * chunk + (tile ^ 1) * side, side)
     for copy in copies:
         copy.wait()
 
@@ -243,23 +257,14 @@
     share = chunk // spots
 
     prefix_x = exchange(right_prefix, half=1)
-    bits = branch_bits.T
-    own, left_own, far_pack, codes = call(
+    small = (cut_side[None, :], branch_bits.T, left_map[None, :], right_map[None, :])
+    far_pack, own, left_own, *small = call(
         stage_kernel,
-        [
-            (depth, gates), (depth, gates), (share, gates),
-            jax.ShapeDtypeStruct((8, paths), jnp.int32),
-        ],
-        right_prefix, left_prefix, right_layer,
-        cut_side, bits, left_map[None, :], right_map[None, :],
+        [(share, gates), (depth, gates), (depth, gates)]
+        + [jax.ShapeDtypeStruct(x.shape, x.dtype) for x in small],
+        right_layer, right_prefix, left_prefix, *small,
         in_space=pltpu.HBM,
-        scratch=(
-            pltpu.SMEM(cut_side.shape, jnp.int32),
-            pltpu.VMEM(bits.shape, jnp.int32),
-            pltpu.VMEM((1, paths), jnp.int32),
-            pltpu.VMEM((1, paths), jnp.int32),
-            pltpu.SemaphoreType.DMA((7,)),
-        ),
+        scratch=(pltpu.SemaphoreType.DMA((7,)),),
     )
     layer_x = exchange(left_layer, half=1)
     far = exchange(far_pack, plane=2)
@@ -276,7 +281,7 @@
     left_factor, left_pick, right_factor, right_pick = call(
         mask_kernel,
         [(gates, paths), (sizes[0] * depth, paths), (gates, paths), (spots * depth, paths)],
-        codes,
+        *small,
     )
     left_pair = join(((0, 2 * depth, depth), (1, 2 * depth, depth)), pair, near)
     left_far = exchange(left_pair, plane=2)
@@ -303,7 +308,7 @@
     right_pieces = [
         mine, exchange(mine, half=1), exchange(for_near, plane=1), exchange(cross, plane=1, half=1)
     ]
-    right_pieces = right_pieces + [exchange(value, tile=1) for value in right_pieces]
+    right_pieces_t = [exchange(piece, tile=1) for piece in right_pieces]
     left_projected = project(
         (
             ((0, 0, 2 * depth), (1, 0, 2 * depth)),
@@ -312,22 +317,29 @@
         left_factor, left_pick, left_pair, left_far, pair_t, near_t, left_far_t,
     )
     rows = left_layer.shape[0]
-    own_mine, own_other = call(left_kernel, [(rows, paths)] * 2, left_layer, left_projected)
-    x_mine, x_other = call(left_kernel, [(rows, paths)] * 2, layer_x, left_projected)
-    left_states = [own_mine, exchange(own_other, tile=1), x_mine, exchange(x_other, tile=1)]
-    left_pieces = tuple((k, 0, rows, spin, 0) for k, spin in enumerate((0, 1, 2, 3)))
+    left_mine, left_other = call(
+        left_kernel, [(2 * rows, paths)] * 2, left_layer, layer_x, left_projected
+    )
+    left_states = [left_mine, exchange(left_other, tile=1)]
+    side = chunk // sizes[2]
+    height = spots * rows
     (amplitude,) = call(
-        functools.partial(amplitude_kernel, left_pieces, len(left_states)),
-        [(spots * rows, sizes[0] * chunk)],
+        functools.partial(amplitude_near_kernel, len(left_states)),
+        [(height, chunk + 3 * side)],
         *left_states, right_near, *right_pieces,
+        scratch=(pltpu.VMEM((chunk + 3 * side, paths), jnp.bfloat16),),
+    )
+    return call(
+        functools.partial(amplitude_rest_kernel, len(left_states)),
+        [(height, sizes[0] * chunk)],
+        amplitude, *left_states, *right_pieces_t,
         scratch=(
-            pltpu.VMEM((sizes[0] * chunk, paths), jnp.bfloat16),
-            pltpu.VMEM((len(left_pieces), rows, sizes[0] * chunk), jnp.bfloat16),
-            pltpu.SemaphoreType.DMA((len(left_pieces),)),
+            pltpu.VMEM((3 * side, paths), jnp.bfloat16),
+            pltpu.VMEM((spots, rows, 3 * side), jnp.bfloat16),
+            pltpu.SemaphoreType.DMA((4 + 3 * spots,)),
         ),
-        out_space=pl.ANY,
-    )
-    return amplitude
+        out_space=pltpu.HBM,
+    )[0]
 
 
 def solution(mesh):

time: 40.9 us -> 43.9 us (1.073)
  waiting for transfers between devices: 17.4 us -> 24.9 us
  starting transfers between devices: 17.2 us -> 12 us
  Pallas kernels: 6.07 us -> 6.66 us
    ppermute x17 -> x16, waiting for transfers between devices: 17.4 us -> 24.9 us  [exchange(): return lax.ppermute(value, DEVICE_AXES, pairs)]
    ppermute x17 -> x16, starting transfers between devices: 17.2 us -> 12 us  [exchange(): return lax.ppermute(value, DEVICE_AXES, pairs)]
    pallas_call x12, Pallas kernels: 6.07 us -> 6.66 us  [call(): pl.pallas_call(kernel, out_shape=shapes, in_specs=[pl.BlockSpec(memory_sp...]
  transfers between devices with their start and end apart: 17 -> 16, of which waited for: 6 -> 8; matrix products, arithmetic and copies ran while one was open for 0% -> 0% of each run, Pallas kernels for 11% -> 12%
where the time goes in v5:
time: 43.9 us; the launch traced here: 43.8 us
  waiting for transfers between devices  24.9 us (57%)
  starting transfers between devices  12 us (27%)
  Pallas kernels  6.66 us (15%)
    ppermute x16, waiting for transfers between devices, exchange(): return lax.ppermute(value, DEVICE_AXES, pairs)  24.9 us
    ppermute x16, starting transfers between devices, exchange(): return lax.ppermute(value, DEVICE_AXES, pairs)  12 us
    pallas_call x12, Pallas kernels, call(): pl.pallas_call(kernel, out_shape=shapes, in_specs=[pl.BlockSpec(memory_sp...  6.66 us
  transfers between devices with their start and end apart: 16, of which 8 were waited for; matrix products, arithmetic and copies ran while one was open for 0% of the time, Pallas kernels for 12%

profile of v5, /device:TPU:0, one launch (start us, length us, event | category | flops | bytes accessed | tf_op | source)
XLA Modules:
  0.0 43.8 jit_solution(1375966678864379769)
XLA Ops:
  0.0 3.0 %collective-permute-start = (bf16[256,1024]{1,0:T(8,128)(2,1)}, bf16[256,1024]{1,0:T(8,128)(2,1)S(1)}, u32[]{:S(2)}, u32[]{:S(2)}) collective-permute-start(bf16[256,1024]{1,0:T(8,128)(2,1)} %own_ref.1), channel_id=1, source_target_pairs={{0,2},{1,3},{2,0},{3,1},{4,6},{5,7},{6,4},{7,5},{8,10},{9,11},{10,... | collective-permute-start | bytes 1572872 | tf_op jit(solution)/shard_map/ppermute | solution.py:251
  3.0 1.0 %shard_map.82 = (bf16[64,1024]{1,0:T(8,128)(2,1)S(1)}, bf16[8,1024]{1,0:T(8,128)(2,1)S(1)}, bf16[8,1024]{1,0:T(8,128)(2,1)S(1)}, s32[1,10]{1,0:T(1,128)S(1)}, s3...) custom-call(bf16[256,1024]{1,0:T(8,128)(2,1)} %layer_ref.3, bf16[8,1024]{1,0:T(8,128)(2,1)} %refs_1_.1, ...), custom_call_target="tpu_custom_call" | custom-call | tf_op jit(solution)/shard_map/pallas_call | solution.py:60
  4.0 11.5 %collective-permute-done.1.refs_1_ = bf16[8,1024]{1,0:T(8,128)(2,1)S(1)} collective-permute-done((bf16[8,1024]{1,0:T(8,128)(2,1)}, bf16[8,1024]{1,0:T(8,128)(2,1)S(1)}, u32[]{:S(2)}, u32[]{:S(2)}) %collective-permute-start.1) | collective-permute-done | bytes 16416 | tf_op jit(solution)/shard_map/ppermute | solution.py:251
  15.5 1.8 %collective-permute-start.2 = (bf16[24,1024]{1,0:T(8,128)(2,1)S(1)}, bf16[24,1024]{1,0:T(8,128)(2,1)S(1)}, u32[]{:S(2)}, u32[]{:S(2)}) collective-permute-start(bf16[24,1024]{1,0:T(8,128)(2,1)S(1)} %shard_map.84.refs_0_), channel_id=1, source_target_pairs={{0,4},{1,5},{2,6},{3,7},{4,0},{5,1},{6,2},{7,3},{8,12},{9,13},{10,... | collective-permute-start | bytes 147464 | tf_op jit(solution)/shard_map/ppermute | solution.py:251
  17.3 2.3 %collective-permute-done.2.refs_1_.refs_0_ = bf16[24,1024]{1,0:T(8,128)(2,1)S(1)} collective-permute-done((bf16[24,1024]{1,0:T(8,128)(2,1)S(1)}, bf16[24,1024]{1,0:T(8,128)(2,1)S(1)}, u32[]{:S(2)}, u32[]{:S(2)}) %collective-permute-start.2) | collective-permute-done | bytes 49184 | tf_op jit(solution)/shard_map/ppermute | solution.py:251
  19.6 2.8 %collective-permute-start.3 = (bf16[16,1024]{1,0:T(8,128)(2,1)S(1)}, bf16[16,1024]{1,0:T(8,128)(2,1)S(1)}, u32[]{:S(2)}, u32[]{:S(2)}) collective-permute-start(bf16[16,1024]{1,0:T(8,128)(2,1)S(1)} %shard_map.85.refs_0_), channel_id=1, source_target_pairs={{0,8},{1,9},{2,10},{3,11},{4,12},{5,13},{6,14},{7,15},{8,0},{9,1},... | collective-permute-start | bytes 98312 | tf_op jit(solution)/shard_map/ppermute | solution.py:251
  22.6 0.5 %collective-permute-start.5 = (bf16[24,1024]{1,0:T(8,128)(2,1)S(1)}, bf16[24,1024]{1,0:T(8,128)(2,1)S(1)}, u32[]{:S(2)}, u32[]{:S(2)}) collective-permute-start(bf16[24,1024]{1,0:T(8,128)(2,1)S(1)} %collective-permute-done.2.refs_1_.refs_0_), channel_id=1, source_target_pairs={{0,1},{1,0},{2,3},{3,2},{4,5},{5,4},{6,7},{7,6},{8,9},{9,8},{10,11... | collective-permute-start | bytes 147464 | tf_op jit(solution)/shard_map/ppermute | solution.py:251
  23.1 3.5 %collective-permute-done.3.refs_1_ = bf16[16,1024]{1,0:T(8,128)(2,1)S(1)} collective-permute-done((bf16[16,1024]{1,0:T(8,128)(2,1)S(1)}, bf16[16,1024]{1,0:T(8,128)(2,1)S(1)}, u32[]{:S(2)}, u32[]{:S(2)}) %collective-permute-start.3) | collective-permute-done | bytes 32800 | tf_op jit(solution)/shard_map/ppermute | solution.py:251
  26.5 1.1 %shard_map.83 = (bf16[1024,256]{1,0:T(8,128)(2,1)S(1)}, bf16[32,256]{1,0:T(8,128)(2,1)S(1)}, bf16[1024,256]{1,0:T(8,128)(2,1)S(1)}, bf16[32,256]{1,0:T(8,128)(2,1)S(1)}) custom-call(s32[1,10]{1,0:T(1,128)S(1)} %get-tuple-element.21.side_ref, s32[10,256]{1,0:T(8,128)S(1)} %get-tuple-element.22.branch_ref, s32[1,256]{1,0:T(1,128)S(1)} %get-tuple-element.23.left_map_ref, ...), custom_call_target="tpu_custom_call" | custom-call | tf_op jit(solution)/shard_map/pallas_call | solution.py:60
  27.7 0.5 %shard_map.86.projected_ref = bf16[1024,512]{1,0:T(8,128)(2,1)S(1)} custom-call(bf16[1024,256]{1,0:T(8,128)(2,1)S(1)} %get-tuple-element.25.factor_ref, bf16[32,256]{1,0:T(8,128)(2,1)S(1)} %get-tuple-element.26.pick_ref, bf16[16,1024]{1,0:T(8,128)(2,1)S(1)} %shard_map.85.refs_0_, bf16[16,1024]{1,0:T(8,128)(2,1)S(1)} %collective-permute-done.3.refs_1_, ...), custom_call_target="tpu_custom_call" | custom-call | tf_op jit(solution)/shard_map/pallas_call | solution.py:60
  28.3 0.7 %shard_map.87 = (bf16[512,256]{1,0:T(8,128)(2,1)S(1)}, bf16[512,256]{1,0:T(8,128)(2,1)S(1)}) custom-call(bf16[256,1024]{1,0:T(8,128)(2,1)S(1)} %copy-done.1, bf16[256,1024]{1,0:T(8,128)(2,1)S(1)} %collective-permute-done.x_ref, bf16[1024,512]{1,0:T(8,128)(2,1)S(1)} %shard_map.86.projected_ref), custom_call_target="tpu_custom_call" | custom-call | tf_op jit(solution)/shard_map/pallas_call | solution.py:60
  29.0 0.5 %collective-permute-start.7 = (bf16[512,256]{1,0:T(8,128)(2,1)S(1)}, bf16[512,256]{1,0:T(8,128)(2,1)S(1)}, u32[]{:S(2)}, u32[]{:S(2)}) collective-permute-start(bf16[512,256]{1,0:T(8,128)(2,1)S(1)} %get-tuple-element.30), channel_id=1, source_target_pairs={{0,1},{1,0},{2,3},{3,2},{4,5},{5,4},{6,7},{7,6},{8,9},{9,8},{10,11... | collective-permute-start | bytes 786440 | tf_op jit(solution)/shard_map/ppermute | solution.py:251
  29.5 0.3 shard_map.88.projected_ref.here_ref
  29.8 0.3 shard_map.90.there_ref
  30.1 0.4 shard_map.91
  30.5 0.9 %collective-permute-start.10 = (bf16[192,256]{1,0:T(8,128)(2,1)S(1)}, bf16[192,256]{1,0:T(8,128)(2,1)S(1)}, u32[]{:S(2)}, u32[]{:S(2)}) collective-permute-start(bf16[192,256]{1,0:T(8,128)(2,1)S(1)} %get-tuple-element.35), channel_id=1, source_target_pairs={{0,4},{1,5},{2,6},{3,7},{4,0},{5,1},{6,2},{7,3},{8,12},{9,13},{10,... | collective-permute-start | bytes 294920 | tf_op jit(solution)/shard_map/ppermute | solution.py:251
  31.5 3.9 %collective-permute-done.10.refs_5_ = bf16[192,256]{1,0:T(8,128)(2,1)S(1)} collective-permute-done((bf16[192,256]{1,0:T(8,128)(2,1)S(1)}, bf16[192,256]{1,0:T(8,128)(2,1)S(1)}, u32[]{:S(2)}, u32[]{:S(2)}) %collective-permute-start.10) | collective-permute-done | bytes 98336 | tf_op jit(solution)/shard_map/ppermute | solution.py:251
  35.4 1.8 %collective-permute-start.11 = (bf16[64,256]{1,0:T(8,128)(2,1)S(1)}, bf16[64,256]{1,0:T(8,128)(2,1)S(1)}, u32[]{:S(2)}, u32[]{:S(2)}) collective-permute-start(bf16[64,256]{1,0:T(8,128)(2,1)S(1)} %get-tuple-element.36), channel_id=1, source_target_pairs={{0,6},{1,7},{2,4},{3,5},{4,2},{5,3},{6,0},{7,1},{8,14},{9,15},{10,... | collective-permute-start | bytes 98312 | tf_op jit(solution)/shard_map/ppermute | solution.py:251
  37.2 0.5 %collective-permute-start.9 = (bf16[64,256]{1,0:T(8,128)(2,1)S(1)}, bf16[64,256]{1,0:T(8,128)(2,1)S(1)}, u32[]{:S(2)}, u32[]{:S(2)}) collective-permute-start(bf16[64,256]{1,0:T(8,128)(2,1)S(1)} %get-tuple-element.34.refs_3_), channel_id=1, source_target_pairs={{0,2},{1,3},{2,0},{3,1},{4,6},{5,7},{6,4},{7,5},{8,10},{9,11},{10,... | collective-permute-start | bytes 98312 | tf_op jit(solution)/shard_map/ppermute | solution.py:251
  37.7 2.5 %collective-permute-done.11.refs_6_ = bf16[64,256]{1,0:T(8,128)(2,1)S(1)} collective-permute-done((bf16[64,256]{1,0:T(8,128)(2,1)S(1)}, bf16[64,256]{1,0:T(8,128)(2,1)S(1)}, u32[]{:S(2)}, u32[]{:S(2)}) %collective-permute-start.11) | collective-permute-done | bytes 32800 | tf_op jit(solution)/shard_map/ppermute | solution.py:251
  40.2 0.9 %collective-permute-done.9.refs_4_ = bf16[64,256]{1,0:T(8,128)(2,1)S(1)} collective-permute-done((bf16[64,256]{1,0:T(8,128)(2,1)S(1)}, bf16[64,256]{1,0:T(8,128)(2,1)S(1)}, u32[]{:S(2)}, u32[]{:S(2)}) %collective-permute-start.9) | collective-permute-done | bytes 32800 | tf_op jit(solution)/shard_map/ppermute | solution.py:251
  41.1 0.3 shard_map.89.refs_2_
  41.4 0.6 %shard_map.92.near_ref = bf16[1024,640]{1,0:T(8,128)(2,1)S(1)} custom-call(bf16[512,256]{1,0:T(8,128)(2,1)S(1)} %get-tuple-element.29.refs_0_, bf16[512,256]{1,0:T(8,128)(2,1)S(1)} %collective-permute-done.7.refs_1_, bf16[256,256]{1,0:T(8,128)(2,1)S(1)} %shard_map.89.refs_2_, bf16[64,256]{1,0:T(8,128)(2,1)S(1)} %get-tuple-element.34.refs_3_, ...), custom_call_target="tpu_custom_call" | custom-call | tf_op jit(solution)/shard_map/pallas_call | solution.py:60
  42.3 1.5 %shard_map.93 = bf16[1024,1024]{1,0:T(8,128)(2,1)} custom-call(bf16[1024,640]{1,0:T(8,128)(2,1)S(1)} %shard_map.92.near_ref, bf16[512,256]{1,0:T(8,128)(2,1)S(1)} %get-tuple-element.29.refs_0_, bf16[512,256]{1,0:T(8,128)(2,1)S(1)} %collective-permute-done.7.refs_1_, bf16[64,256]{1,0:T(8,128)(2,1)S(1)} %collective-permute-done.12.refs_2_, ...), custom_call_target="tpu_custom_call" | custom-call | tf_op jit(solution)/shard_map/pallas_call | solution.py:60
  (24 shorter events, 0.6 us)
Async XLA Ops:
  0.0 28.2 %copy-start.1 = (bf16[256,1024]{1,0:T(8,128)(2,1)S(1)}, bf16[256,1024]{1,0:T(8,128)(2,1)}, u32[]{:S(2)}) copy-start(bf16[256,1024]{1,0:T(8,128)(2,1)} %own_ref.1) | copy-start | bytes 1572868
  0.0 28.2 %collective-permute-start = (bf16[256,1024]{1,0:T(8,128)(2,1)}, bf16[256,1024]{1,0:T(8,128)(2,1)S(1)}, u32[]{:S(2)}, u32[]{:S(2)}) collective-permute-start(bf16[256,1024]{1,0:T(8,128)(2,1)} %own_ref.1), channel_id=1, source_target_pairs={{0,2},{1,3},{2,0},{3,1},{4,6},{5,7},{6,4},{7,5},{8,10},{9,11},{10,... | collective-permute-start | bytes 1572872 | tf_op jit(solution)/shard_map/ppermute | solution.py:251
  3.0 12.6 %collective-permute-start.1 = (bf16[8,1024]{1,0:T(8,128)(2,1)}, bf16[8,1024]{1,0:T(8,128)(2,1)S(1)}, u32[]{:S(2)}, u32[]{:S(2)}) collective-permute-start(bf16[8,1024]{1,0:T(8,128)(2,1)} %refs_1_.1), channel_id=1, source_target_pairs={{0,2},{1,3},{2,0},{3,1},{4,6},{5,7},{6,4},{7,5},{8,10},{9,11},{10,... | collective-permute-start | bytes 49160 | tf_op jit(solution)/shard_map/ppermute | solution.py:251
  15.5 4.1 %collective-permute-start.2 = (bf16[24,1024]{1,0:T(8,128)(2,1)S(1)}, bf16[24,1024]{1,0:T(8,128)(2,1)S(1)}, u32[]{:S(2)}, u32[]{:S(2)}) collective-permute-start(bf16[24,1024]{1,0:T(8,128)(2,1)S(1)} %shard_map.84.refs_0_), channel_id=1, source_target_pairs={{0,4},{1,5},{2,6},{3,7},{4,0},{5,1},{6,2},{7,3},{8,12},{9,13},{10,... | collective-permute-start | bytes 147464 | tf_op jit(solution)/shard_map/ppermute | solution.py:251
  19.6 6.9 %collective-permute-start.3 = (bf16[16,1024]{1,0:T(8,128)(2,1)S(1)}, bf16[16,1024]{1,0:T(8,128)(2,1)S(1)}, u32[]{:S(2)}, u32[]{:S(2)}) collective-permute-start(bf16[16,1024]{1,0:T(8,128)(2,1)S(1)} %shard_map.85.refs_0_), channel_id=1, source_target_pairs={{0,8},{1,9},{2,10},{3,11},{4,12},{5,13},{6,14},{7,15},{8,0},{9,1},... | collective-permute-start | bytes 98312 | tf_op jit(solution)/shard_map/ppermute | solution.py:251
  22.4 7.7 %collective-permute-start.8 = (bf16[64,1024]{1,0:T(8,128)(2,1)S(1)}, bf16[64,1024]{1,0:T(8,128)(2,1)S(1)}, u32[]{:S(2)}, u32[]{:S(2)}) collective-permute-start(bf16[64,1024]{1,0:T(8,128)(2,1)S(1)} %get-tuple-element.33), channel_id=1, source_target_pairs={{0,8},{1,9},{2,10},{3,11},{4,12},{5,13},{6,14},{7,15},{8,0},{9,1},... | collective-permute-start | bytes 393224 | tf_op jit(solution)/shard_map/ppermute | solution.py:251
  22.5 5.1 %collective-permute-start.4 = (bf16[24,1024]{1,0:T(8,128)(2,1)S(1)}, bf16[24,1024]{1,0:T(8,128)(2,1)S(1)}, u32[]{:S(2)}, u32[]{:S(2)}) collective-permute-start(bf16[24,1024]{1,0:T(8,128)(2,1)S(1)} %shard_map.84.refs_0_), channel_id=1, source_target_pairs={{0,1},{1,0},{2,3},{3,2},{4,5},{5,4},{6,7},{7,6},{8,9},{9,8},{10,11... | collective-permute-start | bytes 147464 | tf_op jit(solution)/shard_map/ppermute | solution.py:251
  22.6 5.1 %collective-permute-start.5 = (bf16[24,1024]{1,0:T(8,128)(2,1)S(1)}, bf16[24,1024]{1,0:T(8,128)(2,1)S(1)}, u32[]{:S(2)}, u32[]{:S(2)}) collective-permute-start(bf16[24,1024]{1,0:T(8,128)(2,1)S(1)} %collective-permute-done.2.refs_1_.refs_0_), channel_id=1, source_target_pairs={{0,1},{1,0},{2,3},{3,2},{4,5},{5,4},{6,7},{7,6},{8,9},{9,8},{10,11... | collective-permute-start | bytes 147464 | tf_op jit(solution)/shard_map/ppermute | solution.py:251
  26.5 1.2 %collective-permute-start.6 = (bf16[16,1024]{1,0:T(8,128)(2,1)S(1)}, bf16[16,1024]{1,0:T(8,128)(2,1)S(1)}, u32[]{:S(2)}, u32[]{:S(2)}) collective-permute-start(bf16[16,1024]{1,0:T(8,128)(2,1)S(1)} %collective-permute-done.3.refs_1_), channel_id=1, source_target_pairs={{0,1},{1,0},{2,3},{3,2},{4,5},{5,4},{6,7},{7,6},{8,9},{9,8},{10,11... | collective-permute-start | bytes 98312 | tf_op jit(solution)/shard_map/ppermute | solution.py:251
  28.2 1.9 %copy-start = (bf16[256,1024]{1,0:T(8,128)(2,1)S(1)}, bf16[256,1024]{1,0:T(8,128)(2,1)}, u32[]{:S(2)}) copy-start(bf16[256,1024]{1,0:T(8,128)(2,1)} %layer_ref.3) | copy-start | bytes 1572868
  29.0 12.5 %collective-permute-start.7 = (bf16[512,256]{1,0:T(8,128)(2,1)S(1)}, bf16[512,256]{1,0:T(8,128)(2,1)S(1)}, u32[]{:S(2)}, u32[]{:S(2)}) collective-permute-start(bf16[512,256]{1,0:T(8,128)(2,1)S(1)} %get-tuple-element.30), channel_id=1, source_target_pairs={{0,1},{1,0},{2,3},{3,2},{4,5},{5,4},{6,7},{7,6},{8,9},{9,8},{10,11... | collective-permute-start | bytes 786440 | tf_op jit(solution)/shard_map/ppermute | solution.py:251
  30.5 4.9 %collective-permute-start.10 = (bf16[192,256]{1,0:T(8,128)(2,1)S(1)}, bf16[192,256]{1,0:T(8,128)(2,1)S(1)}, u32[]{:S(2)}, u32[]{:S(2)}) collective-permute-start(bf16[192,256]{1,0:T(8,128)(2,1)S(1)} %get-tuple-element.35), channel_id=1, source_target_pairs={{0,4},{1,5},{2,6},{3,7},{4,0},{5,1},{6,2},{7,3},{8,12},{9,13},{10,... | collective-permute-start | bytes 294920 | tf_op jit(solution)/shard_map/ppermute | solution.py:251
  35.4 6.9 %collective-permute-start.14 = (bf16[192,256]{1,0:T(8,128)(2,1)S(1)}, bf16[192,256]{1,0:T(8,128)(2,1)S(1)}, u32[]{:S(2)}, u32[]{:S(2)}) collective-permute-start(bf16[192,256]{1,0:T(8,128)(2,1)S(1)} %collective-permute-done.10.refs_5_), channel_id=1, source_target_pairs={{0,1},{1,0},{2,3},{3,2},{4,5},{5,4},{6,7},{7,6},{8,9},{9,8},{10,11... | collective-permute-start | bytes 294920 | tf_op jit(solution)/shard_map/ppermute | solution.py:251
  35.4 4.8 %collective-permute-start.11 = (bf16[64,256]{1,0:T(8,128)(2,1)S(1)}, bf16[64,256]{1,0:T(8,128)(2,1)S(1)}, u32[]{:S(2)}, u32[]{:S(2)}) collective-permute-start(bf16[64,256]{1,0:T(8,128)(2,1)S(1)} %get-tuple-element.36), channel_id=1, source_target_pairs={{0,6},{1,7},{2,4},{3,5},{4,2},{5,3},{6,0},{7,1},{8,14},{9,15},{10,... | collective-permute-start | bytes 98312 | tf_op jit(solution)/shard_map/ppermute | solution.py:251
  37.2 3.9 %collective-permute-start.9 = (bf16[64,256]{1,0:T(8,128)(2,1)S(1)}, bf16[64,256]{1,0:T(8,128)(2,1)S(1)}, u32[]{:S(2)}, u32[]{:S(2)}) collective-permute-start(bf16[64,256]{1,0:T(8,128)(2,1)S(1)} %get-tuple-element.34.refs_3_), channel_id=1, source_target_pairs={{0,2},{1,3},{2,0},{3,1},{4,6},{5,7},{6,4},{7,5},{8,10},{9,11},{10,... | collective-permute-start | bytes 98312 | tf_op jit(solution)/shard_map/ppermute | solution.py:251
  37.7 4.3 %collective-permute-start.12 = (bf16[64,256]{1,0:T(8,128)(2,1)S(1)}, bf16[64,256]{1,0:T(8,128)(2,1)S(1)}, u32[]{:S(2)}, u32[]{:S(2)}) collective-permute-start(bf16[64,256]{1,0:T(8,128)(2,1)S(1)} %get-tuple-element.34.refs_3_), channel_id=1, source_target_pairs={{0,1},{1,0},{2,3},{3,2},{4,5},{5,4},{6,7},{7,6},{8,9},{9,8},{10,11... | collective-permute-start | bytes 98312 | tf_op jit(solution)/shard_map/ppermute | solution.py:251
  40.2 1.9 %collective-permute-start.15 = (bf16[64,256]{1,0:T(8,128)(2,1)S(1)}, bf16[64,256]{1,0:T(8,128)(2,1)S(1)}, u32[]{:S(2)}, u32[]{:S(2)}) collective-permute-start(bf16[64,256]{1,0:T(8,128)(2,1)S(1)} %collective-permute-done.11.refs_6_), channel_id=1, source_target_pairs={{0,1},{1,0},{2,3},{3,2},{4,5},{5,4},{6,7},{7,6},{8,9},{9,8},{10,11... | collective-permute-start | bytes 98312 | tf_op jit(solution)/shard_map/ppermute | solution.py:251
  41.1 1.2 %collective-permute-start.13 = (bf16[64,256]{1,0:T(8,128)(2,1)S(1)}, bf16[64,256]{1,0:T(8,128)(2,1)S(1)}, u32[]{:S(2)}, u32[]{:S(2)}) collective-permute-start(bf16[64,256]{1,0:T(8,128)(2,1)S(1)} %collective-permute-done.9.refs_4_), channel_id=1, source_target_pairs={{0,1},{1,0},{2,3},{3,2},{4,5},{5,4},{6,7},{7,6},{8,9},{9,8},{10,11... | collective-permute-start | bytes 98312 | tf_op jit(solution)/shard_map/ppermute | solution.py:251

commit v6 on v5

--- a/solution.py
+++ b/solution.py
@@ -144,20 +144,27 @@
     ).astype(jnp.bfloat16)
 
 
-def right_far_kernel(layer_ref, far_ref, here_ref, there_ref, mine_ref, near_ref, cross_ref):
-    share, _ = mine_ref.shape
+def right_far_kernel(layer_ref, far_ref, here_ref, there_ref, both_ref, near_ref):
+    share = far_ref.shape[0]
     half = near_ref.shape[0] - share
     start = pl.multiple_of(lax.axis_index("tile") * half, half)
     far = far_ref[...]
-    mine_ref[...] = jnp.dot(
+    both_ref[pl.ds(0, share), :] = jnp.dot(
         far, here_ref[...], preferred_element_type=jnp.float32
     ).astype(jnp.bfloat16)
     cross = jnp.dot(far, there_ref[...], preferred_element_type=jnp.float32).astype(jnp.bfloat16)
-    cross_ref[...] = cross
+    both_ref[pl.ds(share, share), :] = cross
     near_ref[pl.ds(half, share), :] = cross
     near_ref[pl.ds(0, half), :] = jnp.dot(
         layer_ref[pl.ds(start, half), :], there_ref[...], preferred_element_type=jnp.float32
     ).astype(jnp.bfloat16)
+
+
+def mix_kernel(both_ref, both_t_ref, out_ref):
+    share = out_ref.shape[0] // 2
+    first = pl.multiple_of(lax.axis_index("tile") * share, share)
+    out_ref[pl.ds(0, share), :] = both_ref[pl.ds(first, share), :]
+    out_ref[pl.ds(share, share), :] = both_t_ref[pl.ds(first, share), :]
 
 
 def left_kernel(own_ref, x_ref, projected_ref, mine_ref, other_ref):
@@ -170,18 +177,6 @@
         other_ref[pl.ds(k * rows, rows), :] = states[:, paths:]
 
 
-def join_right(right_ref, at, mine_ref, x_ref, z_ref, xz_ref):
-    half, share = lax.axis_index("half"), mine_ref.shape[0]
-    side = z_ref.shape[0] - share
-    right_ref[pl.ds(at, side), :] = z_ref[pl.ds(0, side), :]
-    for plane, near_ref, first, far_ref in ((2, mine_ref, 0, x_ref), (3, z_ref, side, xz_ref)):
-        base = at + (plane - 1) * side
-        right_ref[pl.ds(pl.multiple_of(base + half * share, share), share), :] = near_ref[
-            pl.ds(first, share), :
-        ]
-        right_ref[pl.ds(pl.multiple_of(base + (half ^ 1) * share, share), share), :] = far_ref[...]
-
-
 def left_blocks(left_refs):
     for tile, ref in enumerate(left_refs):
         rows = ref.shape[0] // 2
@@ -192,10 +187,11 @@
 
 
 def amplitude_near_kernel(left_count, *refs):
-    left_refs, right_refs, (out_ref, right_ref) = refs[:left_count], refs[left_count:-2], refs[-2:]
-    chunk = right_refs[0].shape[0]
-    right_ref[pl.ds(0, chunk), :] = right_refs[0][...]
-    join_right(right_ref, chunk, *right_refs[1:])
+    left_refs, (own_ref, z_ref, out_ref, right_ref) = refs[:left_count], refs[left_count:]
+    chunk = own_ref.shape[0]
+    side = right_ref.shape[0] - chunk
+    right_ref[pl.ds(0, chunk), :] = own_ref[...]
+    right_ref[pl.ds(chunk, side), :] = z_ref[pl.ds(0, side), :]
     right = right_ref[...]
     for left, rows, row in left_blocks(left_refs):
         out_ref[pl.ds(row, rows), :] = lax.dot_general(
@@ -206,9 +202,24 @@
 def amplitude_rest_kernel(left_count, near_ref, *refs):
     left_refs, right_refs = refs[:left_count], refs[left_count:-4]
     out_ref, right_ref, block_ref, sems = refs[-4:]
-    path, tile = lax.axis_index("path"), lax.axis_index("tile")
-    side = right_ref.shape[0] // 3
+    both_ref, mixed_ref, z_ref, both_t_ref, mixed_t_ref, z_t_ref = right_refs
+    path, half, tile = (lax.axis_index(axis) for axis in DEVICE_AXES)
+    share, halves = both_ref.shape[0] // 2, lax.axis_size("half")
+    side = z_ref.shape[0] - share
     chunk = side * lax.axis_size("tile")
+
+    def place(ref, first, far, core, column_half):
+        start = side + far * chunk + (core * halves + column_half) * share
+        right_ref[pl.ds(pl.multiple_of(start, share), share), :] = ref[pl.ds(first, share), :]
+
+    right_ref[pl.ds(0, side), :] = z_t_ref[pl.ds(0, side), :]
+    for core, near, mixed, z in (
+        (tile, both_ref, mixed_ref, z_ref), (tile ^ 1, both_t_ref, mixed_t_ref, z_t_ref)
+    ):
+        place(near, 0, 0, core, half)
+        place(z, side, 1, core, half)
+        place(mixed, 0, core, core, half ^ 1)
+        place(mixed, share, core, core ^ 1, half ^ 1)
     copies = []
 
     def send(source, row, rows, column, width):
@@ -219,18 +230,18 @@
 
     height = near_ref.shape[0]
     send(near_ref.at[:, pl.ds(0, chunk)], 0, height, path * chunk, chunk)
-    for plane in range(1, 4):
-        source = near_ref.at[:, pl.ds(chunk + (plane - 1) * side, side)]
-        send(source, 0, height, (path ^ plane) * chunk + tile * side, side)
-    join_right(right_ref, 0, *right_refs)
+    source = near_ref.at[:, pl.ds(chunk, side)]
+    send(source, 0, height, (path ^ 1) * chunk + tile * side, side)
     right = right_ref[...]
     for k, (left, rows, row) in enumerate(left_blocks(left_refs)):
         block_ref[k] = lax.dot_general(
             left, right, CONTRACT_LAST, preferred_element_type=jnp.float32
         ).astype(jnp.bfloat16)
-        for plane in range(1, 4):
-            source = block_ref.at[k, :, pl.ds((plane - 1) * side, side)]
-            send(source, row, rows, (path ^ plane) * chunk + (tile ^ 1) * side, side)
+        column = (path ^ 1) * chunk + (tile ^ 1) * side
+        send(block_ref.at[k, :, pl.ds(0, side)], row, rows, column, side)
+        for far in range(2):
+            source = block_ref.at[k, :, pl.ds(side + far * chunk, chunk)]
+            send(source, row, rows, (path ^ (2 + far)) * chunk, chunk)
     for copy in copies:
         copy.wait()
 
@@ -240,13 +251,14 @@
 ):
     sizes = [lax.axis_size(axis) for axis in DEVICE_AXES]
 
-    def exchange(value, plane=0, half=0, tile=0):
+    def exchange(value, plane=0, half=0, tile=0, tile_plane=0):
         pairs = []
         for p in range(sizes[0]):
             for h in range(sizes[1]):
                 for t in range(sizes[2]):
                     source = (p * sizes[1] + h) * sizes[2] + t
-                    target = ((p ^ plane) * sizes[1] + (h ^ half)) * sizes[2] + (t ^ tile)
+                    q = p ^ plane ^ (tile_plane * t)
+                    target = (q * sizes[1] + (h ^ half)) * sizes[2] + (t ^ tile)
                     pairs.append((source, target))
         return lax.ppermute(value, DEVICE_AXES, pairs)
 
@@ -300,15 +312,19 @@
         (((0, 0, depth), (1, 0, depth), (0, depth, depth), (1, depth, depth)),),
         right_factor, right_pick, near, near_t,
     )
-    mine, for_near, cross = call(
+    both, for_near = call(
         right_far_kernel,
-        [(share, paths), (chunk // sizes[2] + share, paths), (share, paths)],
+        [(2 * share, paths), (chunk // sizes[2] + share, paths)],
         right_layer, far, here, there,
     )
+    both_t = exchange(both, tile=1)
+    from_z = exchange(for_near, plane=1)
+    (mix,) = call(mix_kernel, [(2 * share, paths)], both, both_t)
+    mixed = exchange(mix, half=1, tile_plane=1)
     right_pieces = [
-        mine, exchange(mine, half=1), exchange(for_near, plane=1), exchange(cross, plane=1, half=1)
+        both, mixed, from_z,
+        both_t, exchange(mixed, tile=1), exchange(from_z, tile=1),
     ]
-    right_pieces_t = [exchange(piece, tile=1) for piece in right_pieces]
     left_projected = project(
         (
             ((0, 0, 2 * depth), (1, 0, 2 * depth)),
@@ -325,18 +341,18 @@
     height = spots * rows
     (amplitude,) = call(
         functools.partial(amplitude_near_kernel, len(left_states)),
-        [(height, chunk + 3 * side)],
-        *left_states, right_near, *right_pieces,
-        scratch=(pltpu.VMEM((chunk + 3 * side, paths), jnp.bfloat16),),
+        [(height, chunk + side)],
+        *left_states, right_near, from_z,
+        scratch=(pltpu.VMEM((chunk + side, paths), jnp.bfloat16),),
     )
     return call(
         functools.partial(amplitude_rest_kernel, len(left_states)),
         [(height, sizes[0] * chunk)],
-        amplitude, *left_states, *right_pieces_t,
+        amplitude, *left_states, *right_pieces,
         scratch=(
-            pltpu.VMEM((3 * side, paths), jnp.bfloat16),
-            pltpu.VMEM((spots, rows, 3 * side), jnp.bfloat16),
-            pltpu.SemaphoreType.DMA((4 + 3 * spots,)),
+            pltpu.VMEM((2 * chunk + side, paths), jnp.bfloat16),
+            pltpu.VMEM((spots, rows, 2 * chunk + side), jnp.bfloat16),
+            pltpu.SemaphoreType.DMA((2 + 3 * spots,)),
         ),
         out_space=pltpu.HBM,
     )[0]

time: 43.9 us -> 40 us (0.911)
  waiting for transfers between devices: 24.9 us -> 20.5 us
  starting transfers between devices: 12 us -> 12.7 us
    ppermute x16 -> x14, waiting for transfers between devices: 24.9 us -> 20.5 us  [exchange(): return lax.ppermute(value, DEVICE_AXES, pairs)]
    ppermute x16 -> x14, starting transfers between devices: 12 us -> 12.7 us  [exchange(): return lax.ppermute(value, DEVICE_AXES, pairs)]
    pallas_call x12 -> x13, Pallas kernels: 6.66 us -> 6.55 us  [call(): pl.pallas_call(kernel, out_shape=shapes, in_specs=[pl.BlockSpec(memory_sp...]
  transfers between devices with their start and end apart: 16 -> 14, of which waited for: 8 -> 8; matrix products, arithmetic and copies ran while one was open for 0% -> 0% of each run, Pallas kernels for 12% -> 13%
where the time goes in v6:
time: 40 us; the launch traced here: 39.9 us
  waiting for transfers between devices  20.5 us (51%)
  starting transfers between devices  12.7 us (32%)
  Pallas kernels  6.55 us (16%)
    ppermute x14, waiting for transfers between devices, exchange(): return lax.ppermute(value, DEVICE_AXES, pairs)  20.5 us
    ppermute x14, starting transfers between devices, exchange(): return lax.ppermute(value, DEVICE_AXES, pairs)  12.7 us
    pallas_call x13, Pallas kernels, call(): pl.pallas_call(kernel, out_shape=shapes, in_specs=[pl.BlockSpec(memory_sp...  6.55 us
  transfers between devices with their start and end apart: 14, of which 8 were waited for; matrix products, arithmetic and copies ran while one was open for 0% of the time, Pallas kernels for 13%

profile of v6, /device:TPU:0, one launch (start us, length us, event | category | flops | bytes accessed | tf_op | source)
XLA Modules:
  0.0 39.9 jit_solution(8980489381504821068)
XLA Ops:
  0.0 3.0 %collective-permute-start = (bf16[256,1024]{1,0:T(8,128)(2,1)}, bf16[256,1024]{1,0:T(8,128)(2,1)S(1)}, u32[]{:S(2)}, u32[]{:S(2)}) collective-permute-start(bf16[256,1024]{1,0:T(8,128)(2,1)} %own_ref.1), channel_id=1, source_target_pairs={{0,2},{1,3},{2,0},{3,1},{4,6},{5,7},{6,4},{7,5},{8,10},{9,11},{10,... | collective-permute-start | bytes 1572872 | tf_op jit(solution)/shard_map/ppermute | solution.py:263
  3.0 1.0 %shard_map.82 = (bf16[64,1024]{1,0:T(8,128)(2,1)S(1)}, bf16[8,1024]{1,0:T(8,128)(2,1)S(1)}, bf16[8,1024]{1,0:T(8,128)(2,1)S(1)}, s32[1,10]{1,0:T(1,128)S(1)}, s3...) custom-call(bf16[256,1024]{1,0:T(8,128)(2,1)} %layer_ref.3, bf16[8,1024]{1,0:T(8,128)(2,1)} %refs_1_.1, ...), custom_call_target="tpu_custom_call" | custom-call | tf_op jit(solution)/shard_map/pallas_call | solution.py:60
  4.0 11.5 %collective-permute-done.1.refs_1_ = bf16[8,1024]{1,0:T(8,128)(2,1)S(1)} collective-permute-done((bf16[8,1024]{1,0:T(8,128)(2,1)}, bf16[8,1024]{1,0:T(8,128)(2,1)S(1)}, u32[]{:S(2)}, u32[]{:S(2)}) %collective-permute-start.1) | collective-permute-done | bytes 16416 | tf_op jit(solution)/shard_map/ppermute | solution.py:263
  15.5 1.8 %collective-permute-start.2 = (bf16[24,1024]{1,0:T(8,128)(2,1)S(1)}, bf16[24,1024]{1,0:T(8,128)(2,1)S(1)}, u32[]{:S(2)}, u32[]{:S(2)}) collective-permute-start(bf16[24,1024]{1,0:T(8,128)(2,1)S(1)} %shard_map.84.refs_0_), channel_id=1, source_target_pairs={{0,4},{1,5},{2,6},{3,7},{4,0},{5,1},{6,2},{7,3},{8,12},{9,13},{10,... | collective-permute-start | bytes 147464 | tf_op jit(solution)/shard_map/ppermute | solution.py:263
  17.3 2.3 %collective-permute-done.2.refs_1_.refs_0_ = bf16[24,1024]{1,0:T(8,128)(2,1)S(1)} collective-permute-done((bf16[24,1024]{1,0:T(8,128)(2,1)S(1)}, bf16[24,1024]{1,0:T(8,128)(2,1)S(1)}, u32[]{:S(2)}, u32[]{:S(2)}) %collective-permute-start.2) | collective-permute-done | bytes 49184 | tf_op jit(solution)/shard_map/ppermute | solution.py:263
  19.6 2.8 %collective-permute-start.3 = (bf16[16,1024]{1,0:T(8,128)(2,1)S(1)}, bf16[16,1024]{1,0:T(8,128)(2,1)S(1)}, u32[]{:S(2)}, u32[]{:S(2)}) collective-permute-start(bf16[16,1024]{1,0:T(8,128)(2,1)S(1)} %shard_map.85.refs_0_), channel_id=1, source_target_pairs={{0,8},{1,9},{2,10},{3,11},{4,12},{5,13},{6,14},{7,15},{8,0},{9,1},... | collective-permute-start | bytes 98312 | tf_op jit(solution)/shard_map/ppermute | solution.py:263
  22.6 0.5 %collective-permute-start.5 = (bf16[24,1024]{1,0:T(8,128)(2,1)S(1)}, bf16[24,1024]{1,0:T(8,128)(2,1)S(1)}, u32[]{:S(2)}, u32[]{:S(2)}) collective-permute-start(bf16[24,1024]{1,0:T(8,128)(2,1)S(1)} %collective-permute-done.2.refs_1_.refs_0_), channel_id=1, source_target_pairs={{0,1},{1,0},{2,3},{3,2},{4,5},{5,4},{6,7},{7,6},{8,9},{9,8},{10,11... | collective-permute-start | bytes 147464 | tf_op jit(solution)/shard_map/ppermute | solution.py:263
  23.1 3.5 %collective-permute-done.3.refs_1_ = bf16[16,1024]{1,0:T(8,128)(2,1)S(1)} collective-permute-done((bf16[16,1024]{1,0:T(8,128)(2,1)S(1)}, bf16[16,1024]{1,0:T(8,128)(2,1)S(1)}, u32[]{:S(2)}, u32[]{:S(2)}) %collective-permute-start.3) | collective-permute-done | bytes 32800 | tf_op jit(solution)/shard_map/ppermute | solution.py:263
  26.5 1.1 %shard_map.83 = (bf16[1024,256]{1,0:T(8,128)(2,1)S(1)}, bf16[32,256]{1,0:T(8,128)(2,1)S(1)}, bf16[1024,256]{1,0:T(8,128)(2,1)S(1)}, bf16[32,256]{1,0:T(8,128)(2,1)S(1)}) custom-call(s32[1,10]{1,0:T(1,128)S(1)} %get-tuple-element.20.side_ref, s32[10,256]{1,0:T(8,128)S(1)} %get-tuple-element.21.branch_ref, s32[1,256]{1,0:T(1,128)S(1)} %get-tuple-element.22.left_map_ref, ...), custom_call_target="tpu_custom_call" | custom-call | tf_op jit(solution)/shard_map/pallas_call | solution.py:60
  27.7 0.5 %shard_map.86.projected_ref = bf16[1024,512]{1,0:T(8,128)(2,1)S(1)} custom-call(bf16[1024,256]{1,0:T(8,128)(2,1)S(1)} %get-tuple-element.24.factor_ref, bf16[32,256]{1,0:T(8,128)(2,1)S(1)} %get-tuple-element.25.pick_ref, bf16[16,1024]{1,0:T(8,128)(2,1)S(1)} %shard_map.85.refs_0_, bf16[16,1024]{1,0:T(8,128)(2,1)S(1)} %collective-permute-done.3.refs_1_, ...), custom_call_target="tpu_custom_call" | custom-call | tf_op jit(solution)/shard_map/pallas_call | solution.py:60
  28.3 0.7 %shard_map.87 = (bf16[512,256]{1,0:T(8,128)(2,1)S(1)}, bf16[512,256]{1,0:T(8,128)(2,1)S(1)}) custom-call(bf16[256,1024]{1,0:T(8,128)(2,1)S(1)} %copy-done.1, bf16[256,1024]{1,0:T(8,128)(2,1)S(1)} %collective-permute-done.x_ref, bf16[1024,512]{1,0:T(8,128)(2,1)S(1)} %shard_map.86.projected_ref), custom_call_target="tpu_custom_call" | custom-call | tf_op jit(solution)/shard_map/pallas_call | solution.py:60
  29.0 0.5 %collective-permute-start.7 = (bf16[512,256]{1,0:T(8,128)(2,1)S(1)}, bf16[512,256]{1,0:T(8,128)(2,1)S(1)}, u32[]{:S(2)}, u32[]{:S(2)}) collective-permute-start(bf16[512,256]{1,0:T(8,128)(2,1)S(1)} %get-tuple-element.29), channel_id=1, source_target_pairs={{0,1},{1,0},{2,3},{3,2},{4,5},{5,4},{6,7},{7,6},{8,9},{9,8},{10,11... | collective-permute-start | bytes 786440 | tf_op jit(solution)/shard_map/ppermute | solution.py:263
  29.5 0.3 shard_map.88.projected_ref.here_ref
  29.8 0.3 shard_map.90.there_ref
  30.1 0.4 %shard_map.91 = (bf16[128,256]{1,0:T(8,128)(2,1)S(1)}, bf16[192,256]{1,0:T(8,128)(2,1)S(1)}) custom-call(bf16[256,1024]{1,0:T(8,128)(2,1)S(1)} %copy-done, bf16[64,1024]{1,0:T(8,128)(2,1)S(1)} %collective-permute-done.8.far_ref, bf16[1024,256]{1,0:T(8,128)(2,1)S(1)} %shard_map.88.projected_ref.here_ref, bf16[1024,256]{1,0:T(8,128)(2,1)S(1)} %shard_map.90.there_ref), custom_call_target="tpu_custom_call" | custom-call | tf_op jit(solution)/shard_map/pallas_call | solution.py:60
  30.7 0.9 %collective-permute-start.9 = (bf16[192,256]{1,0:T(8,128)(2,1)S(1)}, bf16[192,256]{1,0:T(8,128)(2,1)S(1)}, u32[]{:S(2)}, u32[]{:S(2)}) collective-permute-start(bf16[192,256]{1,0:T(8,128)(2,1)S(1)} %get-tuple-element.33), channel_id=1, source_target_pairs={{0,4},{1,5},{2,6},{3,7},{4,0},{5,1},{6,2},{7,3},{8,12},{9,13},{10,... | collective-permute-start | bytes 294920 | tf_op jit(solution)/shard_map/ppermute | solution.py:263
  31.6 0.3 collective-permute-done.10.both_t_ref.refs_5_
  31.9 1.7 %collective-permute-start.11 = (bf16[128,256]{1,0:T(8,128)(2,1)S(1)}, bf16[128,256]{1,0:T(8,128)(2,1)S(1)}, u32[]{:S(2)}, u32[]{:S(2)}) collective-permute-start(bf16[128,256]{1,0:T(8,128)(2,1)S(1)} %shard_map.93), channel_id=1, source_target_pairs={{0,2},{1,7},{2,0},{3,5},{4,6},{5,3},{6,4},{7,1},{8,10},{9,15},{10,... | collective-permute-start | bytes 196616 | tf_op jit(solution)/shard_map/ppermute | solution.py:263
  33.5 2.4 %collective-permute-done.9.refs_3_.refs_4_ = bf16[192,256]{1,0:T(8,128)(2,1)S(1)} collective-permute-done((bf16[192,256]{1,0:T(8,128)(2,1)S(1)}, bf16[192,256]{1,0:T(8,128)(2,1)S(1)}, u32[]{:S(2)}, u32[]{:S(2)}) %collective-permute-start.9) | collective-permute-done | bytes 98336 | tf_op jit(solution)/shard_map/ppermute | solution.py:263
  35.9 0.2 collective-permute-done.11.refs_3_
  36.1 1.3 %collective-permute-start.12 = (bf16[128,256]{1,0:T(8,128)(2,1)S(1)}, bf16[128,256]{1,0:T(8,128)(2,1)S(1)}, u32[]{:S(2)}, u32[]{:S(2)}) collective-permute-start(bf16[128,256]{1,0:T(8,128)(2,1)S(1)} %collective-permute-done.11.refs_3_), channel_id=1, source_target_pairs={{0,1},{1,0},{2,3},{3,2},{4,5},{5,4},{6,7},{7,6},{8,9},{9,8},{10,11... | collective-permute-start | bytes 196616 | tf_op jit(solution)/shard_map/ppermute | solution.py:263
  37.4 0.3 shard_map.89.refs_2_
  37.8 0.4 %shard_map.92.near_ref = bf16[1024,384]{1,0:T(8,128)(2,1)S(1)} custom-call(bf16[512,256]{1,0:T(8,128)(2,1)S(1)} %get-tuple-element.28.refs_0_, bf16[512,256]{1,0:T(8,128)(2,1)S(1)} %collective-permute-done.7.refs_1_, bf16[256,256]{1,0:T(8,128)(2,1)S(1)} %shard_map.89.refs_2_, bf16[192,256]{1,0:T(8,128)(2,1)S(1)} %collective-permute-done.9.refs_3_.refs_4_), custom_call_target="tpu_custom_call" | custom-call | tf_op jit(solution)/shard_map/pallas_call | solution.py:60
  38.3 1.5 %shard_map.94 = bf16[1024,1024]{1,0:T(8,128)(2,1)} custom-call(bf16[1024,384]{1,0:T(8,128)(2,1)S(1)} %shard_map.92.near_ref, bf16[512,256]{1,0:T(8,128)(2,1)S(1)} %get-tuple-element.28.refs_0_, bf16[512,256]{1,0:T(8,128)(2,1)S(1)} %collective-permute-done.7.refs_1_, bf16[128,256]{1,0:T(8,128)(2,1)S(1)} %get-tuple-element.34.both_ref.refs_2_, ...), custom_call_target="tpu_custom_call" | custom-call | tf_op jit(solution)/shard_map/pallas_call | solution.py:60
  (21 shorter events, 0.7 us)
Async XLA Ops:
  0.0 28.3 %copy-start.1 = (bf16[256,1024]{1,0:T(8,128)(2,1)S(1)}, bf16[256,1024]{1,0:T(8,128)(2,1)}, u32[]{:S(2)}) copy-start(bf16[256,1024]{1,0:T(8,128)(2,1)} %own_ref.1) | copy-start | bytes 1572868
  0.0 28.2 %collective-permute-start = (bf16[256,1024]{1,0:T(8,128)(2,1)}, bf16[256,1024]{1,0:T(8,128)(2,1)S(1)}, u32[]{:S(2)}, u32[]{:S(2)}) collective-permute-start(bf16[256,1024]{1,0:T(8,128)(2,1)} %own_ref.1), channel_id=1, source_target_pairs={{0,2},{1,3},{2,0},{3,1},{4,6},{5,7},{6,4},{7,5},{8,10},{9,11},{10,... | collective-permute-start | bytes 1572872 | tf_op jit(solution)/shard_map/ppermute | solution.py:263
  3.0 12.6 %collective-permute-start.1 = (bf16[8,1024]{1,0:T(8,128)(2,1)}, bf16[8,1024]{1,0:T(8,128)(2,1)S(1)}, u32[]{:S(2)}, u32[]{:S(2)}) collective-permute-start(bf16[8,1024]{1,0:T(8,128)(2,1)} %refs_1_.1), channel_id=1, source_target_pairs={{0,2},{1,3},{2,0},{3,1},{4,6},{5,7},{6,4},{7,5},{8,10},{9,11},{10,... | collective-permute-start | bytes 49160 | tf_op jit(solution)/shard_map/ppermute | solution.py:263
  15.5 4.1 %collective-permute-start.2 = (bf16[24,1024]{1,0:T(8,128)(2,1)S(1)}, bf16[24,1024]{1,0:T(8,128)(2,1)S(1)}, u32[]{:S(2)}, u32[]{:S(2)}) collective-permute-start(bf16[24,1024]{1,0:T(8,128)(2,1)S(1)} %shard_map.84.refs_0_), channel_id=1, source_target_pairs={{0,4},{1,5},{2,6},{3,7},{4,0},{5,1},{6,2},{7,3},{8,12},{9,13},{10,... | collective-permute-start | bytes 147464 | tf_op jit(solution)/shard_map/ppermute | solution.py:263
  19.6 6.9 %collective-permute-start.3 = (bf16[16,1024]{1,0:T(8,128)(2,1)S(1)}, bf16[16,1024]{1,0:T(8,128)(2,1)S(1)}, u32[]{:S(2)}, u32[]{:S(2)}) collective-permute-start(bf16[16,1024]{1,0:T(8,128)(2,1)S(1)} %shard_map.85.refs_0_), channel_id=1, source_target_pairs={{0,8},{1,9},{2,10},{3,11},{4,12},{5,13},{6,14},{7,15},{8,0},{9,1},... | collective-permute-start | bytes 98312 | tf_op jit(solution)/shard_map/ppermute | solution.py:263
  22.4 7.7 %collective-permute-start.8 = (bf16[64,1024]{1,0:T(8,128)(2,1)S(1)}, bf16[64,1024]{1,0:T(8,128)(2,1)S(1)}, u32[]{:S(2)}, u32[]{:S(2)}) collective-permute-start(bf16[64,1024]{1,0:T(8,128)(2,1)S(1)} %get-tuple-element.32), channel_id=1, source_target_pairs={{0,8},{1,9},{2,10},{3,11},{4,12},{5,13},{6,14},{7,15},{8,0},{9,1},... | collective-permute-start | bytes 393224 | tf_op jit(solution)/shard_map/ppermute | solution.py:263
  22.5 5.1 %collective-permute-start.4 = (bf16[24,1024]{1,0:T(8,128)(2,1)S(1)}, bf16[24,1024]{1,0:T(8,128)(2,1)S(1)}, u32[]{:S(2)}, u32[]{:S(2)}) collective-permute-start(bf16[24,1024]{1,0:T(8,128)(2,1)S(1)} %shard_map.84.refs_0_), channel_id=1, source_target_pairs={{0,1},{1,0},{2,3},{3,2},{4,5},{5,4},{6,7},{7,6},{8,9},{9,8},{10,11... | collective-permute-start | bytes 147464 | tf_op jit(solution)/shard_map/ppermute | solution.py:263
  22.6 5.1 %collective-permute-start.5 = (bf16[24,1024]{1,0:T(8,128)(2,1)S(1)}, bf16[24,1024]{1,0:T(8,128)(2,1)S(1)}, u32[]{:S(2)}, u32[]{:S(2)}) collective-permute-start(bf16[24,1024]{1,0:T(8,128)(2,1)S(1)} %collective-permute-done.2.refs_1_.refs_0_), channel_id=1, source_target_pairs={{0,1},{1,0},{2,3},{3,2},{4,5},{5,4},{6,7},{7,6},{8,9},{9,8},{10,11... | collective-permute-start | bytes 147464 | tf_op jit(solution)/shard_map/ppermute | solution.py:263
  26.5 1.2 %collective-permute-start.6 = (bf16[16,1024]{1,0:T(8,128)(2,1)S(1)}, bf16[16,1024]{1,0:T(8,128)(2,1)S(1)}, u32[]{:S(2)}, u32[]{:S(2)}) collective-permute-start(bf16[16,1024]{1,0:T(8,128)(2,1)S(1)} %collective-permute-done.3.refs_1_), channel_id=1, source_target_pairs={{0,1},{1,0},{2,3},{3,2},{4,5},{5,4},{6,7},{7,6},{8,9},{9,8},{10,11... | collective-permute-start | bytes 98312 | tf_op jit(solution)/shard_map/ppermute | solution.py:263
  28.2 1.9 %copy-start = (bf16[256,1024]{1,0:T(8,128)(2,1)S(1)}, bf16[256,1024]{1,0:T(8,128)(2,1)}, u32[]{:S(2)}) copy-start(bf16[256,1024]{1,0:T(8,128)(2,1)} %layer_ref.3) | copy-start | bytes 1572868
  29.0 8.8 %collective-permute-start.7 = (bf16[512,256]{1,0:T(8,128)(2,1)S(1)}, bf16[512,256]{1,0:T(8,128)(2,1)S(1)}, u32[]{:S(2)}, u32[]{:S(2)}) collective-permute-start(bf16[512,256]{1,0:T(8,128)(2,1)S(1)} %get-tuple-element.29), channel_id=1, source_target_pairs={{0,1},{1,0},{2,3},{3,2},{4,5},{5,4},{6,7},{7,6},{8,9},{9,8},{10,11... | collective-permute-start | bytes 786440 | tf_op jit(solution)/shard_map/ppermute | solution.py:263
  30.5 1.3 %collective-permute-start.10 = (bf16[128,256]{1,0:T(8,128)(2,1)S(1)}, bf16[128,256]{1,0:T(8,128)(2,1)S(1)}, u32[]{:S(2)}, u32[]{:S(2)}) collective-permute-start(bf16[128,256]{1,0:T(8,128)(2,1)S(1)} %get-tuple-element.34.both_ref.refs_2_), channel_id=1, source_target_pairs={{0,1},{1,0},{2,3},{3,2},{4,5},{5,4},{6,7},{7,6},{8,9},{9,8},{10,11... | collective-permute-start | bytes 196616 | tf_op jit(solution)/shard_map/ppermute | solution.py:263
  30.7 5.2 %collective-permute-start.9 = (bf16[192,256]{1,0:T(8,128)(2,1)S(1)}, bf16[192,256]{1,0:T(8,128)(2,1)S(1)}, u32[]{:S(2)}, u32[]{:S(2)}) collective-permute-start(bf16[192,256]{1,0:T(8,128)(2,1)S(1)} %get-tuple-element.33), channel_id=1, source_target_pairs={{0,4},{1,5},{2,6},{3,7},{4,0},{5,1},{6,2},{7,3},{8,12},{9,13},{10,... | collective-permute-start | bytes 294920 | tf_op jit(solution)/shard_map/ppermute | solution.py:263
  31.9 4.3 %collective-permute-start.11 = (bf16[128,256]{1,0:T(8,128)(2,1)S(1)}, bf16[128,256]{1,0:T(8,128)(2,1)S(1)}, u32[]{:S(2)}, u32[]{:S(2)}) collective-permute-start(bf16[128,256]{1,0:T(8,128)(2,1)S(1)} %shard_map.93), channel_id=1, source_target_pairs={{0,2},{1,7},{2,0},{3,5},{4,6},{5,3},{6,4},{7,1},{8,10},{9,15},{10,... | collective-permute-start | bytes 196616 | tf_op jit(solution)/shard_map/ppermute | solution.py:263
  35.9 2.4 %collective-permute-start.13 = (bf16[192,256]{1,0:T(8,128)(2,1)S(1)}, bf16[192,256]{1,0:T(8,128)(2,1)S(1)}, u32[]{:S(2)}, u32[]{:S(2)}) collective-permute-start(bf16[192,256]{1,0:T(8,128)(2,1)S(1)} %collective-permute-done.9.refs_3_.refs_4_), channel_id=1, source_target_pairs={{0,1},{1,0},{2,3},{3,2},{4,5},{5,4},{6,7},{7,6},{8,9},{9,8},{10,11... | collective-permute-start | bytes 294920 | tf_op jit(solution)/shard_map/ppermute | solution.py:263
  36.1 2.2 %collective-permute-start.12 = (bf16[128,256]{1,0:T(8,128)(2,1)S(1)}, bf16[128,256]{1,0:T(8,128)(2,1)S(1)}, u32[]{:S(2)}, u32[]{:S(2)}) collective-permute-start(bf16[128,256]{1,0:T(8,128)(2,1)S(1)} %collective-permute-done.11.refs_3_), channel_id=1, source_target_pairs={{0,1},{1,0},{2,3},{3,2},{4,5},{5,4},{6,7},{7,6},{8,9},{9,8},{10,11... | collective-permute-start | bytes 196616 | tf_op jit(solution)/shard_map/ppermute | solution.py:263

commit v7 on v6

--- a/solution.py
+++ b/solution.py
@@ -144,7 +144,9 @@
     ).astype(jnp.bfloat16)
 
 
-def right_far_kernel(layer_ref, far_ref, here_ref, there_ref, both_ref, near_ref):
+def right_far_kernel(pieces, layer_ref, far_ref, here_ref, *refs):
+    (both_ref, near_ref, there_ref), sources = refs[-3:], refs[:-3]
+    project_kernel(pieces, *sources, there_ref)
     share = far_ref.shape[0]
     half = near_ref.shape[0] - share
     start = pl.multiple_of(lax.axis_index("tile") * half, half)
@@ -308,14 +310,12 @@
         right_factor, right_pick, pair, pair_t,
     )
     (right_near,) = call(right_own_kernel, [(chunk, paths)], right_layer, here)
-    there = project(
-        (((0, 0, depth), (1, 0, depth), (0, depth, depth), (1, depth, depth)),),
-        right_factor, right_pick, near, near_t,
-    )
+    pieces = (((0, 0, depth), (1, 0, depth), (0, depth, depth), (1, depth, depth)),)
     both, for_near = call(
-        right_far_kernel,
+        functools.partial(right_far_kernel, pieces),
         [(2 * share, paths), (chunk // sizes[2] + share, paths)],
-        right_layer, far, here, there,
+        right_layer, far, here, right_factor, right_pick, near, near_t,
+        scratch=(pltpu.VMEM((gates, paths), jnp.bfloat16),),
     )
     both_t = exchange(both, tile=1)
     from_z = exchange(for_near, plane=1)

time: 40 us -> 39.9 us (level)
    pallas_call x13 -> x12, Pallas kernels: 6.55 us -> 6.44 us  [call(): pl.pallas_call(kernel, out_shape=shapes, in_specs=[pl.BlockSpec(memory_sp...]
  transfers between devices with their start and end apart: 14 -> 14, of which waited for: 8 -> 8; matrix products, arithmetic and copies ran while one was open for 0% -> 0% of each run, Pallas kernels for 13% -> 12%
where the time goes in v7:
time: 39.9 us; the launch traced here: 39.8 us
  waiting for transfers between devices  20.5 us (51%)
  starting transfers between devices  12.7 us (32%)
  Pallas kernels  6.44 us (16%)
    ppermute x14, waiting for transfers between devices, exchange(): return lax.ppermute(value, DEVICE_AXES, pairs)  20.5 us
    ppermute x14, starting transfers between devices, exchange(): return lax.ppermute(value, DEVICE_AXES, pairs)  12.7 us
    pallas_call x12, Pallas kernels, call(): pl.pallas_call(kernel, out_shape=shapes, in_specs=[pl.BlockSpec(memory_sp...  6.44 us
  transfers between devices with their start and end apart: 14, of which 8 were waited for; matrix products, arithmetic and copies ran while one was open for 0% of the time, Pallas kernels for 12%

profile of v7, /device:TPU:0, one launch (start us, length us, event | category | flops | bytes accessed | tf_op | source)
XLA Modules:
  0.0 39.8 jit_solution(5074202892382762679)
XLA Ops:
  0.0 3.0 %collective-permute-start = (bf16[256,1024]{1,0:T(8,128)(2,1)}, bf16[256,1024]{1,0:T(8,128)(2,1)S(1)}, u32[]{:S(2)}, u32[]{:S(2)}) collective-permute-start(bf16[256,1024]{1,0:T(8,128)(2,1)} %own_ref.1), channel_id=1, source_target_pairs={{0,2},{1,3},{2,0},{3,1},{4,6},{5,7},{6,4},{7,5},{8,10},{9,11},{10,... | collective-permute-start | bytes 1572872 | tf_op jit(solution)/shard_map/ppermute | solution.py:265
  3.0 1.0 %shard_map.82 = (bf16[64,1024]{1,0:T(8,128)(2,1)S(1)}, bf16[8,1024]{1,0:T(8,128)(2,1)S(1)}, bf16[8,1024]{1,0:T(8,128)(2,1)S(1)}, s32[1,10]{1,0:T(1,128)S(1)}, s3...) custom-call(bf16[256,1024]{1,0:T(8,128)(2,1)} %layer_ref.3, bf16[8,1024]{1,0:T(8,128)(2,1)} %refs_1_.1, ...), custom_call_target="tpu_custom_call" | custom-call | tf_op jit(solution)/shard_map/pallas_call | solution.py:60
  4.0 11.5 %collective-permute-done.1.refs_1_ = bf16[8,1024]{1,0:T(8,128)(2,1)S(1)} collective-permute-done((bf16[8,1024]{1,0:T(8,128)(2,1)}, bf16[8,1024]{1,0:T(8,128)(2,1)S(1)}, u32[]{:S(2)}, u32[]{:S(2)}) %collective-permute-start.1) | collective-permute-done | bytes 16416 | tf_op jit(solution)/shard_map/ppermute | solution.py:265
  15.5 1.8 %collective-permute-start.2 = (bf16[24,1024]{1,0:T(8,128)(2,1)S(1)}, bf16[24,1024]{1,0:T(8,128)(2,1)S(1)}, u32[]{:S(2)}, u32[]{:S(2)}) collective-permute-start(bf16[24,1024]{1,0:T(8,128)(2,1)S(1)} %shard_map.84.refs_0_), channel_id=1, source_target_pairs={{0,4},{1,5},{2,6},{3,7},{4,0},{5,1},{6,2},{7,3},{8,12},{9,13},{10,... | collective-permute-start | bytes 147464 | tf_op jit(solution)/shard_map/ppermute | solution.py:265
  17.3 2.3 %collective-permute-done.2.refs_1_.refs_2_ = bf16[24,1024]{1,0:T(8,128)(2,1)S(1)} collective-permute-done((bf16[24,1024]{1,0:T(8,128)(2,1)S(1)}, bf16[24,1024]{1,0:T(8,128)(2,1)S(1)}, u32[]{:S(2)}, u32[]{:S(2)}) %collective-permute-start.2) | collective-permute-done | bytes 49184 | tf_op jit(solution)/shard_map/ppermute | solution.py:265
  19.6 2.8 %collective-permute-start.3 = (bf16[16,1024]{1,0:T(8,128)(2,1)S(1)}, bf16[16,1024]{1,0:T(8,128)(2,1)S(1)}, u32[]{:S(2)}, u32[]{:S(2)}) collective-permute-start(bf16[16,1024]{1,0:T(8,128)(2,1)S(1)} %shard_map.85.refs_0_), channel_id=1, source_target_pairs={{0,8},{1,9},{2,10},{3,11},{4,12},{5,13},{6,14},{7,15},{8,0},{9,1},... | collective-permute-start | bytes 98312 | tf_op jit(solution)/shard_map/ppermute | solution.py:265
  22.4 0.2 collective-permute-start.8
  22.6 0.5 %collective-permute-start.5 = (bf16[24,1024]{1,0:T(8,128)(2,1)S(1)}, bf16[24,1024]{1,0:T(8,128)(2,1)S(1)}, u32[]{:S(2)}, u32[]{:S(2)}) collective-permute-start(bf16[24,1024]{1,0:T(8,128)(2,1)S(1)} %collective-permute-done.2.refs_1_.refs_2_), channel_id=1, source_target_pairs={{0,1},{1,0},{2,3},{3,2},{4,5},{5,4},{6,7},{7,6},{8,9},{9,8},{10,11... | collective-permute-start | bytes 147464 | tf_op jit(solution)/shard_map/ppermute | solution.py:265
  23.1 3.5 %collective-permute-done.3.refs_1_ = bf16[16,1024]{1,0:T(8,128)(2,1)S(1)} collective-permute-done((bf16[16,1024]{1,0:T(8,128)(2,1)S(1)}, bf16[16,1024]{1,0:T(8,128)(2,1)S(1)}, u32[]{:S(2)}, u32[]{:S(2)}) %collective-permute-start.3) | collective-permute-done | bytes 32800 | tf_op jit(solution)/shard_map/ppermute | solution.py:265
  26.5 1.1 %shard_map.83 = (bf16[1024,256]{1,0:T(8,128)(2,1)S(1)}, bf16[32,256]{1,0:T(8,128)(2,1)S(1)}, bf16[1024,256]{1,0:T(8,128)(2,1)S(1)}, bf16[32,256]{1,0:T(8,128)(2,1)S(1)}) custom-call(s32[1,10]{1,0:T(1,128)S(1)} %get-tuple-element.20.side_ref, s32[10,256]{1,0:T(8,128)S(1)} %get-tuple-element.21.branch_ref, s32[1,256]{1,0:T(1,128)S(1)} %get-tuple-element.22.left_map_ref, ...), custom_call_target="tpu_custom_call" | custom-call | tf_op jit(solution)/shard_map/pallas_call | solution.py:60
  27.8 0.5 %shard_map.86.projected_ref = bf16[1024,512]{1,0:T(8,128)(2,1)S(1)} custom-call(bf16[1024,256]{1,0:T(8,128)(2,1)S(1)} %get-tuple-element.24.factor_ref, bf16[32,256]{1,0:T(8,128)(2,1)S(1)} %get-tuple-element.25.pick_ref, bf16[16,1024]{1,0:T(8,128)(2,1)S(1)} %shard_map.85.refs_0_, bf16[16,1024]{1,0:T(8,128)(2,1)S(1)} %collective-permute-done.3.refs_1_, ...), custom_call_target="tpu_custom_call" | custom-call | tf_op jit(solution)/shard_map/pallas_call | solution.py:60
  28.2 0.7 %shard_map.87 = (bf16[512,256]{1,0:T(8,128)(2,1)S(1)}, bf16[512,256]{1,0:T(8,128)(2,1)S(1)}) custom-call(bf16[256,1024]{1,0:T(8,128)(2,1)S(1)} %copy-done.1, bf16[256,1024]{1,0:T(8,128)(2,1)S(1)} %collective-permute-done.x_ref, bf16[1024,512]{1,0:T(8,128)(2,1)S(1)} %shard_map.86.projected_ref), custom_call_target="tpu_custom_call" | custom-call | tf_op jit(solution)/shard_map/pallas_call | solution.py:60
  29.0 0.5 %collective-permute-start.7 = (bf16[512,256]{1,0:T(8,128)(2,1)S(1)}, bf16[512,256]{1,0:T(8,128)(2,1)S(1)}, u32[]{:S(2)}, u32[]{:S(2)}) collective-permute-start(bf16[512,256]{1,0:T(8,128)(2,1)S(1)} %get-tuple-element.29), channel_id=1, source_target_pairs={{0,1},{1,0},{2,3},{3,2},{4,5},{5,4},{6,7},{7,6},{8,9},{9,8},{10,11... | collective-permute-start | bytes 786440 | tf_op jit(solution)/shard_map/ppermute | solution.py:265
  29.5 0.3 shard_map.88.projected_ref.here_ref
  29.8 0.6 %shard_map.90 = (bf16[128,256]{1,0:T(8,128)(2,1)S(1)}, bf16[192,256]{1,0:T(8,128)(2,1)S(1)}) custom-call(bf16[256,1024]{1,0:T(8,128)(2,1)S(1)} %copy-done, bf16[64,1024]{1,0:T(8,128)(2,1)S(1)} %collective-permute-done.8.far_ref, bf16[1024,256]{1,0:T(8,128)(2,1)S(1)} %shard_map.88.projected_ref.here_ref, ...), custom_call_target="tpu_custom_call" | custom-call | tf_op jit(solution)/shard_map/pallas_call | solution.py:60
  30.6 0.9 %collective-permute-start.9 = (bf16[192,256]{1,0:T(8,128)(2,1)S(1)}, bf16[192,256]{1,0:T(8,128)(2,1)S(1)}, u32[]{:S(2)}, u32[]{:S(2)}) collective-permute-start(bf16[192,256]{1,0:T(8,128)(2,1)S(1)} %get-tuple-element.33), channel_id=1, source_target_pairs={{0,4},{1,5},{2,6},{3,7},{4,0},{5,1},{6,2},{7,3},{8,12},{9,13},{10,... | collective-permute-start | bytes 294920 | tf_op jit(solution)/shard_map/ppermute | solution.py:265
  31.4 0.3 collective-permute-done.10.both_t_ref.refs_5_
  31.8 1.7 %collective-permute-start.11 = (bf16[128,256]{1,0:T(8,128)(2,1)S(1)}, bf16[128,256]{1,0:T(8,128)(2,1)S(1)}, u32[]{:S(2)}, u32[]{:S(2)}) collective-permute-start(bf16[128,256]{1,0:T(8,128)(2,1)S(1)} %shard_map.92), channel_id=1, source_target_pairs={{0,2},{1,7},{2,0},{3,5},{4,6},{5,3},{6,4},{7,1},{8,10},{9,15},{10,... | collective-permute-start | bytes 196616 | tf_op jit(solution)/shard_map/ppermute | solution.py:265
  33.4 2.4 %collective-permute-done.9.refs_3_.refs_4_ = bf16[192,256]{1,0:T(8,128)(2,1)S(1)} collective-permute-done((bf16[192,256]{1,0:T(8,128)(2,1)S(1)}, bf16[192,256]{1,0:T(8,128)(2,1)S(1)}, u32[]{:S(2)}, u32[]{:S(2)}) %collective-permute-start.9) | collective-permute-done | bytes 98336 | tf_op jit(solution)/shard_map/ppermute | solution.py:265
  35.8 0.2 collective-permute-done.11.refs_3_
  36.0 1.3 %collective-permute-start.12 = (bf16[128,256]{1,0:T(8,128)(2,1)S(1)}, bf16[128,256]{1,0:T(8,128)(2,1)S(1)}, u32[]{:S(2)}, u32[]{:S(2)}) collective-permute-start(bf16[128,256]{1,0:T(8,128)(2,1)S(1)} %collective-permute-done.11.refs_3_), channel_id=1, source_target_pairs={{0,1},{1,0},{2,3},{3,2},{4,5},{5,4},{6,7},{7,6},{8,9},{9,8},{10,11... | collective-permute-start | bytes 196616 | tf_op jit(solution)/shard_map/ppermute | solution.py:265
  37.3 0.3 shard_map.89.refs_2_
  37.7 0.4 %shard_map.91.near_ref = bf16[1024,384]{1,0:T(8,128)(2,1)S(1)} custom-call(bf16[512,256]{1,0:T(8,128)(2,1)S(1)} %get-tuple-element.28.refs_0_, bf16[512,256]{1,0:T(8,128)(2,1)S(1)} %collective-permute-done.7.refs_1_, bf16[256,256]{1,0:T(8,128)(2,1)S(1)} %shard_map.89.refs_2_, bf16[192,256]{1,0:T(8,128)(2,1)S(1)} %collective-permute-done.9.refs_3_.refs_4_), custom_call_target="tpu_custom_call" | custom-call | tf_op jit(solution)/shard_map/pallas_call | solution.py:60
  38.2 1.5 %shard_map.93 = bf16[1024,1024]{1,0:T(8,128)(2,1)} custom-call(bf16[1024,384]{1,0:T(8,128)(2,1)S(1)} %shard_map.91.near_ref, bf16[512,256]{1,0:T(8,128)(2,1)S(1)} %get-tuple-element.28.refs_0_, bf16[512,256]{1,0:T(8,128)(2,1)S(1)} %collective-permute-done.7.refs_1_, bf16[128,256]{1,0:T(8,128)(2,1)S(1)} %get-tuple-element.34.both_ref.refs_2_, ...), custom_call_target="tpu_custom_call" | custom-call | tf_op jit(solution)/shard_map/pallas_call | solution.py:60
  (20 shorter events, 0.5 us)
Async XLA Ops:
  0.0 28.2 %copy-start.1 = (bf16[256,1024]{1,0:T(8,128)(2,1)S(1)}, bf16[256,1024]{1,0:T(8,128)(2,1)}, u32[]{:S(2)}) copy-start(bf16[256,1024]{1,0:T(8,128)(2,1)} %own_ref.1) | copy-start | bytes 1572868
  0.0 28.2 %collective-permute-start = (bf16[256,1024]{1,0:T(8,128)(2,1)}, bf16[256,1024]{1,0:T(8,128)(2,1)S(1)}, u32[]{:S(2)}, u32[]{:S(2)}) collective-permute-start(bf16[256,1024]{1,0:T(8,128)(2,1)} %own_ref.1), channel_id=1, source_target_pairs={{0,2},{1,3},{2,0},{3,1},{4,6},{5,7},{6,4},{7,5},{8,10},{9,11},{10,... | collective-permute-start | bytes 1572872 | tf_op jit(solution)/shard_map/ppermute | solution.py:265
  3.0 12.6 %collective-permute-start.1 = (bf16[8,1024]{1,0:T(8,128)(2,1)}, bf16[8,1024]{1,0:T(8,128)(2,1)S(1)}, u32[]{:S(2)}, u32[]{:S(2)}) collective-permute-start(bf16[8,1024]{1,0:T(8,128)(2,1)} %refs_1_.1), channel_id=1, source_target_pairs={{0,2},{1,3},{2,0},{3,1},{4,6},{5,7},{6,4},{7,5},{8,10},{9,11},{10,... | collective-permute-start | bytes 49160 | tf_op jit(solution)/shard_map/ppermute | solution.py:265
  15.5 4.1 %collective-permute-start.2 = (bf16[24,1024]{1,0:T(8,128)(2,1)S(1)}, bf16[24,1024]{1,0:T(8,128)(2,1)S(1)}, u32[]{:S(2)}, u32[]{:S(2)}) collective-permute-start(bf16[24,1024]{1,0:T(8,128)(2,1)S(1)} %shard_map.84.refs_0_), channel_id=1, source_target_pairs={{0,4},{1,5},{2,6},{3,7},{4,0},{5,1},{6,2},{7,3},{8,12},{9,13},{10,... | collective-permute-start | bytes 147464 | tf_op jit(solution)/shard_map/ppermute | solution.py:265
  19.6 6.9 %collective-permute-start.3 = (bf16[16,1024]{1,0:T(8,128)(2,1)S(1)}, bf16[16,1024]{1,0:T(8,128)(2,1)S(1)}, u32[]{:S(2)}, u32[]{:S(2)}) collective-permute-start(bf16[16,1024]{1,0:T(8,128)(2,1)S(1)} %shard_map.85.refs_0_), channel_id=1, source_target_pairs={{0,8},{1,9},{2,10},{3,11},{4,12},{5,13},{6,14},{7,15},{8,0},{9,1},... | collective-permute-start | bytes 98312 | tf_op jit(solution)/shard_map/ppermute | solution.py:265
  22.4 7.4 %collective-permute-start.8 = (bf16[64,1024]{1,0:T(8,128)(2,1)S(1)}, bf16[64,1024]{1,0:T(8,128)(2,1)S(1)}, u32[]{:S(2)}, u32[]{:S(2)}) collective-permute-start(bf16[64,1024]{1,0:T(8,128)(2,1)S(1)} %get-tuple-element.32), channel_id=1, source_target_pairs={{0,8},{1,9},{2,10},{3,11},{4,12},{5,13},{6,14},{7,15},{8,0},{9,1},... | collective-permute-start | bytes 393224 | tf_op jit(solution)/shard_map/ppermute | solution.py:265
  22.5 5.1 %collective-permute-start.4 = (bf16[24,1024]{1,0:T(8,128)(2,1)S(1)}, bf16[24,1024]{1,0:T(8,128)(2,1)S(1)}, u32[]{:S(2)}, u32[]{:S(2)}) collective-permute-start(bf16[24,1024]{1,0:T(8,128)(2,1)S(1)} %shard_map.84.refs_0_), channel_id=1, source_target_pairs={{0,1},{1,0},{2,3},{3,2},{4,5},{5,4},{6,7},{7,6},{8,9},{9,8},{10,11... | collective-permute-start | bytes 147464 | tf_op jit(solution)/shard_map/ppermute | solution.py:265
  22.6 5.1 %collective-permute-start.5 = (bf16[24,1024]{1,0:T(8,128)(2,1)S(1)}, bf16[24,1024]{1,0:T(8,128)(2,1)S(1)}, u32[]{:S(2)}, u32[]{:S(2)}) collective-permute-start(bf16[24,1024]{1,0:T(8,128)(2,1)S(1)} %collective-permute-done.2.refs_1_.refs_2_), channel_id=1, source_target_pairs={{0,1},{1,0},{2,3},{3,2},{4,5},{5,4},{6,7},{7,6},{8,9},{9,8},{10,11... | collective-permute-start | bytes 147464 | tf_op jit(solution)/shard_map/ppermute | solution.py:265
  26.5 1.2 %collective-permute-start.6 = (bf16[16,1024]{1,0:T(8,128)(2,1)S(1)}, bf16[16,1024]{1,0:T(8,128)(2,1)S(1)}, u32[]{:S(2)}, u32[]{:S(2)}) collective-permute-start(bf16[16,1024]{1,0:T(8,128)(2,1)S(1)} %collective-permute-done.3.refs_1_), channel_id=1, source_target_pairs={{0,1},{1,0},{2,3},{3,2},{4,5},{5,4},{6,7},{7,6},{8,9},{9,8},{10,11... | collective-permute-start | bytes 98312 | tf_op jit(solution)/shard_map/ppermute | solution.py:265
  27.7 2.1 %copy-start = (bf16[256,1024]{1,0:T(8,128)(2,1)S(1)}, bf16[256,1024]{1,0:T(8,128)(2,1)}, u32[]{:S(2)}) copy-start(bf16[256,1024]{1,0:T(8,128)(2,1)} %layer_ref.3) | copy-start | bytes 1572868
  29.0 8.7 %collective-permute-start.7 = (bf16[512,256]{1,0:T(8,128)(2,1)S(1)}, bf16[512,256]{1,0:T(8,128)(2,1)S(1)}, u32[]{:S(2)}, u32[]{:S(2)}) collective-permute-start(bf16[512,256]{1,0:T(8,128)(2,1)S(1)} %get-tuple-element.29), channel_id=1, source_target_pairs={{0,1},{1,0},{2,3},{3,2},{4,5},{5,4},{6,7},{7,6},{8,9},{9,8},{10,11... | collective-permute-start | bytes 786440 | tf_op jit(solution)/shard_map/ppermute | solution.py:265
  30.4 1.3 %collective-permute-start.10 = (bf16[128,256]{1,0:T(8,128)(2,1)S(1)}, bf16[128,256]{1,0:T(8,128)(2,1)S(1)}, u32[]{:S(2)}, u32[]{:S(2)}) collective-permute-start(bf16[128,256]{1,0:T(8,128)(2,1)S(1)} %get-tuple-element.34.both_ref.refs_2_), channel_id=1, source_target_pairs={{0,1},{1,0},{2,3},{3,2},{4,5},{5,4},{6,7},{7,6},{8,9},{9,8},{10,11... | collective-permute-start | bytes 196616 | tf_op jit(solution)/shard_map/ppermute | solution.py:265
  30.6 5.2 %collective-permute-start.9 = (bf16[192,256]{1,0:T(8,128)(2,1)S(1)}, bf16[192,256]{1,0:T(8,128)(2,1)S(1)}, u32[]{:S(2)}, u32[]{:S(2)}) collective-permute-start(bf16[192,256]{1,0:T(8,128)(2,1)S(1)} %get-tuple-element.33), channel_id=1, source_target_pairs={{0,4},{1,5},{2,6},{3,7},{4,0},{5,1},{6,2},{7,3},{8,12},{9,13},{10,... | collective-permute-start | bytes 294920 | tf_op jit(solution)/shard_map/ppermute | solution.py:265
  31.8 4.3 %collective-permute-start.11 = (bf16[128,256]{1,0:T(8,128)(2,1)S(1)}, bf16[128,256]{1,0:T(8,128)(2,1)S(1)}, u32[]{:S(2)}, u32[]{:S(2)}) collective-permute-start(bf16[128,256]{1,0:T(8,128)(2,1)S(1)} %shard_map.92), channel_id=1, source_target_pairs={{0,2},{1,7},{2,0},{3,5},{4,6},{5,3},{6,4},{7,1},{8,10},{9,15},{10,... | collective-permute-start | bytes 196616 | tf_op jit(solution)/shard_map/ppermute | solution.py:265
  35.8 2.5 %collective-permute-start.13 = (bf16[192,256]{1,0:T(8,128)(2,1)S(1)}, bf16[192,256]{1,0:T(8,128)(2,1)S(1)}, u32[]{:S(2)}, u32[]{:S(2)}) collective-permute-start(bf16[192,256]{1,0:T(8,128)(2,1)S(1)} %collective-permute-done.9.refs_3_.refs_4_), channel_id=1, source_target_pairs={{0,1},{1,0},{2,3},{3,2},{4,5},{5,4},{6,7},{7,6},{8,9},{9,8},{10,11... | collective-permute-start | bytes 294920 | tf_op jit(solution)/shard_map/ppermute | solution.py:265
  36.0 2.2 %collective-permute-start.12 = (bf16[128,256]{1,0:T(8,128)(2,1)S(1)}, bf16[128,256]{1,0:T(8,128)(2,1)S(1)}, u32[]{:S(2)}, u32[]{:S(2)}) collective-permute-start(bf16[128,256]{1,0:T(8,128)(2,1)S(1)} %collective-permute-done.11.refs_3_), channel_id=1, source_target_pairs={{0,1},{1,0},{2,3},{3,2},{4,5},{5,4},{6,7},{7,6},{8,9},{9,8},{10,11... | collective-permute-start | bytes 196616 | tf_op jit(solution)/shard_map/ppermute | solution.py:265
